TPU v7x, 128 devices: a whole 4x4x4 slice. The times are simulated.
128 devices in a mesh: section: 4 (over x), fsdp: 32 (over y, z, core).
Axes of the slice: x: 4, y: 4, z: 4, core: 2. Of those that a mesh axis runs over, the one named last changes fastest.
Arguments:
- grad_parts: bfloat16 [4, 32, 8192, 1024], P('section', 'fsdp'), may hold values from -510 to 510
- first_codes: int32 [4, 8192, 1024], P('section', 'fsdp'), may hold values from -7 to 7
- first_rows: float32 [4, 8192], P('section', 'fsdp'), may hold values from 0.003 to 0.03
- first_columns: float32 [4, 1024], P('section'), may hold values from 0.003 to 0.03
- second_codes: int32 [4, 8192, 1024], P('section', 'fsdp'), may hold values from 1 to 15
- second_rows: float32 [4, 8192], P('section', 'fsdp'), may hold values from 0.001 to 0.01
- second_columns: float32 [4, 1024], P('section'), may hold values from 0.001 to 0.01
Outputs:
- direction: float32 [4, 8192, 1024], P('section', 'fsdp')
- first_scaled: float32 [4, 8192, 1024], P('section', 'fsdp')
- second_scaled: float32 [4, 8192, 1024], P('section', 'fsdp')
- first_rowmax: float32 [4, 8192], P('section', 'fsdp')
- first_colmax: float32 [4, 1024], P('section')
- second_rowmax: float32 [4, 8192], P('section', 'fsdp')
- second_colmax: float32 [4, 1024], P('section')
All inputs are finite; a program needn't handle non-finite values. Where the computation divides by a largest or mean magnitude, that divisor is 1e-20 or more.
Results may differ from a plain program's by a relative error of at most 0.0003.
Values may be sent and summed in bfloat16 or wider, within the bound.
No kernel may reach another device: no remote copies, remote signals or barrier semaphores. Data moves between devices by JAX's collectives and lax.ppermute only.
A program may use at most 192 MiB of HBM per device.

v0:
```python
import functools
import math

import jax
import jax.numpy as jnp
from jax import lax
from jax.experimental import pallas as pl
from jax.experimental.pallas import tpu as pltpu
from jax.sharding import Mesh
from jax.sharding import PartitionSpec as P


AXES = ("section", "y", "z", "core")
FSDP = ("y", "z", "core")

beta_first = 0.9
beta_second = 0.999
clip_rms = 3.0
epsilon = 1e-08
scale_floor = 0.001

RING = 4
ORDER = (1, 3, 2, 0)
TOP = 32767.0
LEAST = 1e-18
SIDE = 8
STEP = 64
VMEM_LIMIT = 20 * 1024 * 1024
F32, I16 = jnp.float32, jnp.int16
VMEM = pltpu.VMEM


def scale_code(peak):
    return jnp.ceil(jnp.log2(jnp.maximum(peak, LEAST)) * 256.0)


def send_factor(code):
    return jnp.exp2(code * (-1.0 / 256.0)) * TOP**4


def encode(values, factor):
    root = lax.rsqrt(lax.rsqrt(jnp.abs(values) * factor))
    root = jnp.where(values < 0.0, -root, root)
    return jnp.round(root).astype(jnp.int32).astype(I16)


def came_factor(side):
    code = side[...].astype(jnp.int32).astype(F32)
    return jnp.exp2(code * (1.0 / 256.0)) * TOP**-4


def decode(codes, factor):
    root = codes.astype(jnp.int32).astype(F32)
    square = root * jnp.abs(root)
    return (square * jnp.abs(square)) * factor


def side_rows(codes):
    line = lax.broadcasted_iota(jnp.int32, (SIDE, codes[0].shape[1]), 0)
    rows = codes[-1]
    for at, code in enumerate(codes[:-1]):
        rows = jnp.where(line == at, code, rows)
    return jnp.broadcast_to(rows, line.shape).astype(jnp.int32).astype(I16)


def call(body, outs, scratch, flops, bytes_accessed, in_specs):
    return pl.pallas_call(
        body,
        out_shape=outs,
        in_specs=in_specs,
        out_specs=tuple(pl.BlockSpec(memory_space=VMEM) for _ in outs),
        scratch_shapes=scratch,
        compiler_params=pltpu.CompilerParams(vmem_limit_bytes=VMEM_LIMIT),
        cost_estimate=pl.CostEstimate(flops=flops, bytes_accessed=bytes_accessed, transcendentals=0),
    )


def in_vmem(n):
    return [pl.BlockSpec(memory_space=VMEM)] * n


def held(value):
    return pltpu.with_memory_space_constraint(value, VMEM)


def gather_copies(wanted, where, parts, outs, sem):
    copies = []
    for (jobs, mine), out in zip(wanted, outs):
        core = where[2] if mine else 1 - where[2]
        for q, (half, delta, low) in enumerate(jobs):
            for i in range(2):
                j = lax.rem(where[1 - half] + ORDER[low + i], RING)
                far = lax.rem(where[half] + delta, RING)
                at = far * RING + j if half == 0 else j * RING + far
                copies.append(
                    pltpu.make_async_copy(
                        parts.at[at, core, half], out.at[q, i], sem.at[len(copies)]
                    )
                )
    return copies


def gather_body(wanted, where, parts, *refs):
    copies = gather_copies(wanted, where, parts, refs[:-1], refs[-1])
    for copy in copies:
        copy.start()
    for copy in copies:
        copy.wait()


def gather_specs():
    return [pl.BlockSpec(memory_space=pltpu.SMEM), pl.BlockSpec(memory_space=pltpu.HBM)]


def gather_outs(parts, wanted):
    rows, cols = parts.shape[3:]
    return (
        tuple(VMEM((4, 2, rows, cols), parts.dtype) for _ in wanted),
        pltpu.SemaphoreType.DMA((8 * len(wanted),)),
        32 * len(wanted) * rows * cols,
    )


def gather(where, parts, wanted):
    outs, sem, moved = gather_outs(parts, wanted)
    body = functools.partial(gather_body, wanted)
    return call(body, outs, [sem], moved // 4, moved, gather_specs())(where, parts)


def chunks(rows, step, carry):
    return lax.fori_loop(0, rows // STEP, lambda n, c: step(pl.multiple_of(n * STEP, STEP), c), carry)


def fold(values, join):
    folded = values[0:8]
    for at in range(8, values.shape[0], 8):
        folded = join(folded, values[at : at + 8])
    return folded


def send_blocks(total, outs, peaks, rows, each):
    code = scale_code(jnp.concatenate(peaks, axis=0))
    factor = send_factor(code)
    for q, out in enumerate(outs):
        for i in range(each):
            line = q * each + i
            by = factor[line : line + 1]

            def step(r, _, line=line, by=by, out=out, i=i):
                out[pl.ds(i * rows + r, STEP), :] = encode(total[line, pl.ds(r, STEP), :], by)

            chunks(rows, step, None)
        out[each * rows : each * rows + SIDE, :] = side_rows(
            [code[q * each + i : q * each + i + 1] for i in range(each)]
        )


def pair_body(relays, wanted, *refs):
    own, came = refs[:2]
    relayed, refs = refs[2 : 2 + relays], refs[2 + relays :]
    copies = []
    if wanted:
        (where, parts), refs = refs[:2], refs[2:]
        copies = gather_copies(wanted, where, parts, refs[4 : 4 + len(wanted)], refs[-1])
    for copy in copies:
        copy.start()
    outs, total = refs[:4], refs[4 + len(wanted)]
    rows, cols = own.shape[2:]
    peaks = []
    for q in range(4):
        by = came_factor(relayed[q].at[2 * rows : 2 * rows + SIDE]) if relayed else None
        for i in range(2):

            def step(r, peak, q=q, i=i, by=by):
                value = own[q, i, pl.ds(r, STEP), :].astype(F32) + came[q, i, pl.ds(r, STEP), :].astype(F32)
                if relayed:
                    value = value + decode(relayed[q][pl.ds(i * rows + r, STEP), :], by[i : i + 1])
                total[2 * q + i, pl.ds(r, STEP), :] = value
                return jnp.maximum(peak, fold(jnp.abs(value), jnp.maximum))

            peak = chunks(rows, step, jnp.zeros((8, cols), F32))
            peaks.append(jnp.max(peak, axis=0, keepdims=True))
    send_blocks(total, outs, peaks, rows, 2)
    for copy in copies:
        copy.wait()


def pair(own, came, relayed=(), where=None, parts=None, wanted=()):
    rows, cols = own.shape[2:]
    outs, scratch = (VMEM((2 * rows + SIDE, cols), I16),) * 4, [VMEM((8, rows, cols), F32)]
    specs, args = in_vmem(2 + len(relayed)), [own, held(came), *[held(r) for r in relayed]]
    if wanted:
        more, sem, _ = gather_outs(parts, wanted)
        outs, scratch = outs + more, scratch + [sem]
        specs, args = specs + gather_specs(), args + [where, parts]
    got = call(
        functools.partial(pair_body, len(relayed), wanted), outs, scratch, 400 * rows * cols, 48 * rows * cols, specs
    )(*args)
    return got[:4], got[4:]


def column_of(row):
    n = row.shape[1]
    return jnp.transpose(jnp.broadcast_to(row, (128, n)))[:, 0:1]


def row_of(column):
    n = column.shape[0]
    return jnp.transpose(jnp.broadcast_to(column, (n, 128)))[0:1, :]


def keep_body(own, came, *refs):
    got, (old, total, first_old, second_old) = refs[:4], (refs[4:10], *refs[10:])
    rows = own.shape[2]
    for half in range(2):
        for i in range(RING):
            ref = got[2 * half + (1 if i < 2 else 0)]
            by = came_factor(ref.at[2 * rows : 2 * rows + SIDE])[i % 2 : i % 2 + 1]

            def step(r, _, ref=ref, by=by, half=half, i=i):
                q = 2 * half + i // 2
                value = own[q, i % 2, pl.ds(r, STEP), :].astype(F32) + came[q, i % 2, pl.ds(r, STEP), :].astype(F32)
                total[half, i, pl.ds(r, STEP), :] = value + decode(ref[pl.ds(i % 2 * rows + r, STEP), :], by)

            chunks(rows, step, None)
    for (codes, row, column), levels, beta, out in (
        (old[:3], 7.0, beta_first, first_old),
        (old[3:], 15.0, beta_second, second_old),
    ):
        tall, wide = column_of(row[...]), column[...]
        for r in range(0, out.shape[0], STEP):
            bound = jnp.minimum(tall[r : r + STEP], wide)
            out[r : r + STEP, :] = codes[0, r : r + STEP, :].astype(F32) * (beta / levels) * bound


def keep(own, came, got, old):
    rows, cols = own.shape[2:]
    each = VMEM((2 * rows, cols), F32)
    return call(
        keep_body, (VMEM((2, RING, rows, cols), F32), each, each), [], 300 * rows * cols, 100 * rows * cols, in_vmem(12)
    )(own, held(came), *[held(g) for g in got], *old)


def middle_body(half, acc, first, second, *refs):
    outs, kept, total = refs[:3], refs[3], refs[4]
    rows, cols = kept.shape
    peaks = []
    for i in range(RING):
        ref = first if i < 2 else second
        by = came_factor(ref.at[2 * rows : 2 * rows + SIDE])[i % 2 : i % 2 + 1]

        def step(r, peak, ref=ref, by=by, i=i):
            value = acc[half, i, pl.ds(r, STEP), :] + decode(ref[pl.ds(i % 2 * rows + r, STEP), :], by)
            if i == 3:
                kept[pl.ds(r, STEP), :] = value
                return peak
            total[i, pl.ds(r, STEP), :] = value
            return jnp.maximum(peak, fold(jnp.abs(value), jnp.maximum))

        peak = chunks(rows, step, jnp.zeros((8, cols), F32))
        if i < 3:
            peaks.append(jnp.max(peak, axis=0, keepdims=True))
    send_blocks(total, outs, peaks, rows, 1)


def middle(acc, first, second, half):
    rows, cols = acc.shape[2:]
    sent = VMEM((rows + SIDE, cols), I16)
    return call(
        functools.partial(middle_body, half),
        (sent, sent, sent, VMEM((rows, cols), F32)),
        [VMEM((3, rows, cols), F32)],
        200 * rows * cols,
        32 * rows * cols,
        in_vmem(3),
    )(acc, held(first), held(second))


def last_body(*refs):
    ins, (grad, squares) = refs[:8], refs[8:]
    rows, cols = ins[0].shape
    square = jnp.zeros((8, cols), F32)
    for half in range(2):
        kept, *got = ins[4 * half : 4 * half + 4]
        by = [came_factor(ref.at[rows : rows + SIDE])[0:1] for ref in got]

        def step(r, square, half=half, kept=kept, got=got, by=by):
            value = kept[pl.ds(r, STEP), :]
            for ref, factor in zip(got, by):
                value = value + decode(ref[pl.ds(r, STEP), :], factor)
            grad[pl.ds(half * rows + r, STEP), :] = value
            return square + fold(value * value, jnp.add)

        square = chunks(rows, step, square)
    folded = square[:, 0:128]
    for at in range(128, cols, 128):
        folded = folded + square[:, at : at + 128]
    squares[...] = jnp.broadcast_to(jnp.sum(folded, axis=0, keepdims=True), squares.shape)


def last(halves, devices):
    rows, cols = halves[0][0].shape
    flat = [a for kept, *got in halves for a in (kept, *[held(g) for g in got])]
    return call(
        last_body,
        (VMEM((2 * rows, cols), F32), VMEM((devices, 128), F32)),
        [],
        100 * rows * cols,
        32 * rows * cols,
        in_vmem(8),
    )(*flat)


def reduce_scatter(parts, old, devices):
    where = jnp.stack([lax.axis_index(a) for a in FSDP]).astype(jnp.int32)
    parts = pltpu.with_memory_space_constraint(parts, pltpu.HBM)
    axis = ("y", "z")

    def hop(value, name, delta):
        return lax.ppermute(value, name, [(i, (i + delta) % RING) for i in range(RING)])

    def four_ways(values):
        return [hop(v, axis[q // 2], 1 if q % 2 == 0 else 3) for q, v in enumerate(values)]

    def swap(value):
        return lax.ppermute(value, "core", [(0, 1), (1, 0)])

    far = tuple((h, 2, low) for h in range(2) for low in (0, 2))
    near = tuple((h, d, low) for h in range(2) for d, low in ((1, 2), (3, 0)))
    join = tuple((h, d, low) for h in range(2) for d, low in ((1, 0), (3, 2)))
    mine = tuple((h, 0, low) for h in range(2) for low in (0, 2))
    (out_far,) = gather(where, parts, ((far, False),))
    came_far = swap(out_far)
    out_near, own_far = gather(where, parts, ((near, False), (far, True)))
    came_near = swap(out_near)
    sent, (out_join, own_near) = pair(
        own_far, came_far, (), where, parts, ((join, False), (near, True))
    )
    got_far = four_ways(sent)
    came_join = swap(out_join)
    sent, (out_mine, own_join, own_mine) = pair(
        own_near, came_near, (), where, parts, ((mine, False), (join, True), (mine, True))
    )
    got_near = four_ways(sent)
    came_mine = swap(out_mine)
    sent, _ = pair(own_join, came_join, got_far)
    got_join = four_ways(sent)
    acc, first_old, second_old = keep(own_mine, came_mine, got_near, old)
    halves = []
    for half in range(2):
        *out, kept = middle(acc, got_join[2 * half], got_join[2 * half + 1], half)
        got = {d: hop(out[k], axis[1 - half], d) for k, d in ((2, 2), (0, 1), (1, 3))}
        halves.append([kept, got[1], got[3], got[2]])
    return *last(halves, devices), first_old, second_old


def clip_body(limit, squares, grad, first_old, second_old, first_new, second_new, peaks):
    rows, cols = grad.shape
    total = jnp.sum(jnp.sum(squares[...], axis=0, keepdims=True), axis=1, keepdims=True)
    scale = limit / jnp.maximum(jnp.sqrt(total), limit)

    def step(r, peak):
        clipped = grad[pl.ds(r, STEP), :] * scale
        first = first_old[pl.ds(r, STEP), :] + (1.0 - beta_first) * clipped
        second = second_old[pl.ds(r, STEP), :] + (1.0 - beta_second) * clipped * clipped
        first_new[pl.ds(r, STEP), :] = first
        second_new[pl.ds(r, STEP), :] = second
        return (
            jnp.maximum(peak[0], fold(jnp.abs(first), jnp.maximum)),
            jnp.maximum(peak[1], fold(second, jnp.maximum)),
        )

    zero = jnp.zeros((8, cols), F32)
    found = chunks(rows, step, (zero, zero))
    lines = []
    for peak in found:
        peak = jnp.max(peak, axis=0, keepdims=True)
        lines += [peak[:, at : at + 128] for at in range(0, cols, 128)]
    lines = jnp.concatenate(lines, axis=0)
    for at in range(peaks.shape[0]):
        peaks[at] = lines


def clip(squares, grad, first_old, second_old, limit, group):
    rows, cols = grad.shape
    each = VMEM((rows, cols), F32)
    return call(
        functools.partial(clip_body, limit),
        (each, each, VMEM((group, 2 * cols // 128, 128), F32)),
        [],
        12 * rows * cols,
        20 * rows * cols,
        in_vmem(4),
    )(held(squares), grad, first_old, second_old)


def rows_body(first_new, second_new, direction, first_rowmax, second_rowmax, by_first, by_second):
    first, second = first_new[...], second_new[...]
    direction[0] = first / (jnp.sqrt(second) + epsilon)
    for values, least, peak, by in (
        (jnp.abs(first), scale_floor, first_rowmax, by_first),
        (second, 0.0, second_rowmax, by_second),
    ):
        tall = jnp.maximum(jnp.max(values, axis=1, keepdims=True), least)
        by[...] = jnp.broadcast_to(1.0 / tall, by.shape)
        peak[...] = row_of(tall)


def row_outputs(first_new, second_new):
    rows, cols = first_new.shape
    step = min(rows, 128)
    whole = pl.BlockSpec((step, cols), lambda r: (r, 0))
    side, line = pl.BlockSpec((step, 128), lambda r: (r, 0)), pl.BlockSpec((1, step), lambda r: (0, r))
    return pl.pallas_call(
        rows_body,
        grid=(rows // step,),
        out_shape=(
            jax.ShapeDtypeStruct((1, rows, cols), F32),
            jax.ShapeDtypeStruct((1, rows), F32),
            jax.ShapeDtypeStruct((1, rows), F32),
            VMEM((rows, 128), F32),
            VMEM((rows, 128), F32),
        ),
        in_specs=[whole, whole],
        out_specs=(pl.BlockSpec((1, step, cols), lambda r: (0, r, 0)), line, line, side, side),
        compiler_params=pltpu.CompilerParams(vmem_limit_bytes=VMEM_LIMIT),
        cost_estimate=pl.CostEstimate(flops=40 * rows * cols, bytes_accessed=12 * rows * cols, transcendentals=0),
        name="row_outputs",
    )(first_new, second_new)


def scaled_body(peaks, first_new, second_new, by_first, by_second, *refs):
    first_scaled, second_scaled, first_colmax, second_colmax, inverse = refs
    half = peaks.shape[1] // 2

    @pl.when(pl.program_id(0) == 0)
    def _():
        found = jnp.max(peaks[...], axis=0)
        for k, (out, least) in enumerate(((first_colmax, scale_floor), (second_colmax, 0.0))):
            wide = [found[k * half + at : k * half + at + 1] for at in range(half)]
            wide = jnp.maximum(jnp.concatenate(wide, axis=1), least)
            out[...] = wide
            inverse[k : k + 1, :] = 1.0 / wide

    for k, (values, by, out) in enumerate(
        ((first_new, by_first, first_scaled), (second_new, by_second, second_scaled))
    ):
        out[0] = values[...] * jnp.maximum(by[:, 0:1], inverse[k : k + 1, :])


def scaled_outputs(peaks, first_new, second_new, by_first, by_second):
    rows, cols = first_new.shape
    step = min(rows, 64)
    whole, side = pl.BlockSpec((step, cols), lambda r: (r, 0)), pl.BlockSpec((step, 128), lambda r: (r, 0))
    out, line = pl.BlockSpec((1, step, cols), lambda r: (0, r, 0)), pl.BlockSpec((1, cols), lambda r: (0, 0))
    big, wide = jax.ShapeDtypeStruct((1, rows, cols), F32), jax.ShapeDtypeStruct((1, cols), F32)
    return pl.pallas_call(
        scaled_body,
        grid=(rows // step,),
        out_shape=(big, big, wide, wide),
        in_specs=[pl.BlockSpec(memory_space=VMEM), whole, whole, side, side],
        out_specs=(out, out, line, line),
        scratch_shapes=[VMEM((8, cols), F32)],
        compiler_params=pltpu.CompilerParams(vmem_limit_bytes=VMEM_LIMIT),
        cost_estimate=pl.CostEstimate(flops=8 * rows * cols, bytes_accessed=16 * rows * cols, transcendentals=0),
        name="scaled_outputs",
    )(held(peaks), first_new, second_new, by_first, by_second)


def exchange(value, axes):
    return lax.all_to_all(value, axes, split_axis=0, concat_axis=0, tiled=True)


def local(
    grad_parts, first_codes, first_rows, first_columns, second_codes, second_rows, second_columns
):
    layer_count, _, row_count, col_count = grad_parts.shape
    entries = layer_count * lax.axis_size("section") * row_count * col_count
    devices, group = lax.axis_size(AXES), lax.axis_size(FSDP)
    parts = grad_parts.reshape(RING * RING, 2, 2, -1, col_count)
    old = (first_codes, first_rows, first_columns, second_codes, second_rows, second_columns)
    gradient, squares, first_old, second_old = reduce_scatter(parts, old, devices)
    squares = exchange(squares, AXES)
    clip_limit = clip_rms * math.sqrt(entries)
    first_new, second_new, peaks = clip(squares, gradient, first_old, second_old, clip_limit, group)
    peaks = exchange(peaks, FSDP)
    direction, first_rowmax, second_rowmax, by_first, by_second = row_outputs(first_new, second_new)
    first_scaled, second_scaled, first_colmax, second_colmax = scaled_outputs(
        peaks, first_new, second_new, by_first, by_second
    )
    return (
        direction,
        first_scaled,
        second_scaled,
        first_rowmax,
        first_colmax,
        second_rowmax,
        second_colmax,
    )


def solution(mesh):
    torus = Mesh(mesh.devices.reshape(mesh.shape["section"], RING, RING, 2), AXES)
    placed = (
        P("section", FSDP, None, None),
        P("section", FSDP, None),
        P("section", FSDP),
        P("section", None),
        P("section", FSDP, None),
        P("section", FSDP),
        P("section", None),
    )
    return jax.shard_map(
        local,
        mesh=torus,
        in_specs=placed,
        out_specs=(
            P("section", FSDP, None),
            P("section", FSDP, None),
            P("section", FSDP, None),
            P("section", FSDP),
            P("section", None),
            P("section", FSDP),
            P("section", None),
        ),
        check_vma=False,
    )
```

profile of v0, /device:TPU:1, one launch (start us, length us, event | category | flops | bytes accessed | tf_op | source)
XLA Modules:
  0.0 129.1 jit_solution(10694257721634037335)
XLA Ops:
  0.6 0.1 pad_add_fusion.where.refs_2_
  0.7 2.1 %shard_map.127 = bf16[4,2,128,1024]{3,2,1,0:T(8,128)(2,1)S(1)} custom-call(s32[3]{0:T(128)S(1)} %pad_add_fusion.where.refs_2_, bf16[16,2,2,128,1024]{4,3,2,1,0:T(8,128)(2,1)} %bitcast.10), custom_call_target="tpu_custom_call" | custom-call | flops 1048576 | bytes 4194304 | tf_op jit(solution)/shard_map/pallas_call | solution.py:127
  2.9 1.5 %collective-permute-start = (bf16[4,2,128,1024]{3,2,1,0:T(8,128)(2,1)S(1)}, bf16[4,2,128,1024]{3,2,1,0:T(8,128)(2,1)S(1)}, u32[]{:S(2)}, u32[]{:S(2)}) collective-permute-start(bf16[4,2,128,1024]{3,2,1,0:T(8,128)(2,1)S(1)} %shard_map.127), channel_id=1, source_target_pairs={{0,1},{1,0},{2,3},{3,2},{4,5},{5,4},{6,7},{7,6},{8,9},{9,8},{10,11... | collective-permute-start | bytes 6291464 | tf_op jit(solution)/shard_map/ppermute | solution.py:326
  4.3 2.8 %shard_map.126 = (bf16[4,2,128,1024]{3,2,1,0:T(8,128)(2,1)S(1)}, bf16[4,2,128,1024]{3,2,1,0:T(8,128)(2,1)S(1)}) custom-call(s32[3]{0:T(128)S(1)} %pad_add_fusion.where.refs_2_, bf16[16,2,2,128,1024]{4,3,2,1,0:T(8,128)(2,1)} %bitcast.11), custom_call_target="tpu_custom_call" | custom-call | flops 2097152 | bytes 8388608 | tf_op jit(solution)/shard_map/pallas_call | solution.py:127
  7.1 0.1 collective-permute-start.1
  7.2 0.9 collective-permute-done.refs_1_
  8.1 3.0 %shard_map.128 = (s16[264,1024]{1,0:T(8,128)(2,1)S(1)}, s16[264,1024]{1,0:T(8,128)(2,1)S(1)}, s16[264,1024]{1,0:T(8,128)(2,1)S(1)}, s16[264,1024]{1,0:T(8,128)(2...) custom-call(bf16[4,2,128,1024]{3,2,1,0:T(8,128)(2,1)S(1)} %get-tuple-element.51.refs_0_, ...), custom_call_target="tpu_custom_call" | custom-call | flops 52428800 | bytes 6291456 | tf_op jit(solution)/shard_map/pallas_call | solution.py:196
  11.1 0.5 collective-permute-start.7
  11.6 0.0 collective-permute-done.1.refs_1_
  11.6 3.5 %shard_map.129 = (s16[264,1024]{1,0:T(8,128)(2,1)S(1)}, s16[264,1024]{1,0:T(8,128)(2,1)S(1)}, s16[264,1024]{1,0:T(8,128)(2,1)S(1)}, s16[264,1024]{1,0:T(8,128)(2...) custom-call(bf16[4,2,128,1024]{3,2,1,0:T(8,128)(2,1)S(1)} %get-tuple, ...), custom_call_target="tpu_custom_call" | custom-call | flops 52428800 | bytes 6291456 | tf_op jit(solution)/shard_map/pallas_call | solution.py:196
  15.1 0.2 collective-permute-start.2
  15.4 1.4 %collective-permute-start.8 = (s16[264,1024]{1,0:T(8,128)(2,1)S(1)}, s16[264,1024]{1,0:T(8,128)(2,1)S(1)}, u32[]{:S(2)}, u32[]{:S(2)}) collective-permute-start(s16[264,1024]{1,0:T(8,128)(2,1)S(1)} %get-tuple-element.63), channel_id=1, source_target_pairs={{0,8},{8,16},{16,24},{24,0},{1,9},{9,17},{17,25},{25,1},{2,10},{10... | collective-permute-start | bytes 1622024 | tf_op jit(solution)/shard_map/ppermute | solution.py:320
  16.8 1.5 %collective-permute-start.9 = (s16[264,1024]{1,0:T(8,128)(2,1)S(1)}, s16[264,1024]{1,0:T(8,128)(2,1)S(1)}, u32[]{:S(2)}, u32[]{:S(2)}) collective-permute-start(s16[264,1024]{1,0:T(8,128)(2,1)S(1)} %get-tuple-element.64), channel_id=1, source_target_pairs={{0,24},{8,0},{16,8},{24,16},{1,25},{9,1},{17,9},{25,17},{2,26},{10... | collective-permute-start | bytes 1622024 | tf_op jit(solution)/shard_map/ppermute | solution.py:320
  18.2 1.6 %collective-permute-start.10 = (s16[264,1024]{1,0:T(8,128)(2,1)S(1)}, s16[264,1024]{1,0:T(8,128)(2,1)S(1)}, u32[]{:S(2)}, u32[]{:S(2)}) collective-permute-start(s16[264,1024]{1,0:T(8,128)(2,1)S(1)} %get-tuple-element.65), channel_id=1, source_target_pairs={{0,2},{2,4},{4,6},{6,0},{1,3},{3,5},{5,7},{7,1},{8,10},{10,12},{12... | collective-permute-start | bytes 1622024 | tf_op jit(solution)/shard_map/ppermute | solution.py:320
  19.9 10.5 %collective-permute-done.8.refs_2_ = s16[264,1024]{1,0:T(8,128)(2,1)S(1)} collective-permute-done((s16[264,1024]{1,0:T(8,128)(2,1)S(1)}, s16[264,1024]{1,0:T(8,128)(2,1)S(1)}, u32[]{:S(2)}, u32[]{:S(2)}) %collective-permute-start.8) | collective-permute-done | bytes 540704 | tf_op jit(solution)/shard_map/ppermute | solution.py:320
  30.4 3.6 %collective-permute-start.11 = (s16[264,1024]{1,0:T(8,128)(2,1)S(1)}, s16[264,1024]{1,0:T(8,128)(2,1)S(1)}, u32[]{:S(2)}, u32[]{:S(2)}) collective-permute-start(s16[264,1024]{1,0:T(8,128)(2,1)S(1)} %get-tuple-element.66), channel_id=1, source_target_pairs={{0,6},{2,0},{4,2},{6,4},{1,7},{3,1},{5,3},{7,5},{8,14},{10,8},{12,... | collective-permute-start | bytes 1622024 | tf_op jit(solution)/shard_map/ppermute | solution.py:320
  34.0 2.7 %collective-permute-start.4 = (s16[264,1024]{1,0:T(8,128)(2,1)S(1)}, s16[264,1024]{1,0:T(8,128)(2,1)S(1)}, u32[]{:S(2)}, u32[]{:S(2)}) collective-permute-start(s16[264,1024]{1,0:T(8,128)(2,1)S(1)} %get-tuple-element.57), channel_id=1, source_target_pairs={{0,24},{8,0},{16,8},{24,16},{1,25},{9,1},{17,9},{25,17},{2,26},{10... | collective-permute-start | bytes 1622024 | tf_op jit(solution)/shard_map/ppermute | solution.py:320
  36.7 7.8 %collective-permute-done.11.refs_5_ = s16[264,1024]{1,0:T(8,128)(2,1)S(1)} collective-permute-done((s16[264,1024]{1,0:T(8,128)(2,1)S(1)}, s16[264,1024]{1,0:T(8,128)(2,1)S(1)}, u32[]{:S(2)}, u32[]{:S(2)}) %collective-permute-start.11) | collective-permute-done | bytes 540704 | tf_op jit(solution)/shard_map/ppermute | solution.py:320
  44.5 0.4 collective-permute-start.5
  44.9 3.0 %collective-permute-start.6 = (s16[264,1024]{1,0:T(8,128)(2,1)S(1)}, s16[264,1024]{1,0:T(8,128)(2,1)S(1)}, u32[]{:S(2)}, u32[]{:S(2)}) collective-permute-start(s16[264,1024]{1,0:T(8,128)(2,1)S(1)} %get-tuple-element.59), channel_id=1, source_target_pairs={{0,6},{2,0},{4,2},{6,4},{1,7},{3,1},{5,3},{7,5},{8,14},{10,8},{12,... | collective-permute-start | bytes 1622024 | tf_op jit(solution)/shard_map/ppermute | solution.py:320
  47.9 0.0 copy-start.4
  47.9 0.0 copy-start.5
  47.9 3.5 %shard_map.131 = (s16[264,1024]{1,0:T(8,128)(2,1)S(1)}, s16[264,1024]{1,0:T(8,128)(2,1)S(1)}, s16[264,1024]{1,0:T(8,128)(2,1)S(1)}, s16[264,1024]{1,0:T(8,128)(2,1)S(1)}) custom-call(bf16[4,2,128,1024]{3,2,1,0:T(8,128)(2,1)S(1)} %get-tuple-element.61.refs_0_, bf16[4,2,128,1024]{3,2,1,0:T(8,128)(2,1)S(1)} %collective-permute-done.7.refs_1_, ...), custom_call_target="tpu_custom_call" | custom-call | flops 52428800 | bytes 6291456 | tf_op jit(solution)/shard_map/pallas_call | solution.py:196
  51.4 0.1 collective-permute-start.17
  51.5 2.7 %collective-permute-start.18 = (s16[264,1024]{1,0:T(8,128)(2,1)S(1)}, s16[264,1024]{1,0:T(8,128)(2,1)S(1)}, u32[]{:S(2)}, u32[]{:S(2)}) collective-permute-start(s16[264,1024]{1,0:T(8,128)(2,1)S(1)} %get-tuple-element.74), channel_id=1, source_target_pairs={{0,6},{2,0},{4,2},{6,4},{1,7},{3,1},{5,3},{7,5},{8,14},{10,8},{12,... | collective-permute-start | bytes 1622024 | tf_op jit(solution)/shard_map/ppermute | solution.py:320
  54.2 4.3 %collective-permute-done.5.refs_2_ = s16[264,1024]{1,0:T(8,128)(2,1)S(1)} collective-permute-done((s16[264,1024]{1,0:T(8,128)(2,1)S(1)}, s16[264,1024]{1,0:T(8,128)(2,1)S(1)}, u32[]{:S(2)}, u32[]{:S(2)}) %collective-permute-start.5) | collective-permute-done | bytes 540704 | tf_op jit(solution)/shard_map/ppermute | solution.py:320
  58.5 0.0 collective-permute-start.12
  58.5 0.0 collective-permute-done.6.refs_3_
  58.5 2.7 %collective-permute-start.13 = (s16[264,1024]{1,0:T(8,128)(2,1)S(1)}, s16[264,1024]{1,0:T(8,128)(2,1)S(1)}, u32[]{:S(2)}, u32[]{:S(2)}) collective-permute-start(s16[264,1024]{1,0:T(8,128)(2,1)S(1)} %get-tuple-element.68), channel_id=1, source_target_pairs={{0,24},{8,0},{16,8},{24,16},{1,25},{9,1},{17,9},{25,17},{2,26},{10... | collective-permute-start | bytes 1622024 | tf_op jit(solution)/shard_map/ppermute | solution.py:320
  61.3 2.1 %shard_map.130 = (f32[2,4,128,1024]{3,2,1,0:T(8,128)S(1)}, f32[256,1024]{1,0:T(8,128)S(1)}, f32[256,1024]{1,0:T(8,128)S(1)}) custom-call(bf16[4,2,128,1024]{3,2,1,0:T(8,128)(2,1)S(1)} %get-tuple-element.54.own, bf16[4,2,128,1024]{3,2,1,0:T(8,128)(2,1)S(1)} %collective-permute-done.2.came, s16[264,1024]{1,0:T(8,128)(2,1)S(1)} %collective-permute-done.3.refs_0_, ...), custom_call_target="tpu_custom_call" | custom-call | flops 39321600 | bytes 13107200 | tf_op jit(solution)/shard_map/pallas_call | solution.py:239
  63.3 6.8 %collective-permute-done.17.first = s16[264,1024]{1,0:T(8,128)(2,1)S(1)} collective-permute-done((s16[264,1024]{1,0:T(8,128)(2,1)S(1)}, s16[264,1024]{1,0:T(8,128)(2,1)S(1)}, u32[]{:S(2)}, u32[]{:S(2)}) %collective-permute-start.17) | collective-permute-done | bytes 540704 | tf_op jit(solution)/shard_map/ppermute | solution.py:320
  70.1 1.3 %shard_map.133 = (s16[136,1024]{1,0:T(8,128)(2,1)S(1)}, s16[136,1024]{1,0:T(8,128)(2,1)S(1)}, s16[136,1024]{1,0:T(8,128)(2,1)S(1)}, f32[128,1024]{1,0:T(8,128)S(1)}) custom-call(f32[2,4,128,1024]{3,2,1,0:T(8,128)S(1)} %get-tuple-element.60.acc, s16[264,1024]{1,0:T(8,128)(2,1)S(1)} %collective-permute-done.17.first, ...), custom_call_target="tpu_custom_call" | custom-call | flops 26214400 | bytes 4194304 | tf_op jit(solution)/shard_map/pallas_call | solution.py:269
  71.4 0.1 collective-permute-start.19
  71.5 2.7 %collective-permute-start.20 = (s16[136,1024]{1,0:T(8,128)(2,1)S(1)}, s16[136,1024]{1,0:T(8,128)(2,1)S(1)}, u32[]{:S(2)}, u32[]{:S(2)}) collective-permute-start(s16[136,1024]{1,0:T(8,128)(2,1)S(1)} %get-tuple-element.77), channel_id=1, source_target_pairs={{0,24},{8,0},{16,8},{24,16},{1,25},{9,1},{17,9},{25,17},{2,26},{10... | collective-permute-start | bytes 835592 | tf_op jit(solution)/shard_map/ppermute | solution.py:320
  74.2 0.3 collective-permute-start.21
  74.4 1.3 %shard_map.132 = (s16[136,1024]{1,0:T(8,128)(2,1)S(1)}, s16[136,1024]{1,0:T(8,128)(2,1)S(1)}, s16[136,1024]{1,0:T(8,128)(2,1)S(1)}, f32[128,1024]{1,0:T(8,128)S(1)}) custom-call(f32[2,4,128,1024]{3,2,1,0:T(8,128)S(1)} %get-tuple-element.60.acc, s16[264,1024]{1,0:T(8,128)(2,1)S(1)} %collective-permute-done.12.first, ...), custom_call_target="tpu_custom_call" | custom-call | flops 26214400 | bytes 4194304 | tf_op jit(solution)/shard_map/pallas_call | solution.py:269
  75.7 0.6 collective-permute-start.14
  76.4 2.1 %collective-permute-start.15 = (s16[136,1024]{1,0:T(8,128)(2,1)S(1)}, s16[136,1024]{1,0:T(8,128)(2,1)S(1)}, u32[]{:S(2)}, u32[]{:S(2)}) collective-permute-start(s16[136,1024]{1,0:T(8,128)(2,1)S(1)} %get-tuple-element.71), channel_id=1, source_target_pairs={{0,6},{2,0},{4,2},{6,4},{1,7},{3,1},{5,3},{7,5},{8,14},{10,8},{12,... | collective-permute-start | bytes 835592 | tf_op jit(solution)/shard_map/ppermute | solution.py:320
  78.5 1.7 %collective-permute-start.16 = (s16[136,1024]{1,0:T(8,128)(2,1)S(1)}, s16[136,1024]{1,0:T(8,128)(2,1)S(1)}, u32[]{:S(2)}, u32[]{:S(2)}) collective-permute-start(s16[136,1024]{1,0:T(8,128)(2,1)S(1)} %get-tuple-element.72), channel_id=1, source_target_pairs={{0,4},{2,6},{4,0},{6,2},{1,5},{3,7},{5,1},{7,3},{8,12},{10,14},{12... | collective-permute-start | bytes 835592 | tf_op jit(solution)/shard_map/ppermute | solution.py:320
  80.2 4.1 %collective-permute-done.21.refs_7_ = s16[136,1024]{1,0:T(8,128)(2,1)S(1)} collective-permute-done((s16[136,1024]{1,0:T(8,128)(2,1)S(1)}, s16[136,1024]{1,0:T(8,128)(2,1)S(1)}, u32[]{:S(2)}, u32[]{:S(2)}) %collective-permute-start.21) | collective-permute-done | bytes 278560 | tf_op jit(solution)/shard_map/ppermute | solution.py:320
  84.4 3.7 %collective-permute-done.16.refs_3_ = s16[136,1024]{1,0:T(8,128)(2,1)S(1)} collective-permute-done((s16[136,1024]{1,0:T(8,128)(2,1)S(1)}, s16[136,1024]{1,0:T(8,128)(2,1)S(1)}, u32[]{:S(2)}, u32[]{:S(2)}) %collective-permute-start.16) | collective-permute-done | bytes 278560 | tf_op jit(solution)/shard_map/ppermute | solution.py:320
  88.0 1.0 shard_map.134
  89.0 23.0 %all_to_all.16 = f32[128,1,128]{2,1,0:T(1,128)S(1)} all-to-all(f32[128,1,128]{2,1,0:T(1,128)S(1)} %bitcast.9), channel_id=1, replica_groups=mesh['section'=4,'y'=4,'z'=4,'core'=2] {'section','y','z','core'}, dimensions={0} | all-to-all | bytes 131072 | tf_op jit(solution)/shard_map/all_to_all | solution.py:471
  112.1 1.2 shard_map.135
  113.3 4.7 %all-to-all-start.1 = ((f32[32,16,128]{2,1,0:T(8,128)}), f32[32,16,128]{2,1,0:T(8,128)S(1)}, u32[]{:S(2)}, u32[]{:S(2)}) async-start(f32[32,16,128]{2,1,0:T(8,128)} %get-tuple-element.86), calls=%async_computation.1 | async-start | bytes 524288 | tf_op jit(solution)/shard_map/all_to_all | solution.py:471
  118.0 1.3 %row_outputs.1 = (f32[1,256,1024]{2,1,0:T(8,128)}, f32[1,256]{1,0:T(1,128)}, f32[1,256]{1,0:T(1,128)}, f32[256,128]{1,0:T(8,128)S(1)}, f32[256,128]{1,0:T(8,128)S(1)}) custom-call(f32[256,1024]{1,0:T(8,128)S(1)} %get-tuple-element.83.first_new, f32[256,1024]{1,0:T(8,128)S(1)} %get-tuple-element.84.second_new), custom_call_target="tpu_custom_call" | custom-call | flops 10485760 | bytes 3145728 | tf_op jit(solution)/shard_map/row_outputs/pallas_call | solution.py:414
  119.4 7.7 %all-to-all-done.1.peaks = f32[32,16,128]{2,1,0:T(8,128)S(1)} async-done(((f32[32,16,128]{2,1,0:T(8,128)}), f32[32,16,128]{2,1,0:T(8,128)S(1)}, u32[]{:S(2)}, u32[]{:S(2)}) %all-to-all-start.1) | async-done | bytes 262176 | tf_op jit(solution)/shard_map/all_to_all | solution.py:471
  127.1 2.0 %scaled_outputs.1 = (f32[1,256,1024]{2,1,0:T(8,128)}, f32[1,256,1024]{2,1,0:T(8,128)}, f32[1,1024]{1,0:T(1,128)}, f32[1,1024]{1,0:T(1,128)}) custom-call(f32[32,16,128]{2,1,0:T(8,128)S(1)} %all-to-all-done.1.peaks, f32[256,1024]{1,0:T(8,128)S(1)} %get-tuple-element.83.first_new, f32[256,1024]{1,0:T(8,128)S(1)} %get-tuple-element.84.second_new, ...), custom_call_target="tpu_custom_call" | custom-call | flops 2097152 | bytes 4194304 | tf_op jit(solution)/shard_map/scaled_outputs/pallas_call | solution.py:457
  (24 shorter events, 0.1 us)
Async XLA Ops:
  2.9 5.2 %collective-permute-start = (bf16[4,2,128,1024]{3,2,1,0:T(8,128)(2,1)S(1)}, bf16[4,2,128,1024]{3,2,1,0:T(8,128)(2,1)S(1)}, u32[]{:S(2)}, u32[]{:S(2)}) collective-permute-start(bf16[4,2,128,1024]{3,2,1,0:T(8,128)(2,1)S(1)} %shard_map.127), channel_id=1, source_target_pairs={{0,1},{1,0},{2,3},{3,2},{4,5},{5,4},{6,7},{7,6},{8,9},{9,8},{10,11... | collective-permute-start | bytes 6291464 | tf_op jit(solution)/shard_map/ppermute | solution.py:326
  7.1 4.5 %collective-permute-start.1 = (bf16[4,2,128,1024]{3,2,1,0:T(8,128)(2,1)S(1)}, bf16[4,2,128,1024]{3,2,1,0:T(8,128)(2,1)S(1)}, u32[]{:S(2)}, u32[]{:S(2)}) collective-permute-start(bf16[4,2,128,1024]{3,2,1,0:T(8,128)(2,1)S(1)} %get-tuple-element.53), channel_id=1, source_target_pairs={{0,1},{1,0},{2,3},{3,2},{4,5},{5,4},{6,7},{7,6},{8,9},{9,8},{10,11... | collective-permute-start | bytes 6291464 | tf_op jit(solution)/shard_map/ppermute | solution.py:326
  11.1 33.8 %collective-permute-start.7 = (bf16[4,2,128,1024]{3,2,1,0:T(8,128)(2,1)S(1)}, bf16[4,2,128,1024]{3,2,1,0:T(8,128)(2,1)S(1)}, u32[]{:S(2)}, u32[]{:S(2)}) collective-permute-start(bf16[4,2,128,1024]{3,2,1,0:T(8,128)(2,1)S(1)} %get-tuple-element.62), channel_id=1, source_target_pairs={{0,1},{1,0},{2,3},{3,2},{4,5},{5,4},{6,7},{7,6},{8,9},{9,8},{10,11... | collective-permute-start | bytes 6291464 | tf_op jit(solution)/shard_map/ppermute | solution.py:326
  15.1 46.1 %collective-permute-start.2 = (bf16[4,2,128,1024]{3,2,1,0:T(8,128)(2,1)S(1)}, bf16[4,2,128,1024]{3,2,1,0:T(8,128)(2,1)S(1)}, u32[]{:S(2)}, u32[]{:S(2)}) collective-permute-start(bf16[4,2,128,1024]{3,2,1,0:T(8,128)(2,1)S(1)} %get-tuple-element.55), channel_id=1, source_target_pairs={{0,1},{1,0},{2,3},{3,2},{4,5},{5,4},{6,7},{7,6},{8,9},{9,8},{10,11... | collective-permute-start | bytes 6291464 | tf_op jit(solution)/shard_map/ppermute | solution.py:326
  15.4 15.0 %collective-permute-start.8 = (s16[264,1024]{1,0:T(8,128)(2,1)S(1)}, s16[264,1024]{1,0:T(8,128)(2,1)S(1)}, u32[]{:S(2)}, u32[]{:S(2)}) collective-permute-start(s16[264,1024]{1,0:T(8,128)(2,1)S(1)} %get-tuple-element.63), channel_id=1, source_target_pairs={{0,8},{8,16},{16,24},{24,0},{1,9},{9,17},{17,25},{25,1},{2,10},{10... | collective-permute-start | bytes 1622024 | tf_op jit(solution)/shard_map/ppermute | solution.py:320
  16.8 17.3 %collective-permute-start.9 = (s16[264,1024]{1,0:T(8,128)(2,1)S(1)}, s16[264,1024]{1,0:T(8,128)(2,1)S(1)}, u32[]{:S(2)}, u32[]{:S(2)}) collective-permute-start(s16[264,1024]{1,0:T(8,128)(2,1)S(1)} %get-tuple-element.64), channel_id=1, source_target_pairs={{0,24},{8,0},{16,8},{24,16},{1,25},{9,1},{17,9},{25,17},{2,26},{10... | collective-permute-start | bytes 1622024 | tf_op jit(solution)/shard_map/ppermute | solution.py:320
  18.2 15.8 %collective-permute-start.10 = (s16[264,1024]{1,0:T(8,128)(2,1)S(1)}, s16[264,1024]{1,0:T(8,128)(2,1)S(1)}, u32[]{:S(2)}, u32[]{:S(2)}) collective-permute-start(s16[264,1024]{1,0:T(8,128)(2,1)S(1)} %get-tuple-element.65), channel_id=1, source_target_pairs={{0,2},{2,4},{4,6},{6,0},{1,3},{3,5},{5,7},{7,1},{8,10},{10,12},{12... | collective-permute-start | bytes 1622024 | tf_op jit(solution)/shard_map/ppermute | solution.py:320
  30.4 14.1 %collective-permute-start.11 = (s16[264,1024]{1,0:T(8,128)(2,1)S(1)}, s16[264,1024]{1,0:T(8,128)(2,1)S(1)}, u32[]{:S(2)}, u32[]{:S(2)}) collective-permute-start(s16[264,1024]{1,0:T(8,128)(2,1)S(1)} %get-tuple-element.66), channel_id=1, source_target_pairs={{0,6},{2,0},{4,2},{6,4},{1,7},{3,1},{5,3},{7,5},{8,14},{10,8},{12,... | collective-permute-start | bytes 1622024 | tf_op jit(solution)/shard_map/ppermute | solution.py:320
  34.0 17.4 %collective-permute-start.3 = (s16[264,1024]{1,0:T(8,128)(2,1)S(1)}, s16[264,1024]{1,0:T(8,128)(2,1)S(1)}, u32[]{:S(2)}, u32[]{:S(2)}) collective-permute-start(s16[264,1024]{1,0:T(8,128)(2,1)S(1)} %get-tuple-element.56), channel_id=1, source_target_pairs={{0,8},{8,16},{16,24},{24,0},{1,9},{9,17},{17,25},{25,1},{2,10},{10... | collective-permute-start | bytes 1622024 | tf_op jit(solution)/shard_map/ppermute | solution.py:320
  34.0 17.5 %collective-permute-start.4 = (s16[264,1024]{1,0:T(8,128)(2,1)S(1)}, s16[264,1024]{1,0:T(8,128)(2,1)S(1)}, u32[]{:S(2)}, u32[]{:S(2)}) collective-permute-start(s16[264,1024]{1,0:T(8,128)(2,1)S(1)} %get-tuple-element.57), channel_id=1, source_target_pairs={{0,24},{8,0},{16,8},{24,16},{1,25},{9,1},{17,9},{25,17},{2,26},{10... | collective-permute-start | bytes 1622024 | tf_op jit(solution)/shard_map/ppermute | solution.py:320
  44.5 14.0 %collective-permute-start.5 = (s16[264,1024]{1,0:T(8,128)(2,1)S(1)}, s16[264,1024]{1,0:T(8,128)(2,1)S(1)}, u32[]{:S(2)}, u32[]{:S(2)}) collective-permute-start(s16[264,1024]{1,0:T(8,128)(2,1)S(1)} %get-tuple-element.58), channel_id=1, source_target_pairs={{0,2},{2,4},{4,6},{6,0},{1,3},{3,5},{5,7},{7,1},{8,10},{10,12},{12... | collective-permute-start | bytes 1622024 | tf_op jit(solution)/shard_map/ppermute | solution.py:320
  44.9 13.6 %collective-permute-start.6 = (s16[264,1024]{1,0:T(8,128)(2,1)S(1)}, s16[264,1024]{1,0:T(8,128)(2,1)S(1)}, u32[]{:S(2)}, u32[]{:S(2)}) collective-permute-start(s16[264,1024]{1,0:T(8,128)(2,1)S(1)} %get-tuple-element.59), channel_id=1, source_target_pairs={{0,6},{2,0},{4,2},{6,4},{1,7},{3,1},{5,3},{7,5},{8,14},{10,8},{12,... | collective-permute-start | bytes 1622024 | tf_op jit(solution)/shard_map/ppermute | solution.py:320
  47.9 13.3 %copy-start = (s32[1,256,1024]{2,1,0:T(8,128)S(1)}, s32[1,256,1024]{2,1,0:T(8,128)}, u32[]{:S(2)}) copy-start(s32[1,256,1024]{2,1,0:T(8,128)} %refs_4_.1) | copy-start | bytes 3145732
  47.9 13.3 %copy-start.1 = (s32[1,256,1024]{2,1,0:T(8,128)S(1)}, s32[1,256,1024]{2,1,0:T(8,128)}, u32[]{:S(2)}) copy-start(s32[1,256,1024]{2,1,0:T(8,128)} %refs_7_.1) | copy-start | bytes 3145732
  47.9 13.3 %copy-start.2 = (f32[1,1024]{1,0:T(1,128)S(1)}, f32[1,1024]{1,0:T(1,128)}, u32[]{:S(2)}) copy-start(f32[1,1024]{1,0:T(1,128)} %refs_6_.1) | copy-start | bytes 12292
  47.9 13.3 %copy-start.3 = (f32[1,1024]{1,0:T(1,128)S(1)}, f32[1,1024]{1,0:T(1,128)}, u32[]{:S(2)}) copy-start(f32[1,1024]{1,0:T(1,128)} %refs_9_.1) | copy-start | bytes 12292
  47.9 13.3 %copy-start.4 = (f32[1,256]{1,0:T(1,128)S(1)}, f32[1,256]{1,0:T(1,128)}, u32[]{:S(2)}) copy-start(f32[1,256]{1,0:T(1,128)} %refs_5_.1) | copy-start | bytes 3076
  47.9 13.3 %copy-start.5 = (f32[1,256]{1,0:T(1,128)S(1)}, f32[1,256]{1,0:T(1,128)}, u32[]{:S(2)}) copy-start(f32[1,256]{1,0:T(1,128)} %refs_8_.1) | copy-start | bytes 3076
  51.4 18.7 %collective-permute-start.17 = (s16[264,1024]{1,0:T(8,128)(2,1)S(1)}, s16[264,1024]{1,0:T(8,128)(2,1)S(1)}, u32[]{:S(2)}, u32[]{:S(2)}) collective-permute-start(s16[264,1024]{1,0:T(8,128)(2,1)S(1)} %get-tuple-element.73), channel_id=1, source_target_pairs={{0,2},{2,4},{4,6},{6,0},{1,3},{3,5},{5,7},{7,1},{8,10},{10,12},{12... | collective-permute-start | bytes 1622024 | tf_op jit(solution)/shard_map/ppermute | solution.py:320
  51.5 18.6 %collective-permute-start.18 = (s16[264,1024]{1,0:T(8,128)(2,1)S(1)}, s16[264,1024]{1,0:T(8,128)(2,1)S(1)}, u32[]{:S(2)}, u32[]{:S(2)}) collective-permute-start(s16[264,1024]{1,0:T(8,128)(2,1)S(1)} %get-tuple-element.74), channel_id=1, source_target_pairs={{0,6},{2,0},{4,2},{6,4},{1,7},{3,1},{5,3},{7,5},{8,14},{10,8},{12,... | collective-permute-start | bytes 1622024 | tf_op jit(solution)/shard_map/ppermute | solution.py:320
  58.5 15.9 %collective-permute-start.12 = (s16[264,1024]{1,0:T(8,128)(2,1)S(1)}, s16[264,1024]{1,0:T(8,128)(2,1)S(1)}, u32[]{:S(2)}, u32[]{:S(2)}) collective-permute-start(s16[264,1024]{1,0:T(8,128)(2,1)S(1)} %get-tuple-element.67), channel_id=1, source_target_pairs={{0,8},{8,16},{16,24},{24,0},{1,9},{9,17},{17,25},{25,1},{2,10},{10... | collective-permute-start | bytes 1622024 | tf_op jit(solution)/shard_map/ppermute | solution.py:320
  58.5 15.9 %collective-permute-start.13 = (s16[264,1024]{1,0:T(8,128)(2,1)S(1)}, s16[264,1024]{1,0:T(8,128)(2,1)S(1)}, u32[]{:S(2)}, u32[]{:S(2)}) collective-permute-start(s16[264,1024]{1,0:T(8,128)(2,1)S(1)} %get-tuple-element.68), channel_id=1, source_target_pairs={{0,24},{8,0},{16,8},{24,16},{1,25},{9,1},{17,9},{25,17},{2,26},{10... | collective-permute-start | bytes 1622024 | tf_op jit(solution)/shard_map/ppermute | solution.py:320
  71.4 7.1 %collective-permute-start.19 = (s16[136,1024]{1,0:T(8,128)(2,1)S(1)}, s16[136,1024]{1,0:T(8,128)(2,1)S(1)}, u32[]{:S(2)}, u32[]{:S(2)}) collective-permute-start(s16[136,1024]{1,0:T(8,128)(2,1)S(1)} %get-tuple-element.76), channel_id=1, source_target_pairs={{0,8},{8,16},{16,24},{24,0},{1,9},{9,17},{17,25},{25,1},{2,10},{10... | collective-permute-start | bytes 835592 | tf_op jit(solution)/shard_map/ppermute | solution.py:320
  71.5 8.7 %collective-permute-start.20 = (s16[136,1024]{1,0:T(8,128)(2,1)S(1)}, s16[136,1024]{1,0:T(8,128)(2,1)S(1)}, u32[]{:S(2)}, u32[]{:S(2)}) collective-permute-start(s16[136,1024]{1,0:T(8,128)(2,1)S(1)} %get-tuple-element.77), channel_id=1, source_target_pairs={{0,24},{8,0},{16,8},{24,16},{1,25},{9,1},{17,9},{25,17},{2,26},{10... | collective-permute-start | bytes 835592 | tf_op jit(solution)/shard_map/ppermute | solution.py:320
  74.2 10.2 %collective-permute-start.21 = (s16[136,1024]{1,0:T(8,128)(2,1)S(1)}, s16[136,1024]{1,0:T(8,128)(2,1)S(1)}, u32[]{:S(2)}, u32[]{:S(2)}) collective-permute-start(s16[136,1024]{1,0:T(8,128)(2,1)S(1)} %get-tuple-element.78), channel_id=1, source_target_pairs={{0,16},{8,24},{16,0},{24,8},{1,17},{9,25},{17,1},{25,9},{2,18},{10... | collective-permute-start | bytes 835592 | tf_op jit(solution)/shard_map/ppermute | solution.py:320
  75.7 8.6 %collective-permute-start.14 = (s16[136,1024]{1,0:T(8,128)(2,1)S(1)}, s16[136,1024]{1,0:T(8,128)(2,1)S(1)}, u32[]{:S(2)}, u32[]{:S(2)}) collective-permute-start(s16[136,1024]{1,0:T(8,128)(2,1)S(1)} %get-tuple-element.70), channel_id=1, source_target_pairs={{0,2},{2,4},{4,6},{6,0},{1,3},{3,5},{5,7},{7,1},{8,10},{10,12},{12... | collective-permute-start | bytes 835592 | tf_op jit(solution)/shard_map/ppermute | solution.py:320
  76.4 8.0 %collective-permute-start.15 = (s16[136,1024]{1,0:T(8,128)(2,1)S(1)}, s16[136,1024]{1,0:T(8,128)(2,1)S(1)}, u32[]{:S(2)}, u32[]{:S(2)}) collective-permute-start(s16[136,1024]{1,0:T(8,128)(2,1)S(1)} %get-tuple-element.71), channel_id=1, source_target_pairs={{0,6},{2,0},{4,2},{6,4},{1,7},{3,1},{5,3},{7,5},{8,14},{10,8},{12,... | collective-permute-start | bytes 835592 | tf_op jit(solution)/shard_map/ppermute | solution.py:320
  78.5 9.5 %collective-permute-start.16 = (s16[136,1024]{1,0:T(8,128)(2,1)S(1)}, s16[136,1024]{1,0:T(8,128)(2,1)S(1)}, u32[]{:S(2)}, u32[]{:S(2)}) collective-permute-start(s16[136,1024]{1,0:T(8,128)(2,1)S(1)} %get-tuple-element.72), channel_id=1, source_target_pairs={{0,4},{2,6},{4,0},{6,2},{1,5},{3,7},{5,1},{7,3},{8,12},{10,14},{12... | collective-permute-start | bytes 835592 | tf_op jit(solution)/shard_map/ppermute | solution.py:320
  113.3 13.8 %all-to-all-start.1 = ((f32[32,16,128]{2,1,0:T(8,128)}), f32[32,16,128]{2,1,0:T(8,128)S(1)}, u32[]{:S(2)}, u32[]{:S(2)}) async-start(f32[32,16,128]{2,1,0:T(8,128)} %get-tuple-element.86), calls=%async_computation.1 | async-start | bytes 524288 | tf_op jit(solution)/shard_map/all_to_all | solution.py:471
where the time goes:
time: 129 us
  waiting for transfers between devices  45.8 us (36%)
  starting transfers between devices  34.1 us (26%)
  Pallas kernels  25.3 us (20%)
  blocking collectives  23 us (18%)
    ppermute x18, waiting for transfers between devices, hop(): lax.ppermute(value, name, [(i, (i + delta) % RING) for i in range(RING)])  37.2 us
    ppermute x18, starting transfers between devices, hop(): lax.ppermute(value, name, [(i, (i + delta) % RING) for i in range(RING)])  27.1 us
    all_to_all x1, blocking collectives, exchange(): return lax.all_to_all(value, axes, split_axis=0, concat_axis=0, tiled=True)  23 us
    pallas_call x3, Pallas kernels, pair(): call(functools.partial(pair_body, len(relayed), wanted), outs, scratch, 4...  10.1 us
    all_to_all x1, waiting for transfers between devices, exchange(): return lax.all_to_all(value, axes, split_axis=0, concat_axis=0, tiled=True)  7.72 us
    pallas_call x2, Pallas kernels, gather(): call(body, outs, [sem], moved // 4, moved, gather_specs())(where, parts)  4.96 us
    all_to_all x1, starting transfers between devices, exchange(): return lax.all_to_all(value, axes, split_axis=0, concat_axis=0, tiled=True)  4.75 us
    pallas_call x2, Pallas kernels, middle(): call(functools.partial(middle_body, half), (sent, sent, sent, VMEM((rows,...  2.62 us
  transfers between devices with their start and end apart: 23, of which 8 were waited for; matrix products, arithmetic and copies ran while one was open for 0% of the time, Pallas kernels for 15%

commit v1 on v0

--- a/solution.py
+++ b/solution.py
@@ -210,7 +210,7 @@
 
 
 def keep_body(own, came, *refs):
-    got, (old, total, first_old, second_old) = refs[:4], (refs[4:10], *refs[10:])
+    got, total = refs[:4], refs[4]
     rows = own.shape[2]
     for half in range(2):
         for i in range(RING):
@@ -223,9 +223,19 @@
                 total[half, i, pl.ds(r, STEP), :] = value + decode(ref[pl.ds(i % 2 * rows + r, STEP), :], by)
 
             chunks(rows, step, None)
-    for (codes, row, column), levels, beta, out in (
-        (old[:3], 7.0, beta_first, first_old),
-        (old[3:], 15.0, beta_second, second_old),
+
+
+def keep(own, came, got):
+    rows, cols = own.shape[2:]
+    return call(
+        keep_body, (VMEM((2, RING, rows, cols), F32),), [], 200 * rows * cols, 80 * rows * cols, in_vmem(6)
+    )(own, held(came), *[held(g) for g in got])[0]
+
+
+def old_body(*refs):
+    for (codes, row, column, out), levels, beta in (
+        ((*refs[:3], refs[6]), 7.0, beta_first),
+        ((*refs[3:6], refs[7]), 15.0, beta_second),
     ):
         tall, wide = column_of(row[...]), column[...]
         for r in range(0, out.shape[0], STEP):
@@ -233,12 +243,10 @@
             out[r : r + STEP, :] = codes[0, r : r + STEP, :].astype(F32) * (beta / levels) * bound
 
 
-def keep(own, came, got, old):
-    rows, cols = own.shape[2:]
-    each = VMEM((2 * rows, cols), F32)
-    return call(
-        keep_body, (VMEM((2, RING, rows, cols), F32), each, each), [], 300 * rows * cols, 100 * rows * cols, in_vmem(12)
-    )(own, held(came), *[held(g) for g in got], *old)
+def old_moments(old):
+    _, rows, cols = old[0].shape
+    each = VMEM((rows, cols), F32)
+    return call(old_body, (each, each), [], 10 * rows * cols, 16 * rows * cols, in_vmem(6))(*old)
 
 
 def middle_body(half, acc, first, second, *refs):
@@ -311,7 +319,7 @@
     )(*flat)
 
 
-def reduce_scatter(parts, old, devices):
+def reduce_scatter(parts, devices):
     where = jnp.stack([lax.axis_index(a) for a in FSDP]).astype(jnp.int32)
     parts = pltpu.with_memory_space_constraint(parts, pltpu.HBM)
     axis = ("y", "z")
@@ -345,13 +353,14 @@
     came_mine = swap(out_mine)
     sent, _ = pair(own_join, came_join, got_far)
     got_join = four_ways(sent)
-    acc, first_old, second_old = keep(own_mine, came_mine, got_near, old)
+    acc = keep(own_mine, came_mine, got_near)
     halves = []
     for half in range(2):
         *out, kept = middle(acc, got_join[2 * half], got_join[2 * half + 1], half)
-        got = {d: hop(out[k], axis[1 - half], d) for k, d in ((2, 2), (0, 1), (1, 3))}
-        halves.append([kept, got[1], got[3], got[2]])
-    return *last(halves, devices), first_old, second_old
+        got = [hop(out[2], axis[1 - half], 2)]
+        got += [hop(out[0], axis[1 - half], 1), hop(out[1], axis[1 - half], 3)]
+        halves.append([kept] + got)
+    return last(halves, devices)
 
 
 def clip_body(limit, squares, grad, first_old, second_old, first_new, second_new, peaks):
@@ -479,8 +488,9 @@
     devices, group = lax.axis_size(AXES), lax.axis_size(FSDP)
     parts = grad_parts.reshape(RING * RING, 2, 2, -1, col_count)
     old = (first_codes, first_rows, first_columns, second_codes, second_rows, second_columns)
-    gradient, squares, first_old, second_old = reduce_scatter(parts, old, devices)
+    gradient, squares = reduce_scatter(parts, devices)
     squares = exchange(squares, AXES)
+    first_old, second_old = old_moments(old)
     clip_limit = clip_rms * math.sqrt(entries)
     first_new, second_new, peaks = clip(squares, gradient, first_old, second_old, clip_limit, group)
     peaks = exchange(peaks, FSDP)

time: 129 us -> 133 us (1.031)
  blocking collectives: 23 us -> 0 us
  starting transfers between devices: 34.1 us -> 45.1 us
  waiting for transfers between devices: 45.8 us -> 56.2 us
  local copies, waits for them, and re-layouts: 0.03 us -> 4.42 us
    all_to_all x1 -> x0, blocking collectives: 23 us -> none  [exchange(): return lax.all_to_all(value, axes, split_axis=0, concat_axis=0, tiled=True)]
    all_to_all x1 -> x2, starting transfers between devices: 4.75 us -> 15 us  [exchange(): return lax.all_to_all(value, axes, split_axis=0, concat_axis=0, tiled=True)]
    all_to_all x1 -> x2, waiting for transfers between devices: 7.72 us -> 14.6 us  [exchange(): return lax.all_to_all(value, axes, split_axis=0, concat_axis=0, tiled=True)]
    unnamed x12 -> x20, local copies, waits for them, and re-layouts: 0.03 us -> 4.42 us
    ppermute x18, waiting for transfers between devices: 37.2 us -> 40.7 us  [hop(): lax.ppermute(value, name, [(i, (i + delta) % RING) for i in range(RING)])]
  transfers between devices with their start and end apart: 23 -> 24, of which waited for: 8 -> 10; matrix products, arithmetic and copies ran while one was open for 0% -> 0% of each run, Pallas kernels for 15% -> 14%
where the time goes in v1:
time: 133 us
  waiting for transfers between devices  56.2 us (42%)
  starting transfers between devices  45.1 us (34%)
  Pallas kernels  25.9 us (19%)
  local copies, waits for them, and re-layouts  4.42 us (3%)
    ppermute x18, waiting for transfers between devices, hop(): lax.ppermute(value, name, [(i, (i + delta) % RING) for i in range(RING)])  40.7 us
    ppermute x18, starting transfers between devices, hop(): lax.ppermute(value, name, [(i, (i + delta) % RING) for i in range(RING)])  27.9 us
    all_to_all x2, starting transfers between devices, exchange(): return lax.all_to_all(value, axes, split_axis=0, concat_axis=0, tiled=True)  15 us
    all_to_all x2, waiting for transfers between devices, exchange(): return lax.all_to_all(value, axes, split_axis=0, concat_axis=0, tiled=True)  14.6 us
    pallas_call x3, Pallas kernels, pair(): call(functools.partial(pair_body, len(relayed), wanted), outs, scratch, 4...  10 us
    pallas_call x2, Pallas kernels, gather(): call(body, outs, [sem], moved // 4, moved, gather_specs())(where, parts)  4.96 us
    unnamed x20, local copies, waits for them, and re-layouts  4.42 us
  transfers between devices with their start and end apart: 24, of which 10 were waited for; matrix products, arithmetic and copies ran while one was open for 0% of the time, Pallas kernels for 14%

profile of v1, /device:TPU:1, one launch (start us, length us, event | category | flops | bytes accessed | tf_op | source)
XLA Modules:
  0.0 132.5 jit_solution(2445647534253029013)
XLA Ops:
  0.7 2.1 %shard_map.127 = bf16[4,2,128,1024]{3,2,1,0:T(8,128)(2,1)S(1)} custom-call(s32[3]{0:T(128)S(1)} %pad_add_fusion.where.refs_2_, bf16[16,2,2,128,1024]{4,3,2,1,0:T(8,128)(2,1)} %bitcast.9), custom_call_target="tpu_custom_call" | custom-call | flops 1048576 | bytes 4194304 | tf_op jit(solution)/shard_map/pallas_call | solution.py:127
  2.9 1.5 %collective-permute-start = (bf16[4,2,128,1024]{3,2,1,0:T(8,128)(2,1)S(1)}, bf16[4,2,128,1024]{3,2,1,0:T(8,128)(2,1)S(1)}, u32[]{:S(2)}, u32[]{:S(2)}) collective-permute-start(bf16[4,2,128,1024]{3,2,1,0:T(8,128)(2,1)S(1)} %shard_map.127), channel_id=1, source_target_pairs={{0,1},{1,0},{2,3},{3,2},{4,5},{5,4},{6,7},{7,6},{8,9},{9,8},{10,11... | collective-permute-start | bytes 6291464 | tf_op jit(solution)/shard_map/ppermute | solution.py:334
  4.3 2.8 %shard_map.126 = (bf16[4,2,128,1024]{3,2,1,0:T(8,128)(2,1)S(1)}, bf16[4,2,128,1024]{3,2,1,0:T(8,128)(2,1)S(1)}) custom-call(s32[3]{0:T(128)S(1)} %pad_add_fusion.where.refs_2_, bf16[16,2,2,128,1024]{4,3,2,1,0:T(8,128)(2,1)} %bitcast.10), custom_call_target="tpu_custom_call" | custom-call | flops 2097152 | bytes 8388608 | tf_op jit(solution)/shard_map/pallas_call | solution.py:127
  7.1 0.1 collective-permute-start.1
  7.2 0.9 collective-permute-done.refs_1_
  8.1 3.1 %shard_map.128 = (s16[264,1024]{1,0:T(8,128)(2,1)S(1)}, s16[264,1024]{1,0:T(8,128)(2,1)S(1)}, s16[264,1024]{1,0:T(8,128)(2,1)S(1)}, s16[264,1024]{1,0:T(8,128)(2...) custom-call(bf16[4,2,128,1024]{3,2,1,0:T(8,128)(2,1)S(1)} %get-tuple-element.50.refs_0_, ...), custom_call_target="tpu_custom_call" | custom-call | flops 52428800 | bytes 6291456 | tf_op jit(solution)/shard_map/pallas_call | solution.py:196
  11.2 0.5 collective-permute-start.7
  11.6 3.5 %shard_map.129 = (s16[264,1024]{1,0:T(8,128)(2,1)S(1)}, s16[264,1024]{1,0:T(8,128)(2,1)S(1)}, s16[264,1024]{1,0:T(8,128)(2,1)S(1)}, s16[264,1024]{1,0:T(8,128)(2...) custom-call(bf16[4,2,128,1024]{3,2,1,0:T(8,128)(2,1)S(1)} %get-tuple, ...), custom_call_target="tpu_custom_call" | custom-call | flops 52428800 | bytes 6291456 | tf_op jit(solution)/shard_map/pallas_call | solution.py:196
  15.2 0.2 collective-permute-start.2
  15.4 1.7 %collective-permute-start.10 = (s16[264,1024]{1,0:T(8,128)(2,1)S(1)}, s16[264,1024]{1,0:T(8,128)(2,1)S(1)}, u32[]{:S(2)}, u32[]{:S(2)}) collective-permute-start(s16[264,1024]{1,0:T(8,128)(2,1)S(1)} %get-tuple-element.63), channel_id=1, source_target_pairs={{0,2},{2,4},{4,6},{6,0},{1,3},{3,5},{5,7},{7,1},{8,10},{10,12},{12... | collective-permute-start | bytes 1622024 | tf_op jit(solution)/shard_map/ppermute | solution.py:328
  17.1 2.1 %collective-permute-start.11 = (s16[264,1024]{1,0:T(8,128)(2,1)S(1)}, s16[264,1024]{1,0:T(8,128)(2,1)S(1)}, u32[]{:S(2)}, u32[]{:S(2)}) collective-permute-start(s16[264,1024]{1,0:T(8,128)(2,1)S(1)} %get-tuple-element.64), channel_id=1, source_target_pairs={{0,6},{2,0},{4,2},{6,4},{1,7},{3,1},{5,3},{7,5},{8,14},{10,8},{12,... | collective-permute-start | bytes 1622024 | tf_op jit(solution)/shard_map/ppermute | solution.py:328
  19.3 1.3 collective-permute-start.8
  20.6 11.0 %collective-permute-done.10.refs_4_ = s16[264,1024]{1,0:T(8,128)(2,1)S(1)} collective-permute-done((s16[264,1024]{1,0:T(8,128)(2,1)S(1)}, s16[264,1024]{1,0:T(8,128)(2,1)S(1)}, u32[]{:S(2)}, u32[]{:S(2)}) %collective-permute-start.10) | collective-permute-done | bytes 540704 | tf_op jit(solution)/shard_map/ppermute | solution.py:328
  31.5 2.7 %collective-permute-start.9 = (s16[264,1024]{1,0:T(8,128)(2,1)S(1)}, s16[264,1024]{1,0:T(8,128)(2,1)S(1)}, u32[]{:S(2)}, u32[]{:S(2)}) collective-permute-start(s16[264,1024]{1,0:T(8,128)(2,1)S(1)} %get-tuple-element.62), channel_id=1, source_target_pairs={{0,24},{8,0},{16,8},{24,16},{1,25},{9,1},{17,9},{25,17},{2,26},{10... | collective-permute-start | bytes 1622024 | tf_op jit(solution)/shard_map/ppermute | solution.py:328
  34.3 2.7 %collective-permute-start.4 = (s16[264,1024]{1,0:T(8,128)(2,1)S(1)}, s16[264,1024]{1,0:T(8,128)(2,1)S(1)}, u32[]{:S(2)}, u32[]{:S(2)}) collective-permute-start(s16[264,1024]{1,0:T(8,128)(2,1)S(1)} %get-tuple-element.56), channel_id=1, source_target_pairs={{0,24},{8,0},{16,8},{24,16},{1,25},{9,1},{17,9},{25,17},{2,26},{10... | collective-permute-start | bytes 1622024 | tf_op jit(solution)/shard_map/ppermute | solution.py:328
  36.9 8.0 %collective-permute-done.9.refs_3_ = s16[264,1024]{1,0:T(8,128)(2,1)S(1)} collective-permute-done((s16[264,1024]{1,0:T(8,128)(2,1)S(1)}, s16[264,1024]{1,0:T(8,128)(2,1)S(1)}, u32[]{:S(2)}, u32[]{:S(2)}) %collective-permute-start.9) | collective-permute-done | bytes 540704 | tf_op jit(solution)/shard_map/ppermute | solution.py:328
  44.9 2.7 %collective-permute-start.6 = (s16[264,1024]{1,0:T(8,128)(2,1)S(1)}, s16[264,1024]{1,0:T(8,128)(2,1)S(1)}, u32[]{:S(2)}, u32[]{:S(2)}) collective-permute-start(s16[264,1024]{1,0:T(8,128)(2,1)S(1)} %get-tuple-element.58), channel_id=1, source_target_pairs={{0,6},{2,0},{4,2},{6,4},{1,7},{3,1},{5,3},{7,5},{8,14},{10,8},{12,... | collective-permute-start | bytes 1622024 | tf_op jit(solution)/shard_map/ppermute | solution.py:328
  47.6 3.5 %shard_map.131 = (s16[264,1024]{1,0:T(8,128)(2,1)S(1)}, s16[264,1024]{1,0:T(8,128)(2,1)S(1)}, s16[264,1024]{1,0:T(8,128)(2,1)S(1)}, s16[264,1024]{1,0:T(8,128)(2,1)S(1)}) custom-call(bf16[4,2,128,1024]{3,2,1,0:T(8,128)(2,1)S(1)} %get-tuple-element.59.refs_0_, bf16[4,2,128,1024]{3,2,1,0:T(8,128)(2,1)S(1)} %collective-permute-done.7.refs_1_, ...), custom_call_target="tpu_custom_call" | custom-call | flops 52428800 | bytes 6291456 | tf_op jit(solution)/shard_map/pallas_call | solution.py:196
  51.2 5.3 %collective-permute-done.4.refs_1_ = s16[264,1024]{1,0:T(8,128)(2,1)S(1)} collective-permute-done((s16[264,1024]{1,0:T(8,128)(2,1)S(1)}, s16[264,1024]{1,0:T(8,128)(2,1)S(1)}, u32[]{:S(2)}, u32[]{:S(2)}) %collective-permute-start.4) | collective-permute-done | bytes 540704 | tf_op jit(solution)/shard_map/ppermute | solution.py:328
  56.5 0.9 collective-permute-start.18
  57.4 0.8 collective-permute-start.12
  58.2 2.9 %collective-permute-start.13 = (s16[264,1024]{1,0:T(8,128)(2,1)S(1)}, s16[264,1024]{1,0:T(8,128)(2,1)S(1)}, u32[]{:S(2)}, u32[]{:S(2)}) collective-permute-start(s16[264,1024]{1,0:T(8,128)(2,1)S(1)} %get-tuple-element.66), channel_id=1, source_target_pairs={{0,24},{8,0},{16,8},{24,16},{1,25},{9,1},{17,9},{25,17},{2,26},{10... | collective-permute-start | bytes 1622024 | tf_op jit(solution)/shard_map/ppermute | solution.py:328
  61.1 1.7 %shard_map.130.acc = f32[2,4,128,1024]{3,2,1,0:T(8,128)S(1)} custom-call(bf16[4,2,128,1024]{3,2,1,0:T(8,128)(2,1)S(1)} %get-tuple-element.53.own, bf16[4,2,128,1024]{3,2,1,0:T(8,128)(2,1)S(1)} %collective-permute-done.2.came, s16[264,1024]{1,0:T(8,128)(2,1)S(1)} %collective-permute-done.3.refs_0_, s16[264,1024]{1,0:T(8,128)(2,1)S(1)} %collective-permute-done.4.refs_1_, ...), custom_call_target="tpu_custom_call" | custom-call | flops 26214400 | bytes 10485760 | tf_op jit(solution)/shard_map/pallas_call | solution.py:230
  62.8 5.6 %collective-permute-done.17.first = s16[264,1024]{1,0:T(8,128)(2,1)S(1)} collective-permute-done((s16[264,1024]{1,0:T(8,128)(2,1)S(1)}, s16[264,1024]{1,0:T(8,128)(2,1)S(1)}, u32[]{:S(2)}, u32[]{:S(2)}) %collective-permute-start.17) | collective-permute-done | bytes 540704 | tf_op jit(solution)/shard_map/ppermute | solution.py:328
  68.4 1.2 collective-permute-done.18.second
  69.5 1.3 shard_map.133
  70.8 2.5 %collective-permute-start.19 = (s16[136,1024]{1,0:T(8,128)(2,1)S(1)}, s16[136,1024]{1,0:T(8,128)(2,1)S(1)}, u32[]{:S(2)}, u32[]{:S(2)}) collective-permute-start(s16[136,1024]{1,0:T(8,128)(2,1)S(1)} %get-tuple-element.74), channel_id=1, source_target_pairs={{0,16},{8,24},{16,0},{24,8},{1,17},{9,25},{17,1},{25,9},{2,18},{10... | collective-permute-start | bytes 835592 | tf_op jit(solution)/shard_map/ppermute | solution.py:328
  73.3 1.6 %collective-permute-start.20 = (s16[136,1024]{1,0:T(8,128)(2,1)S(1)}, s16[136,1024]{1,0:T(8,128)(2,1)S(1)}, u32[]{:S(2)}, u32[]{:S(2)}) collective-permute-start(s16[136,1024]{1,0:T(8,128)(2,1)S(1)} %get-tuple-element.75), channel_id=1, source_target_pairs={{0,8},{8,16},{16,24},{24,0},{1,9},{9,17},{17,25},{25,1},{2,10},{10... | collective-permute-start | bytes 835592 | tf_op jit(solution)/shard_map/ppermute | solution.py:328
  74.9 1.1 collective-permute-start.21
  76.0 1.3 shard_map.132
  77.4 2.1 %collective-permute-start.14 = (s16[136,1024]{1,0:T(8,128)(2,1)S(1)}, s16[136,1024]{1,0:T(8,128)(2,1)S(1)}, u32[]{:S(2)}, u32[]{:S(2)}) collective-permute-start(s16[136,1024]{1,0:T(8,128)(2,1)S(1)} %get-tuple-element.68), channel_id=1, source_target_pairs={{0,4},{2,6},{4,0},{6,2},{1,5},{3,7},{5,1},{7,3},{8,12},{10,14},{12... | collective-permute-start | bytes 835592 | tf_op jit(solution)/shard_map/ppermute | solution.py:328
  79.5 1.9 %collective-permute-start.15 = (s16[136,1024]{1,0:T(8,128)(2,1)S(1)}, s16[136,1024]{1,0:T(8,128)(2,1)S(1)}, u32[]{:S(2)}, u32[]{:S(2)}) collective-permute-start(s16[136,1024]{1,0:T(8,128)(2,1)S(1)} %get-tuple-element.69), channel_id=1, source_target_pairs={{0,2},{2,4},{4,6},{6,0},{1,3},{3,5},{5,7},{7,1},{8,10},{10,12},{12... | collective-permute-start | bytes 835592 | tf_op jit(solution)/shard_map/ppermute | solution.py:328
  81.4 0.7 collective-permute-start.16
  82.2 5.4 %collective-permute-done.20.refs_6_ = s16[136,1024]{1,0:T(8,128)(2,1)S(1)} collective-permute-done((s16[136,1024]{1,0:T(8,128)(2,1)S(1)}, s16[136,1024]{1,0:T(8,128)(2,1)S(1)}, u32[]{:S(2)}, u32[]{:S(2)}) %collective-permute-start.20) | collective-permute-done | bytes 278560 | tf_op jit(solution)/shard_map/ppermute | solution.py:328
  87.6 4.2 %collective-permute-done.15.refs_2_ = s16[136,1024]{1,0:T(8,128)(2,1)S(1)} collective-permute-done((s16[136,1024]{1,0:T(8,128)(2,1)S(1)}, s16[136,1024]{1,0:T(8,128)(2,1)S(1)}, u32[]{:S(2)}, u32[]{:S(2)}) %collective-permute-start.15) | collective-permute-done | bytes 278560 | tf_op jit(solution)/shard_map/ppermute | solution.py:328
  91.8 1.6 %shard_map.134 = (f32[256,1024]{1,0:T(8,128)S(1)}, f32[128,128]{1,0:T(8,128)}) custom-call(f32[128,1024]{1,0:T(8,128)S(1)} %get-tuple-element.67.refs_0_, s16[136,1024]{1,0:T(8,128)(2,1)S(1)} %collective-permute-done.14.refs_1_, s16[136,1024]{1,0:T(8,128)(2,1)S(1)} %collective-permute-done.15.refs_2_, s16[136,1024]{1,0:T(8,128)(2,1)S(1)} %collective-permute-done.16.refs_3_, ...), custom_call_target="tpu_custom_call" | custom-call | flops 13107200 | bytes 4194304 | tf_op jit(solution)/shard_map/pallas_call | solution.py:312
  93.4 10.3 %all-to-all-start = ((f32[128,1,128]{2,1,0:T(1,128)}), f32[128,1,128]{2,1,0:T(1,128)S(1)}, u32[]{:S(2)}, u32[]{:S(2)}) async-start(f32[128,1,128]{2,1,0:T(1,128)} %bitcast.5), calls=%async_computation | async-start | bytes 131072 | tf_op jit(solution)/shard_map/all_to_all | solution.py:480
  103.8 0.4 shard_map.135
  104.2 1.0 copy-done
  105.1 1.0 copy-done.2
  106.1 6.9 %all-to-all-done = f32[128,1,128]{2,1,0:T(1,128)S(1)} async-done(((f32[128,1,128]{2,1,0:T(1,128)}), f32[128,1,128]{2,1,0:T(1,128)S(1)}, u32[]{:S(2)}, u32[]{:S(2)}) %all-to-all-start) | async-done | bytes 65568 | tf_op jit(solution)/shard_map/all_to_all | solution.py:480
  113.0 1.2 copy-done.1
  114.2 1.2 copy-done.3
  115.5 1.2 shard_map.136
  116.7 4.7 %all-to-all-start.1 = ((f32[32,16,128]{2,1,0:T(8,128)}), f32[32,16,128]{2,1,0:T(8,128)S(1)}, u32[]{:S(2)}, u32[]{:S(2)}) async-start(f32[32,16,128]{2,1,0:T(8,128)} %get-tuple-element.84), calls=%async_computation.1 | async-start | bytes 524288 | tf_op jit(solution)/shard_map/all_to_all | solution.py:480
  121.4 1.3 %row_outputs.1 = (f32[1,256,1024]{2,1,0:T(8,128)}, f32[1,256]{1,0:T(1,128)}, f32[1,256]{1,0:T(1,128)}, f32[256,128]{1,0:T(8,128)S(1)}, f32[256,128]{1,0:T(8,128)S(1)}) custom-call(f32[256,1024]{1,0:T(8,128)S(1)} %get-tuple-element.81.first_new, f32[256,1024]{1,0:T(8,128)S(1)} %get-tuple-element.82.second_new), custom_call_target="tpu_custom_call" | custom-call | flops 10485760 | bytes 3145728 | tf_op jit(solution)/shard_map/row_outputs/pallas_call | solution.py:423
  122.8 7.7 %all-to-all-done.1.peaks = f32[32,16,128]{2,1,0:T(8,128)S(1)} async-done(((f32[32,16,128]{2,1,0:T(8,128)}), f32[32,16,128]{2,1,0:T(8,128)S(1)}, u32[]{:S(2)}, u32[]{:S(2)}) %all-to-all-start.1) | async-done | bytes 262176 | tf_op jit(solution)/shard_map/all_to_all | solution.py:480
  130.5 2.0 %scaled_outputs.1 = (f32[1,256,1024]{2,1,0:T(8,128)}, f32[1,256,1024]{2,1,0:T(8,128)}, f32[1,1024]{1,0:T(1,128)}, f32[1,1024]{1,0:T(1,128)}) custom-call(f32[32,16,128]{2,1,0:T(8,128)S(1)} %all-to-all-done.1.peaks, f32[256,1024]{1,0:T(8,128)S(1)} %get-tuple-element.81.first_new, f32[256,1024]{1,0:T(8,128)S(1)} %get-tuple-element.82.second_new, ...), custom_call_target="tpu_custom_call" | custom-call | flops 2097152 | bytes 4194304 | tf_op jit(solution)/shard_map/scaled_outputs/pallas_call | solution.py:466
  (34 shorter events, 0.2 us)
Async XLA Ops:
  2.9 5.2 %collective-permute-start = (bf16[4,2,128,1024]{3,2,1,0:T(8,128)(2,1)S(1)}, bf16[4,2,128,1024]{3,2,1,0:T(8,128)(2,1)S(1)}, u32[]{:S(2)}, u32[]{:S(2)}) collective-permute-start(bf16[4,2,128,1024]{3,2,1,0:T(8,128)(2,1)S(1)} %shard_map.127), channel_id=1, source_target_pairs={{0,1},{1,0},{2,3},{3,2},{4,5},{5,4},{6,7},{7,6},{8,9},{9,8},{10,11... | collective-permute-start | bytes 6291464 | tf_op jit(solution)/shard_map/ppermute | solution.py:334
  7.1 4.5 %collective-permute-start.1 = (bf16[4,2,128,1024]{3,2,1,0:T(8,128)(2,1)S(1)}, bf16[4,2,128,1024]{3,2,1,0:T(8,128)(2,1)S(1)}, u32[]{:S(2)}, u32[]{:S(2)}) collective-permute-start(bf16[4,2,128,1024]{3,2,1,0:T(8,128)(2,1)S(1)} %get-tuple-element.52), channel_id=1, source_target_pairs={{0,1},{1,0},{2,3},{3,2},{4,5},{5,4},{6,7},{7,6},{8,9},{9,8},{10,11... | collective-permute-start | bytes 6291464 | tf_op jit(solution)/shard_map/ppermute | solution.py:334
  11.2 33.8 %collective-permute-start.7 = (bf16[4,2,128,1024]{3,2,1,0:T(8,128)(2,1)S(1)}, bf16[4,2,128,1024]{3,2,1,0:T(8,128)(2,1)S(1)}, u32[]{:S(2)}, u32[]{:S(2)}) collective-permute-start(bf16[4,2,128,1024]{3,2,1,0:T(8,128)(2,1)S(1)} %get-tuple-element.60), channel_id=1, source_target_pairs={{0,1},{1,0},{2,3},{3,2},{4,5},{5,4},{6,7},{7,6},{8,9},{9,8},{10,11... | collective-permute-start | bytes 6291464 | tf_op jit(solution)/shard_map/ppermute | solution.py:334
  15.2 45.9 %collective-permute-start.2 = (bf16[4,2,128,1024]{3,2,1,0:T(8,128)(2,1)S(1)}, bf16[4,2,128,1024]{3,2,1,0:T(8,128)(2,1)S(1)}, u32[]{:S(2)}, u32[]{:S(2)}) collective-permute-start(bf16[4,2,128,1024]{3,2,1,0:T(8,128)(2,1)S(1)} %get-tuple-element.54), channel_id=1, source_target_pairs={{0,1},{1,0},{2,3},{3,2},{4,5},{5,4},{6,7},{7,6},{8,9},{9,8},{10,11... | collective-permute-start | bytes 6291464 | tf_op jit(solution)/shard_map/ppermute | solution.py:334
  15.4 16.1 %collective-permute-start.10 = (s16[264,1024]{1,0:T(8,128)(2,1)S(1)}, s16[264,1024]{1,0:T(8,128)(2,1)S(1)}, u32[]{:S(2)}, u32[]{:S(2)}) collective-permute-start(s16[264,1024]{1,0:T(8,128)(2,1)S(1)} %get-tuple-element.63), channel_id=1, source_target_pairs={{0,2},{2,4},{4,6},{6,0},{1,3},{3,5},{5,7},{7,1},{8,10},{10,12},{12... | collective-permute-start | bytes 1622024 | tf_op jit(solution)/shard_map/ppermute | solution.py:328
  17.1 17.1 %collective-permute-start.11 = (s16[264,1024]{1,0:T(8,128)(2,1)S(1)}, s16[264,1024]{1,0:T(8,128)(2,1)S(1)}, u32[]{:S(2)}, u32[]{:S(2)}) collective-permute-start(s16[264,1024]{1,0:T(8,128)(2,1)S(1)} %get-tuple-element.64), channel_id=1, source_target_pairs={{0,6},{2,0},{4,2},{6,4},{1,7},{3,1},{5,3},{7,5},{8,14},{10,8},{12,... | collective-permute-start | bytes 1622024 | tf_op jit(solution)/shard_map/ppermute | solution.py:328
  19.3 15.0 %collective-permute-start.8 = (s16[264,1024]{1,0:T(8,128)(2,1)S(1)}, s16[264,1024]{1,0:T(8,128)(2,1)S(1)}, u32[]{:S(2)}, u32[]{:S(2)}) collective-permute-start(s16[264,1024]{1,0:T(8,128)(2,1)S(1)} %get-tuple-element.61), channel_id=1, source_target_pairs={{0,8},{8,16},{16,24},{24,0},{1,9},{9,17},{17,25},{25,1},{2,10},{10... | collective-permute-start | bytes 1622024 | tf_op jit(solution)/shard_map/ppermute | solution.py:328
  31.5 13.4 %collective-permute-start.9 = (s16[264,1024]{1,0:T(8,128)(2,1)S(1)}, s16[264,1024]{1,0:T(8,128)(2,1)S(1)}, u32[]{:S(2)}, u32[]{:S(2)}) collective-permute-start(s16[264,1024]{1,0:T(8,128)(2,1)S(1)} %get-tuple-element.62), channel_id=1, source_target_pairs={{0,24},{8,0},{16,8},{24,16},{1,25},{9,1},{17,9},{25,17},{2,26},{10... | collective-permute-start | bytes 1622024 | tf_op jit(solution)/shard_map/ppermute | solution.py:328
  34.3 16.8 %collective-permute-start.3 = (s16[264,1024]{1,0:T(8,128)(2,1)S(1)}, s16[264,1024]{1,0:T(8,128)(2,1)S(1)}, u32[]{:S(2)}, u32[]{:S(2)}) collective-permute-start(s16[264,1024]{1,0:T(8,128)(2,1)S(1)} %get-tuple-element.55), channel_id=1, source_target_pairs={{0,8},{8,16},{16,24},{24,0},{1,9},{9,17},{17,25},{25,1},{2,10},{10... | collective-permute-start | bytes 1622024 | tf_op jit(solution)/shard_map/ppermute | solution.py:328
  34.3 22.3 %collective-permute-start.4 = (s16[264,1024]{1,0:T(8,128)(2,1)S(1)}, s16[264,1024]{1,0:T(8,128)(2,1)S(1)}, u32[]{:S(2)}, u32[]{:S(2)}) collective-permute-start(s16[264,1024]{1,0:T(8,128)(2,1)S(1)} %get-tuple-element.56), channel_id=1, source_target_pairs={{0,24},{8,0},{16,8},{24,16},{1,25},{9,1},{17,9},{25,17},{2,26},{10... | collective-permute-start | bytes 1622024 | tf_op jit(solution)/shard_map/ppermute | solution.py:328
  44.9 12.5 %collective-permute-start.5 = (s16[264,1024]{1,0:T(8,128)(2,1)S(1)}, s16[264,1024]{1,0:T(8,128)(2,1)S(1)}, u32[]{:S(2)}, u32[]{:S(2)}) collective-permute-start(s16[264,1024]{1,0:T(8,128)(2,1)S(1)} %get-tuple-element.57), channel_id=1, source_target_pairs={{0,2},{2,4},{4,6},{6,0},{1,3},{3,5},{5,7},{7,1},{8,10},{10,12},{12... | collective-permute-start | bytes 1622024 | tf_op jit(solution)/shard_map/ppermute | solution.py:328
  44.9 13.3 %collective-permute-start.6 = (s16[264,1024]{1,0:T(8,128)(2,1)S(1)}, s16[264,1024]{1,0:T(8,128)(2,1)S(1)}, u32[]{:S(2)}, u32[]{:S(2)}) collective-permute-start(s16[264,1024]{1,0:T(8,128)(2,1)S(1)} %get-tuple-element.58), channel_id=1, source_target_pairs={{0,6},{2,0},{4,2},{6,4},{1,7},{3,1},{5,3},{7,5},{8,14},{10,8},{12,... | collective-permute-start | bytes 1622024 | tf_op jit(solution)/shard_map/ppermute | solution.py:328
  51.1 17.3 %collective-permute-start.17 = (s16[264,1024]{1,0:T(8,128)(2,1)S(1)}, s16[264,1024]{1,0:T(8,128)(2,1)S(1)}, u32[]{:S(2)}, u32[]{:S(2)}) collective-permute-start(s16[264,1024]{1,0:T(8,128)(2,1)S(1)} %get-tuple-element.71), channel_id=1, source_target_pairs={{0,2},{2,4},{4,6},{6,0},{1,3},{3,5},{5,7},{7,1},{8,10},{10,12},{12... | collective-permute-start | bytes 1622024 | tf_op jit(solution)/shard_map/ppermute | solution.py:328
  56.5 13.0 %collective-permute-start.18 = (s16[264,1024]{1,0:T(8,128)(2,1)S(1)}, s16[264,1024]{1,0:T(8,128)(2,1)S(1)}, u32[]{:S(2)}, u32[]{:S(2)}) collective-permute-start(s16[264,1024]{1,0:T(8,128)(2,1)S(1)} %get-tuple-element.72), channel_id=1, source_target_pairs={{0,6},{2,0},{4,2},{6,4},{1,7},{3,1},{5,3},{7,5},{8,14},{10,8},{12,... | collective-permute-start | bytes 1622024 | tf_op jit(solution)/shard_map/ppermute | solution.py:328
  57.4 18.5 %collective-permute-start.12 = (s16[264,1024]{1,0:T(8,128)(2,1)S(1)}, s16[264,1024]{1,0:T(8,128)(2,1)S(1)}, u32[]{:S(2)}, u32[]{:S(2)}) collective-permute-start(s16[264,1024]{1,0:T(8,128)(2,1)S(1)} %get-tuple-element.65), channel_id=1, source_target_pairs={{0,8},{8,16},{16,24},{24,0},{1,9},{9,17},{17,25},{25,1},{2,10},{10... | collective-permute-start | bytes 1622024 | tf_op jit(solution)/shard_map/ppermute | solution.py:328
  58.2 17.8 %collective-permute-start.13 = (s16[264,1024]{1,0:T(8,128)(2,1)S(1)}, s16[264,1024]{1,0:T(8,128)(2,1)S(1)}, u32[]{:S(2)}, u32[]{:S(2)}) collective-permute-start(s16[264,1024]{1,0:T(8,128)(2,1)S(1)} %get-tuple-element.66), channel_id=1, source_target_pairs={{0,24},{8,0},{16,8},{24,16},{1,25},{9,1},{17,9},{25,17},{2,26},{10... | collective-permute-start | bytes 1622024 | tf_op jit(solution)/shard_map/ppermute | solution.py:328
  70.8 10.6 %collective-permute-start.19 = (s16[136,1024]{1,0:T(8,128)(2,1)S(1)}, s16[136,1024]{1,0:T(8,128)(2,1)S(1)}, u32[]{:S(2)}, u32[]{:S(2)}) collective-permute-start(s16[136,1024]{1,0:T(8,128)(2,1)S(1)} %get-tuple-element.74), channel_id=1, source_target_pairs={{0,16},{8,24},{16,0},{24,8},{1,17},{9,25},{17,1},{25,9},{2,18},{10... | collective-permute-start | bytes 835592 | tf_op jit(solution)/shard_map/ppermute | solution.py:328
  73.3 14.3 %collective-permute-start.20 = (s16[136,1024]{1,0:T(8,128)(2,1)S(1)}, s16[136,1024]{1,0:T(8,128)(2,1)S(1)}, u32[]{:S(2)}, u32[]{:S(2)}) collective-permute-start(s16[136,1024]{1,0:T(8,128)(2,1)S(1)} %get-tuple-element.75), channel_id=1, source_target_pairs={{0,8},{8,16},{16,24},{24,0},{1,9},{9,17},{17,25},{25,1},{2,10},{10... | collective-permute-start | bytes 835592 | tf_op jit(solution)/shard_map/ppermute | solution.py:328
  74.9 12.7 %collective-permute-start.21 = (s16[136,1024]{1,0:T(8,128)(2,1)S(1)}, s16[136,1024]{1,0:T(8,128)(2,1)S(1)}, u32[]{:S(2)}, u32[]{:S(2)}) collective-permute-start(s16[136,1024]{1,0:T(8,128)(2,1)S(1)} %get-tuple-element.76), channel_id=1, source_target_pairs={{0,24},{8,0},{16,8},{24,16},{1,25},{9,1},{17,9},{25,17},{2,26},{10... | collective-permute-start | bytes 835592 | tf_op jit(solution)/shard_map/ppermute | solution.py:328
  77.3 26.4 %copy-start.4 = (s32[1,256,1024]{2,1,0:T(8,128)S(1)}, s32[1,256,1024]{2,1,0:T(8,128)}, u32[]{:S(2)}) copy-start(s32[1,256,1024]{2,1,0:T(8,128)} %refs_0_.1) | copy-start | bytes 3145732
  77.3 26.4 %copy-start.5 = (s32[1,256,1024]{2,1,0:T(8,128)S(1)}, s32[1,256,1024]{2,1,0:T(8,128)}, u32[]{:S(2)}) copy-start(s32[1,256,1024]{2,1,0:T(8,128)} %refs_3_.1) | copy-start | bytes 3145732
  77.3 26.4 %copy-start.6 = (f32[1,1024]{1,0:T(1,128)S(1)}, f32[1,1024]{1,0:T(1,128)}, u32[]{:S(2)}) copy-start(f32[1,1024]{1,0:T(1,128)} %refs_2_.1) | copy-start | bytes 12292
  77.3 26.4 %copy-start.7 = (f32[1,1024]{1,0:T(1,128)S(1)}, f32[1,1024]{1,0:T(1,128)}, u32[]{:S(2)}) copy-start(f32[1,1024]{1,0:T(1,128)} %refs_5_.1) | copy-start | bytes 12292
  77.3 26.4 %copy-start.8 = (f32[1,256]{1,0:T(1,128)S(1)}, f32[1,256]{1,0:T(1,128)}, u32[]{:S(2)}) copy-start(f32[1,256]{1,0:T(1,128)} %refs_1_.1) | copy-start | bytes 3076
  77.4 26.4 %copy-start.9 = (f32[1,256]{1,0:T(1,128)S(1)}, f32[1,256]{1,0:T(1,128)}, u32[]{:S(2)}) copy-start(f32[1,256]{1,0:T(1,128)} %refs_4_.1) | copy-start | bytes 3076
  77.4 10.2 %collective-permute-start.14 = (s16[136,1024]{1,0:T(8,128)(2,1)S(1)}, s16[136,1024]{1,0:T(8,128)(2,1)S(1)}, u32[]{:S(2)}, u32[]{:S(2)}) collective-permute-start(s16[136,1024]{1,0:T(8,128)(2,1)S(1)} %get-tuple-element.68), channel_id=1, source_target_pairs={{0,4},{2,6},{4,0},{6,2},{1,5},{3,7},{5,1},{7,3},{8,12},{10,14},{12... | collective-permute-start | bytes 835592 | tf_op jit(solution)/shard_map/ppermute | solution.py:328
  79.5 12.3 %collective-permute-start.15 = (s16[136,1024]{1,0:T(8,128)(2,1)S(1)}, s16[136,1024]{1,0:T(8,128)(2,1)S(1)}, u32[]{:S(2)}, u32[]{:S(2)}) collective-permute-start(s16[136,1024]{1,0:T(8,128)(2,1)S(1)} %get-tuple-element.69), channel_id=1, source_target_pairs={{0,2},{2,4},{4,6},{6,0},{1,3},{3,5},{5,7},{7,1},{8,10},{10,12},{12... | collective-permute-start | bytes 835592 | tf_op jit(solution)/shard_map/ppermute | solution.py:328
  81.4 10.4 %collective-permute-start.16 = (s16[136,1024]{1,0:T(8,128)(2,1)S(1)}, s16[136,1024]{1,0:T(8,128)(2,1)S(1)}, u32[]{:S(2)}, u32[]{:S(2)}) collective-permute-start(s16[136,1024]{1,0:T(8,128)(2,1)S(1)} %get-tuple-element.70), channel_id=1, source_target_pairs={{0,6},{2,0},{4,2},{6,4},{1,7},{3,1},{5,3},{7,5},{8,14},{10,8},{12,... | collective-permute-start | bytes 835592 | tf_op jit(solution)/shard_map/ppermute | solution.py:328
  93.4 19.6 %all-to-all-start = ((f32[128,1,128]{2,1,0:T(1,128)}), f32[128,1,128]{2,1,0:T(1,128)S(1)}, u32[]{:S(2)}, u32[]{:S(2)}) async-start(f32[128,1,128]{2,1,0:T(1,128)} %bitcast.5), calls=%async_computation | async-start | bytes 131072 | tf_op jit(solution)/shard_map/all_to_all | solution.py:480
  104.2 1.0 copy-start
  105.1 1.0 copy-start.2
  113.0 1.2 copy-start.1
  114.2 1.2 copy-start.3
  116.7 13.8 %all-to-all-start.1 = ((f32[32,16,128]{2,1,0:T(8,128)}), f32[32,16,128]{2,1,0:T(8,128)S(1)}, u32[]{:S(2)}, u32[]{:S(2)}) async-start(f32[32,16,128]{2,1,0:T(8,128)} %get-tuple-element.84), calls=%async_computation.1 | async-start | bytes 524288 | tf_op jit(solution)/shard_map/all_to_all | solution.py:480

commit v2 on v0

--- a/solution.py
+++ b/solution.py
@@ -115,9 +115,9 @@
 def gather_outs(parts, wanted):
     rows, cols = parts.shape[3:]
     return (
-        tuple(VMEM((4, 2, rows, cols), parts.dtype) for _ in wanted),
-        pltpu.SemaphoreType.DMA((8 * len(wanted),)),
-        32 * len(wanted) * rows * cols,
+        tuple(VMEM((2, 2, rows, cols), parts.dtype) for _ in wanted),
+        pltpu.SemaphoreType.DMA((4 * len(wanted),)),
+        16 * len(wanted) * rows * cols,
     )
 
 
@@ -161,13 +161,13 @@
     copies = []
     if wanted:
         (where, parts), refs = refs[:2], refs[2:]
-        copies = gather_copies(wanted, where, parts, refs[4 : 4 + len(wanted)], refs[-1])
+        copies = gather_copies(wanted, where, parts, refs[2 : 2 + len(wanted)], refs[-1])
     for copy in copies:
         copy.start()
-    outs, total = refs[:4], refs[4 + len(wanted)]
+    outs, total = refs[:2], refs[2 + len(wanted)]
     rows, cols = own.shape[2:]
     peaks = []
-    for q in range(4):
+    for q in range(2):
         by = came_factor(relayed[q].at[2 * rows : 2 * rows + SIDE]) if relayed else None
         for i in range(2):
 
@@ -187,16 +187,16 @@
 
 def pair(own, came, relayed=(), where=None, parts=None, wanted=()):
     rows, cols = own.shape[2:]
-    outs, scratch = (VMEM((2 * rows + SIDE, cols), I16),) * 4, [VMEM((8, rows, cols), F32)]
+    outs, scratch = (VMEM((2 * rows + SIDE, cols), I16),) * 2, [VMEM((4, rows, cols), F32)]
     specs, args = in_vmem(2 + len(relayed)), [own, held(came), *[held(r) for r in relayed]]
     if wanted:
         more, sem, _ = gather_outs(parts, wanted)
         outs, scratch = outs + more, scratch + [sem]
         specs, args = specs + gather_specs(), args + [where, parts]
     got = call(
-        functools.partial(pair_body, len(relayed), wanted), outs, scratch, 400 * rows * cols, 48 * rows * cols, specs
+        functools.partial(pair_body, len(relayed), wanted), outs, scratch, 200 * rows * cols, 24 * rows * cols, specs
     )(*args)
-    return got[:4], got[4:]
+    return got[:2], got[2:]
 
 
 def column_of(row):
@@ -209,17 +209,18 @@
     return jnp.transpose(jnp.broadcast_to(column, (n, 128)))[0:1, :]
 
 
-def keep_body(own, came, *refs):
-    got, (old, total, first_old, second_old) = refs[:4], (refs[4:10], *refs[10:])
-    rows = own.shape[2]
+def keep_body(*refs):
+    owns, cames, got, old = refs[:2], refs[2:4], refs[4:8], refs[8:14]
+    total, first_old, second_old = refs[14:]
+    rows = owns[0].shape[2]
     for half in range(2):
         for i in range(RING):
             ref = got[2 * half + (1 if i < 2 else 0)]
             by = came_factor(ref.at[2 * rows : 2 * rows + SIDE])[i % 2 : i % 2 + 1]
 
-            def step(r, _, ref=ref, by=by, half=half, i=i):
-                q = 2 * half + i // 2
-                value = own[q, i % 2, pl.ds(r, STEP), :].astype(F32) + came[q, i % 2, pl.ds(r, STEP), :].astype(F32)
+            def step(r, _, ref=ref, by=by, half=half, i=i, own=owns[half], came=cames[half]):
+                at = (i // 2, i % 2, pl.ds(r, STEP))
+                value = own[at].astype(F32) + came[at].astype(F32)
                 total[half, i, pl.ds(r, STEP), :] = value + decode(ref[pl.ds(i % 2 * rows + r, STEP), :], by)
 
             chunks(rows, step, None)
@@ -234,11 +235,11 @@
 
 
 def keep(own, came, got, old):
-    rows, cols = own.shape[2:]
+    rows, cols = own[0].shape[2:]
     each = VMEM((2 * rows, cols), F32)
     return call(
-        keep_body, (VMEM((2, RING, rows, cols), F32), each, each), [], 300 * rows * cols, 100 * rows * cols, in_vmem(12)
-    )(own, held(came), *[held(g) for g in got], *old)
+        keep_body, (VMEM((2, RING, rows, cols), F32), each, each), [], 300 * rows * cols, 100 * rows * cols, in_vmem(14)
+    )(*own, *[held(c) for c in came], *[held(g) for g in got], *old)
 
 
 def middle_body(half, acc, first, second, *refs):
@@ -319,38 +320,51 @@
     def hop(value, name, delta):
         return lax.ppermute(value, name, [(i, (i + delta) % RING) for i in range(RING)])
 
-    def four_ways(values):
-        return [hop(v, axis[q // 2], 1 if q % 2 == 0 else 3) for q, v in enumerate(values)]
-
     def swap(value):
         return lax.ppermute(value, "core", [(0, 1), (1, 0)])
 
-    far = tuple((h, 2, low) for h in range(2) for low in (0, 2))
-    near = tuple((h, d, low) for h in range(2) for d, low in ((1, 2), (3, 0)))
-    join = tuple((h, d, low) for h in range(2) for d, low in ((1, 0), (3, 2)))
-    mine = tuple((h, 0, low) for h in range(2) for low in (0, 2))
-    (out_far,) = gather(where, parts, ((far, False),))
-    came_far = swap(out_far)
-    out_near, own_far = gather(where, parts, ((near, False), (far, True)))
-    came_near = swap(out_near)
-    sent, (out_join, own_near) = pair(
-        own_far, came_far, (), where, parts, ((join, False), (near, True))
-    )
-    got_far = four_ways(sent)
-    came_join = swap(out_join)
-    sent, (out_mine, own_join, own_mine) = pair(
-        own_near, came_near, (), where, parts, ((mine, False), (join, True), (mine, True))
-    )
-    got_near = four_ways(sent)
-    came_mine = swap(out_mine)
-    sent, _ = pair(own_join, came_join, got_far)
-    got_join = four_ways(sent)
-    acc, first_old, second_old = keep(own_mine, came_mine, got_near, old)
+    def stage(half, own, came, relayed, wanted):
+        sent, more = pair(own, came, relayed, where, parts, wanted)
+        got = []
+        for value, delta in zip(sent, (1, 3)):
+            got.append(hop(value, axis[half], delta))
+        return got, more
+
+    def jobs(half, *each):
+        return tuple((half, delta, low) for delta, low in each)
+
+    far, near, join, mine = (
+        [jobs(half, *each) for half in range(2)]
+        for each in (((2, 0), (2, 2)), ((1, 2), (3, 0)), ((1, 0), (3, 2)), ((0, 0), (0, 2)))
+    )
+    (out,) = gather(where, parts, ((far[0], False),))
+    came_far_0 = swap(out)
+    out, own_far_0 = gather(where, parts, ((far[1], False), (far[0], True)))
+    came_far_1 = swap(out)
+    far_0, (out, own_far_1) = stage(0, own_far_0, came_far_0, (), ((near[0], False), (far[1], True)))
+    came_near_0 = swap(out)
+    far_1, (out, own_near_0) = stage(1, own_far_1, came_far_1, (), ((near[1], False), (near[0], True)))
+    came_near_1 = swap(out)
+    near_0, (out, own_near_1) = stage(0, own_near_0, came_near_0, (), ((join[0], False), (near[1], True)))
+    came_join_0 = swap(out)
+    near_1, (out, own_join_0) = stage(1, own_near_1, came_near_1, (), ((join[1], False), (join[0], True)))
+    came_join_1 = swap(out)
+    join_0, (out, own_join_1) = stage(0, own_join_0, came_join_0, far_0, ((mine[0], False), (join[1], True)))
+    came_mine_0 = swap(out)
+    join_1, (out, own_mine_0, own_mine_1) = stage(
+        1, own_join_1, came_join_1, far_1, ((mine[1], False), (mine[0], True), (mine[1], True))
+    )
+    came_mine_1 = swap(out)
+    acc, first_old, second_old = keep(
+        (own_mine_0, own_mine_1), (came_mine_0, came_mine_1), (*near_0, *near_1), old
+    )
     halves = []
-    for half in range(2):
-        *out, kept = middle(acc, got_join[2 * half], got_join[2 * half + 1], half)
-        got = {d: hop(out[k], axis[1 - half], d) for k, d in ((2, 2), (0, 1), (1, 3))}
-        halves.append([kept, got[1], got[3], got[2]])
+    for half, joined in enumerate((join_0, join_1)):
+        *out, kept = middle(acc, *joined, half)
+        got = []
+        for k, delta in ((2, 2), (0, 1), (1, 3)):
+            got.append(hop(out[k], axis[1 - half], delta))
+        halves.append([kept] + got)
     return *last(halves, devices), first_old, second_old
 
 

time: 129 us -> 133 us (1.031)
  starting transfers between devices: 34.1 us -> 41.7 us
  blocking collectives: 23 us -> 17 us
  Pallas kernels: 25.3 us -> 27.6 us
    all_to_all x1, blocking collectives: 23 us -> 17 us  [exchange(): return lax.all_to_all(value, axes, split_axis=0, concat_axis=0, tiled=True)]
    ppermute x4 -> x8, starting transfers between devices: 2.22 us -> 6.62 us  [swap(): return lax.ppermute(value, 'core', [(0, 1), (1, 0)])]
    pallas_call x3 -> x6, Pallas kernels: 10.1 us -> 13.4 us  [pair(): call(functools.partial(pair_body, len(relayed), wanted), outs, scratch, 2...]
    ppermute x18, starting transfers between devices: 27.1 us -> 30.3 us  [hop(): lax.ppermute(value, name, [(i, (i + delta) % RING) for i in range(RING)])]
  transfers between devices with their start and end apart: 23 -> 27, of which waited for: 8 -> 10; matrix products, arithmetic and copies ran while one was open for 0% -> 0% of each run, Pallas kernels for 15% -> 16%
where the time goes in v2:
time: 133 us
  waiting for transfers between devices  45.5 us (34%)
  starting transfers between devices  41.7 us (31%)
  Pallas kernels  27.6 us (21%)
  blocking collectives  17 us (13%)
    ppermute x18, waiting for transfers between devices, hop(): lax.ppermute(value, name, [(i, (i + delta) % RING) for i in range(RING)])  37.7 us
    ppermute x18, starting transfers between devices, hop(): lax.ppermute(value, name, [(i, (i + delta) % RING) for i in range(RING)])  30.3 us
    all_to_all x1, blocking collectives, exchange(): return lax.all_to_all(value, axes, split_axis=0, concat_axis=0, tiled=True)  17 us
    pallas_call x6, Pallas kernels, pair(): call(functools.partial(pair_body, len(relayed), wanted), outs, scratch, 2...  13.4 us
    all_to_all x1, waiting for transfers between devices, exchange(): return lax.all_to_all(value, axes, split_axis=0, concat_axis=0, tiled=True)  7.72 us
    ppermute x8, starting transfers between devices, swap(): return lax.ppermute(value, 'core', [(0, 1), (1, 0)])  6.62 us
    all_to_all x1, starting transfers between devices, exchange(): return lax.all_to_all(value, axes, split_axis=0, concat_axis=0, tiled=True)  4.75 us
    pallas_call x2, Pallas kernels, gather(): call(body, outs, [sem], moved // 4, moved, gather_specs())(where, parts)  3.9 us
  transfers between devices with their start and end apart: 27, of which 10 were waited for; matrix products, arithmetic and copies ran while one was open for 0% of the time, Pallas kernels for 16%

profile of v2, /device:TPU:1, one launch (start us, length us, event | category | flops | bytes accessed | tf_op | source)
XLA Modules:
  0.0 132.7 jit_solution(4520395705119943824)
XLA Ops:
  0.7 1.8 %shard_map.127 = bf16[2,2,128,1024]{3,2,1,0:T(8,128)(2,1)S(1)} custom-call(s32[3]{0:T(128)S(1)} %pad_add_fusion.where.refs_2_.refs_4_, bf16[16,2,2,128,1024]{4,3,2,1,0:T(8,128)(2,1)} %bitcast.10), custom_call_target="tpu_custom_call" | custom-call | flops 524288 | bytes 2097152 | tf_op jit(solution)/shard_map/pallas_call | solution.py:127
  2.5 1.5 %collective-permute-start = (bf16[2,2,128,1024]{3,2,1,0:T(8,128)(2,1)S(1)}, bf16[2,2,128,1024]{3,2,1,0:T(8,128)(2,1)S(1)}, u32[]{:S(2)}, u32[]{:S(2)}) collective-permute-start(bf16[2,2,128,1024]{3,2,1,0:T(8,128)(2,1)S(1)} %shard_map.127), channel_id=1, source_target_pairs={{0,1},{1,0},{2,3},{3,2},{4,5},{5,4},{6,7},{7,6},{8,9},{9,8},{10,11... | collective-permute-start | bytes 3145736 | tf_op jit(solution)/shard_map/ppermute | solution.py:324
  4.0 2.1 %shard_map.126 = (bf16[2,2,128,1024]{3,2,1,0:T(8,128)(2,1)S(1)}, bf16[2,2,128,1024]{3,2,1,0:T(8,128)(2,1)S(1)}) custom-call(s32[3]{0:T(128)S(1)} %pad_add_fusion.where.refs_2_.refs_4_, bf16[16,2,2,128,1024]{4,3,2,1,0:T(8,128)(2,1)} %bitcast.11), custom_call_target="tpu_custom_call" | custom-call | flops 1048576 | bytes 4194304 | tf_op jit(solution)/shard_map/pallas_call | solution.py:127
  6.2 2.1 %shard_map.128 = (s16[264,1024]{1,0:T(8,128)(2,1)S(1)}, s16[264,1024]{1,0:T(8,128)(2,1)S(1)}, bf16[2,2,128,1024]{3,2,1,0:T(8,128)(2,1)S(1)}, bf16[2,2,128,1024]{3,2,1,0:T(8,128)(2,1)S(1)}) custom-call(bf16[2,2,128,1024]{3,2,1,0:T(8,128)(2,1)S(1)} %get-tuple-element.59.refs_0_, bf16[2,2,128,1024]{3,2,1,0:T(8,128)(2,1)S(1)} %collective-permute-done.refs_1_, ...), custom_call_target="tpu_custom_call" | custom-call | flops 26214400 | bytes 3145728 | tf_op jit(solution)/shard_map/pallas_call | solution.py:196
  8.4 0.5 collective-permute-start.2
  8.9 2.1 %shard_map.129 = (s16[264,1024]{1,0:T(8,128)(2,1)S(1)}, s16[264,1024]{1,0:T(8,128)(2,1)S(1)}, bf16[2,2,128,1024]{3,2,1,0:T(8,128)(2,1)S(1)}, bf16[2,2,128,1024]{3,2,1,0:T(8,128)(2,1)S(1)}) custom-call(bf16[2,2,128,1024]{3,2,1,0:T(8,128)(2,1)S(1)} %get-tuple-element.60.refs_0_, bf16[2,2,128,1024]{3,2,1,0:T(8,128)(2,1)S(1)} %collective-permute-done.1.refs_1_, ...), custom_call_target="tpu_custom_call" | custom-call | flops 26214400 | bytes 3145728 | tf_op jit(solution)/shard_map/pallas_call | solution.py:196
  11.0 0.1 collective-permute-start.3
  11.2 2.1 %shard_map.130 = (s16[264,1024]{1,0:T(8,128)(2,1)S(1)}, s16[264,1024]{1,0:T(8,128)(2,1)S(1)}, bf16[2,2,128,1024]{3,2,1,0:T(8,128)(2,1)S(1)}, bf16[2,2,128,1024]{3,2,1,0:T(8,128)(2,1)S(1)}) custom-call(bf16[2,2,128,1024]{3,2,1,0:T(8,128)(2,1)S(1)} %get-tuple-element.62.refs_0_, bf16[2,2,128,1024]{3,2,1,0:T(8,128)(2,1)S(1)} %collective-permute-done.2.refs_1_, ...), custom_call_target="tpu_custom_call" | custom-call | flops 26214400 | bytes 3145728 | tf_op jit(solution)/shard_map/pallas_call | solution.py:196
  13.3 0.5 collective-permute-start.4
  13.8 1.4 %collective-permute-start.5 = (s16[264,1024]{1,0:T(8,128)(2,1)S(1)}, s16[264,1024]{1,0:T(8,128)(2,1)S(1)}, u32[]{:S(2)}, u32[]{:S(2)}) collective-permute-start(s16[264,1024]{1,0:T(8,128)(2,1)S(1)} %get-tuple-element.68), channel_id=1, source_target_pairs={{0,8},{8,16},{16,24},{24,0},{1,9},{9,17},{17,25},{25,1},{2,10},{10... | collective-permute-start | bytes 1622024 | tf_op jit(solution)/shard_map/ppermute | solution.py:321
  15.3 2.1 %shard_map.131 = (s16[264,1024]{1,0:T(8,128)(2,1)S(1)}, s16[264,1024]{1,0:T(8,128)(2,1)S(1)}, bf16[2,2,128,1024]{3,2,1,0:T(8,128)(2,1)S(1)}, bf16[2,2,128,1024]{3,2,1,0:T(8,128)(2,1)S(1)}) custom-call(bf16[2,2,128,1024]{3,2,1,0:T(8,128)(2,1)S(1)} %get-tuple-element.64.refs_0_, bf16[2,2,128,1024]{3,2,1,0:T(8,128)(2,1)S(1)} %collective-permute-done.3.refs_1_, ...), custom_call_target="tpu_custom_call" | custom-call | flops 26214400 | bytes 3145728 | tf_op jit(solution)/shard_map/pallas_call | solution.py:196
  17.4 0.4 collective-permute-start.7
  17.8 1.3 collective-permute-start.6
  19.1 1.7 %collective-permute-start.8 = (s16[264,1024]{1,0:T(8,128)(2,1)S(1)}, s16[264,1024]{1,0:T(8,128)(2,1)S(1)}, u32[]{:S(2)}, u32[]{:S(2)}) collective-permute-start(s16[264,1024]{1,0:T(8,128)(2,1)S(1)} %get-tuple-element.72), channel_id=1, source_target_pairs={{0,2},{2,4},{4,6},{6,0},{1,3},{3,5},{5,7},{7,1},{8,10},{10,12},{12... | collective-permute-start | bytes 1622024 | tf_op jit(solution)/shard_map/ppermute | solution.py:321
  20.9 8.3 %collective-permute-done.5.refs_2_ = s16[264,1024]{1,0:T(8,128)(2,1)S(1)} collective-permute-done((s16[264,1024]{1,0:T(8,128)(2,1)S(1)}, s16[264,1024]{1,0:T(8,128)(2,1)S(1)}, u32[]{:S(2)}, u32[]{:S(2)}) %collective-permute-start.5) | collective-permute-done | bytes 540704 | tf_op jit(solution)/shard_map/ppermute | solution.py:321
  29.2 3.6 %collective-permute-start.9 = (s16[264,1024]{1,0:T(8,128)(2,1)S(1)}, s16[264,1024]{1,0:T(8,128)(2,1)S(1)}, u32[]{:S(2)}, u32[]{:S(2)}) collective-permute-start(s16[264,1024]{1,0:T(8,128)(2,1)S(1)} %get-tuple-element.73), channel_id=1, source_target_pairs={{0,6},{2,0},{4,2},{6,4},{1,7},{3,1},{5,3},{7,5},{8,14},{10,8},{12,... | collective-permute-start | bytes 1622024 | tf_op jit(solution)/shard_map/ppermute | solution.py:321
  32.9 2.4 %shard_map.132 = (s16[264,1024]{1,0:T(8,128)(2,1)S(1)}, s16[264,1024]{1,0:T(8,128)(2,1)S(1)}, bf16[2,2,128,1024]{3,2,1,0:T(8,128)(2,1)S(1)}, bf16[2,2,128,1024]{3,2,1,0:T(8,128)(2,1)S(1)}) custom-call(bf16[2,2,128,1024]{3,2,1,0:T(8,128)(2,1)S(1)} %get-tuple-element.66.refs_0_, bf16[2,2,128,1024]{3,2,1,0:T(8,128)(2,1)S(1)} %collective-permute-done.4.refs_1_, ...), custom_call_target="tpu_custom_call" | custom-call | flops 26214400 | bytes 3145728 | tf_op jit(solution)/shard_map/pallas_call | solution.py:196
  35.3 1.5 %collective-permute-start.10 = (bf16[2,2,128,1024]{3,2,1,0:T(8,128)(2,1)S(1)}, bf16[2,2,128,1024]{3,2,1,0:T(8,128)(2,1)S(1)}, u32[]{:S(2)}, u32[]{:S(2)}) collective-permute-start(bf16[2,2,128,1024]{3,2,1,0:T(8,128)(2,1)S(1)} %get-tuple-element.76), channel_id=1, source_target_pairs={{0,1},{1,0},{2,3},{3,2},{4,5},{5,4},{6,7},{7,6},{8,9},{9,8},{10,11... | collective-permute-start | bytes 3145736 | tf_op jit(solution)/shard_map/ppermute | solution.py:324
  36.8 2.7 %collective-permute-start.13 = (s16[264,1024]{1,0:T(8,128)(2,1)S(1)}, s16[264,1024]{1,0:T(8,128)(2,1)S(1)}, u32[]{:S(2)}, u32[]{:S(2)}) collective-permute-start(s16[264,1024]{1,0:T(8,128)(2,1)S(1)} %get-tuple-element.79), channel_id=1, source_target_pairs={{0,24},{8,0},{16,8},{24,16},{1,25},{9,1},{17,9},{25,17},{2,26},{10... | collective-permute-start | bytes 1622024 | tf_op jit(solution)/shard_map/ppermute | solution.py:321
  39.5 4.1 %collective-permute-done.9.refs_3_ = s16[264,1024]{1,0:T(8,128)(2,1)S(1)} collective-permute-done((s16[264,1024]{1,0:T(8,128)(2,1)S(1)}, s16[264,1024]{1,0:T(8,128)(2,1)S(1)}, u32[]{:S(2)}, u32[]{:S(2)}) %collective-permute-start.9) | collective-permute-done | bytes 540704 | tf_op jit(solution)/shard_map/ppermute | solution.py:321
  43.6 0.4 collective-permute-start.14
  44.0 2.5 %shard_map.133 = (s16[264,1024]{1,0:T(8,128)(2,1)S(1)}, s16[264,1024]{1,0:T(8,128)(2,1)S(1)}, bf16[2,2,128,1024]{3,2,1,0:T(8,128)(2,1)S(1)}, bf16[2,2,128,1024]{...) custom-call(bf16[2,2,128,1024]{3,2,1,0:T(8,128)(2,1)S(1)} %get-tuple-element.70.refs_0_, ...), custom_call_target="tpu_custom_call" | custom-call | flops 26214400 | bytes 3145728 | tf_op jit(solution)/shard_map/pallas_call | solution.py:196
  46.5 1.9 %collective-permute-start.11 = (bf16[2,2,128,1024]{3,2,1,0:T(8,128)(2,1)S(1)}, bf16[2,2,128,1024]{3,2,1,0:T(8,128)(2,1)S(1)}, u32[]{:S(2)}, u32[]{:S(2)}) collective-permute-start(bf16[2,2,128,1024]{3,2,1,0:T(8,128)(2,1)S(1)} %get-tuple-element.77), channel_id=1, source_target_pairs={{0,1},{1,0},{2,3},{3,2},{4,5},{5,4},{6,7},{7,6},{8,9},{9,8},{10,11... | collective-permute-start | bytes 3145736 | tf_op jit(solution)/shard_map/ppermute | solution.py:324
  48.4 2.9 %collective-permute-start.15 = (s16[264,1024]{1,0:T(8,128)(2,1)S(1)}, s16[264,1024]{1,0:T(8,128)(2,1)S(1)}, u32[]{:S(2)}, u32[]{:S(2)}) collective-permute-start(s16[264,1024]{1,0:T(8,128)(2,1)S(1)} %get-tuple-element.81), channel_id=1, source_target_pairs={{0,6},{2,0},{4,2},{6,4},{1,7},{3,1},{5,3},{7,5},{8,14},{10,8},{12,... | collective-permute-start | bytes 1622024 | tf_op jit(solution)/shard_map/ppermute | solution.py:321
  51.3 0.7 collective-permute-start.21
  52.0 5.9 %collective-permute-done.14.refs_6_ = s16[264,1024]{1,0:T(8,128)(2,1)S(1)} collective-permute-done((s16[264,1024]{1,0:T(8,128)(2,1)S(1)}, s16[264,1024]{1,0:T(8,128)(2,1)S(1)}, u32[]{:S(2)}, u32[]{:S(2)}) %collective-permute-start.14) | collective-permute-done | bytes 540704 | tf_op jit(solution)/shard_map/ppermute | solution.py:321
  57.9 1.2 collective-permute-start.22
  59.1 3.8 %collective-permute-done.15.refs_7_ = s16[264,1024]{1,0:T(8,128)(2,1)S(1)} collective-permute-done((s16[264,1024]{1,0:T(8,128)(2,1)S(1)}, s16[264,1024]{1,0:T(8,128)(2,1)S(1)}, u32[]{:S(2)}, u32[]{:S(2)}) %collective-permute-start.15) | collective-permute-done | bytes 540704 | tf_op jit(solution)/shard_map/ppermute | solution.py:321
  62.8 2.7 %collective-permute-start.17 = (s16[264,1024]{1,0:T(8,128)(2,1)S(1)}, s16[264,1024]{1,0:T(8,128)(2,1)S(1)}, u32[]{:S(2)}, u32[]{:S(2)}) collective-permute-start(s16[264,1024]{1,0:T(8,128)(2,1)S(1)} %get-tuple-element.84), channel_id=1, source_target_pairs={{0,24},{8,0},{16,8},{24,16},{1,25},{9,1},{17,9},{25,17},{2,26},{10... | collective-permute-start | bytes 1622024 | tf_op jit(solution)/shard_map/ppermute | solution.py:321
  65.6 2.1 %shard_map.134 = (f32[2,4,128,1024]{3,2,1,0:T(8,128)S(1)}, f32[256,1024]{1,0:T(8,128)S(1)}, f32[256,1024]{1,0:T(8,128)S(1)}) custom-call(bf16[2,2,128,1024]{3,2,1,0:T(8,128)(2,1)S(1)} %get-tuple-element.74.refs_0_, bf16[2,2,128,1024]{3,2,1,0:T(8,128)(2,1)S(1)} %get-tuple-element.75.refs_1_, bf16[2,2,128,1024]{3,2,1,0:T(8,128)(2,1)S(1)} %collective-permute-done.10.refs_2_, ...), custom_call_target="tpu_custom_call" | custom-call | flops 39321600 | bytes 13107200 | tf_op jit(solution)/shard_map/pallas_call | solution.py:240
  67.6 1.8 %collective-permute-done.21.first = s16[264,1024]{1,0:T(8,128)(2,1)S(1)} collective-permute-done((s16[264,1024]{1,0:T(8,128)(2,1)S(1)}, s16[264,1024]{1,0:T(8,128)(2,1)S(1)}, u32[]{:S(2)}, u32[]{:S(2)}) %collective-permute-start.21) | collective-permute-done | bytes 540704 | tf_op jit(solution)/shard_map/ppermute | solution.py:321
  69.5 4.0 %collective-permute-done.22.second = s16[264,1024]{1,0:T(8,128)(2,1)S(1)} collective-permute-done((s16[264,1024]{1,0:T(8,128)(2,1)S(1)}, s16[264,1024]{1,0:T(8,128)(2,1)S(1)}, u32[]{:S(2)}, u32[]{:S(2)}) %collective-permute-start.22) | collective-permute-done | bytes 540704 | tf_op jit(solution)/shard_map/ppermute | solution.py:321
  73.5 1.3 shard_map.136
  74.8 1.7 %collective-permute-start.23 = (s16[136,1024]{1,0:T(8,128)(2,1)S(1)}, s16[136,1024]{1,0:T(8,128)(2,1)S(1)}, u32[]{:S(2)}, u32[]{:S(2)}) collective-permute-start(s16[136,1024]{1,0:T(8,128)(2,1)S(1)} %get-tuple-element.92), channel_id=1, source_target_pairs={{0,16},{8,24},{16,0},{24,8},{1,17},{9,25},{17,1},{25,9},{2,18},{10... | collective-permute-start | bytes 835592 | tf_op jit(solution)/shard_map/ppermute | solution.py:321
  76.5 0.4 collective-permute-start.24
  76.9 2.3 %collective-permute-start.25 = (s16[136,1024]{1,0:T(8,128)(2,1)S(1)}, s16[136,1024]{1,0:T(8,128)(2,1)S(1)}, u32[]{:S(2)}, u32[]{:S(2)}) collective-permute-start(s16[136,1024]{1,0:T(8,128)(2,1)S(1)} %get-tuple-element.94), channel_id=1, source_target_pairs={{0,24},{8,0},{16,8},{24,16},{1,25},{9,1},{17,9},{25,17},{2,26},{10... | collective-permute-start | bytes 835592 | tf_op jit(solution)/shard_map/ppermute | solution.py:321
  79.2 1.3 shard_map.135
  80.5 4.6 %collective-permute-start.18 = (s16[136,1024]{1,0:T(8,128)(2,1)S(1)}, s16[136,1024]{1,0:T(8,128)(2,1)S(1)}, u32[]{:S(2)}, u32[]{:S(2)}) collective-permute-start(s16[136,1024]{1,0:T(8,128)(2,1)S(1)} %get-tuple-element.86), channel_id=1, source_target_pairs={{0,4},{2,6},{4,0},{6,2},{1,5},{3,7},{5,1},{7,3},{8,12},{10,14},{12... | collective-permute-start | bytes 835592 | tf_op jit(solution)/shard_map/ppermute | solution.py:321
  85.1 2.7 %collective-permute-start.20 = (s16[136,1024]{1,0:T(8,128)(2,1)S(1)}, s16[136,1024]{1,0:T(8,128)(2,1)S(1)}, u32[]{:S(2)}, u32[]{:S(2)}) collective-permute-start(s16[136,1024]{1,0:T(8,128)(2,1)S(1)} %get-tuple-element.88), channel_id=1, source_target_pairs={{0,6},{2,0},{4,2},{6,4},{1,7},{3,1},{5,3},{7,5},{8,14},{10,8},{12,... | collective-permute-start | bytes 835592 | tf_op jit(solution)/shard_map/ppermute | solution.py:321
  87.8 3.1 %collective-permute-done.24.refs_6_ = s16[136,1024]{1,0:T(8,128)(2,1)S(1)} collective-permute-done((s16[136,1024]{1,0:T(8,128)(2,1)S(1)}, s16[136,1024]{1,0:T(8,128)(2,1)S(1)}, u32[]{:S(2)}, u32[]{:S(2)}) %collective-permute-start.24) | collective-permute-done | bytes 278560 | tf_op jit(solution)/shard_map/ppermute | solution.py:321
  91.0 6.7 %collective-permute-done.19.refs_2_ = s16[136,1024]{1,0:T(8,128)(2,1)S(1)} collective-permute-done((s16[136,1024]{1,0:T(8,128)(2,1)S(1)}, s16[136,1024]{1,0:T(8,128)(2,1)S(1)}, u32[]{:S(2)}, u32[]{:S(2)}) %collective-permute-start.19) | collective-permute-done | bytes 278560 | tf_op jit(solution)/shard_map/ppermute | solution.py:321
  97.6 1.0 shard_map.137
  98.7 17.0 %all_to_all.16 = f32[128,1,128]{2,1,0:T(1,128)S(1)} all-to-all(f32[128,1,128]{2,1,0:T(1,128)S(1)} %bitcast.9), channel_id=1, replica_groups=mesh['section'=4,'y'=4,'z'=4,'core'=2] {'section','y','z','core'}, dimensions={0} | all-to-all | bytes 131072 | tf_op jit(solution)/shard_map/all_to_all | solution.py:485
  115.7 1.2 shard_map.138
  116.9 4.7 %all-to-all-start.1 = ((f32[32,16,128]{2,1,0:T(8,128)}), f32[32,16,128]{2,1,0:T(8,128)S(1)}, u32[]{:S(2)}, u32[]{:S(2)}) async-start(f32[32,16,128]{2,1,0:T(8,128)} %get-tuple-element.102), calls=%async_computation.1 | async-start | bytes 524288 | tf_op jit(solution)/shard_map/all_to_all | solution.py:485
  121.7 1.3 %row_outputs.1 = (f32[1,256,1024]{2,1,0:T(8,128)}, f32[1,256]{1,0:T(1,128)}, f32[1,256]{1,0:T(1,128)}, f32[256,128]{1,0:T(8,128)S(1)}, f32[256,128]{1,0:T(8,128)S(1)}) custom-call(f32[256,1024]{1,0:T(8,128)S(1)} %get-tuple-element.99.first_new, f32[256,1024]{1,0:T(8,128)S(1)} %get-tuple-element.100.second_new), custom_call_target="tpu_custom_call" | custom-call | flops 10485760 | bytes 3145728 | tf_op jit(solution)/shard_map/row_outputs/pallas_call | solution.py:428
  123.0 7.7 %all-to-all-done.1.peaks = f32[32,16,128]{2,1,0:T(8,128)S(1)} async-done(((f32[32,16,128]{2,1,0:T(8,128)}), f32[32,16,128]{2,1,0:T(8,128)S(1)}, u32[]{:S(2)}, u32[]{:S(2)}) %all-to-all-start.1) | async-done | bytes 262176 | tf_op jit(solution)/shard_map/all_to_all | solution.py:485
  130.7 2.0 %scaled_outputs.1 = (f32[1,256,1024]{2,1,0:T(8,128)}, f32[1,256,1024]{2,1,0:T(8,128)}, f32[1,1024]{1,0:T(1,128)}, f32[1,1024]{1,0:T(1,128)}) custom-call(f32[32,16,128]{2,1,0:T(8,128)S(1)} %all-to-all-done.1.peaks, f32[256,1024]{1,0:T(8,128)S(1)} %get-tuple-element.99.first_new, f32[256,1024]{1,0:T(8,128)S(1)} %get-tuple-element.100.second_new, ...), custom_call_target="tpu_custom_call" | custom-call | flops 2097152 | bytes 4194304 | tf_op jit(solution)/shard_map/scaled_outputs/pallas_call | solution.py:471
  (35 shorter events, 0.3 us)
Async XLA Ops:
  2.5 3.7 %collective-permute-start = (bf16[2,2,128,1024]{3,2,1,0:T(8,128)(2,1)S(1)}, bf16[2,2,128,1024]{3,2,1,0:T(8,128)(2,1)S(1)}, u32[]{:S(2)}, u32[]{:S(2)}) collective-permute-start(bf16[2,2,128,1024]{3,2,1,0:T(8,128)(2,1)S(1)} %shard_map.127), channel_id=1, source_target_pairs={{0,1},{1,0},{2,3},{3,2},{4,5},{5,4},{6,7},{7,6},{8,9},{9,8},{10,11... | collective-permute-start | bytes 3145736 | tf_op jit(solution)/shard_map/ppermute | solution.py:324
  6.1 2.8 %collective-permute-start.1 = (bf16[2,2,128,1024]{3,2,1,0:T(8,128)(2,1)S(1)}, bf16[2,2,128,1024]{3,2,1,0:T(8,128)(2,1)S(1)}, u32[]{:S(2)}, u32[]{:S(2)}) collective-permute-start(bf16[2,2,128,1024]{3,2,1,0:T(8,128)(2,1)S(1)} %get-tuple-element.61), channel_id=1, source_target_pairs={{0,1},{1,0},{2,3},{3,2},{4,5},{5,4},{6,7},{7,6},{8,9},{9,8},{10,11... | collective-permute-start | bytes 3145736 | tf_op jit(solution)/shard_map/ppermute | solution.py:324
  8.4 2.8 %collective-permute-start.2 = (bf16[2,2,128,1024]{3,2,1,0:T(8,128)(2,1)S(1)}, bf16[2,2,128,1024]{3,2,1,0:T(8,128)(2,1)S(1)}, u32[]{:S(2)}, u32[]{:S(2)}) collective-permute-start(bf16[2,2,128,1024]{3,2,1,0:T(8,128)(2,1)S(1)} %get-tuple-element.63), channel_id=1, source_target_pairs={{0,1},{1,0},{2,3},{3,2},{4,5},{5,4},{6,7},{7,6},{8,9},{9,8},{10,11... | collective-permute-start | bytes 3145736 | tf_op jit(solution)/shard_map/ppermute | solution.py:324
  11.0 4.2 %collective-permute-start.3 = (bf16[2,2,128,1024]{3,2,1,0:T(8,128)(2,1)S(1)}, bf16[2,2,128,1024]{3,2,1,0:T(8,128)(2,1)S(1)}, u32[]{:S(2)}, u32[]{:S(2)}) collective-permute-start(bf16[2,2,128,1024]{3,2,1,0:T(8,128)(2,1)S(1)} %get-tuple-element.65), channel_id=1, source_target_pairs={{0,1},{1,0},{2,3},{3,2},{4,5},{5,4},{6,7},{7,6},{8,9},{9,8},{10,11... | collective-permute-start | bytes 3145736 | tf_op jit(solution)/shard_map/ppermute | solution.py:324
  13.3 19.5 %collective-permute-start.4 = (bf16[2,2,128,1024]{3,2,1,0:T(8,128)(2,1)S(1)}, bf16[2,2,128,1024]{3,2,1,0:T(8,128)(2,1)S(1)}, u32[]{:S(2)}, u32[]{:S(2)}) collective-permute-start(bf16[2,2,128,1024]{3,2,1,0:T(8,128)(2,1)S(1)} %get-tuple-element.67), channel_id=1, source_target_pairs={{0,1},{1,0},{2,3},{3,2},{4,5},{5,4},{6,7},{7,6},{8,9},{9,8},{10,11... | collective-permute-start | bytes 3145736 | tf_op jit(solution)/shard_map/ppermute | solution.py:324
  13.8 15.3 %collective-permute-start.5 = (s16[264,1024]{1,0:T(8,128)(2,1)S(1)}, s16[264,1024]{1,0:T(8,128)(2,1)S(1)}, u32[]{:S(2)}, u32[]{:S(2)}) collective-permute-start(s16[264,1024]{1,0:T(8,128)(2,1)S(1)} %get-tuple-element.68), channel_id=1, source_target_pairs={{0,8},{8,16},{16,24},{24,0},{1,9},{9,17},{17,25},{25,1},{2,10},{10... | collective-permute-start | bytes 1622024 | tf_op jit(solution)/shard_map/ppermute | solution.py:321
  17.4 26.6 %collective-permute-start.7 = (bf16[2,2,128,1024]{3,2,1,0:T(8,128)(2,1)S(1)}, bf16[2,2,128,1024]{3,2,1,0:T(8,128)(2,1)S(1)}, u32[]{:S(2)}, u32[]{:S(2)}) collective-permute-start(bf16[2,2,128,1024]{3,2,1,0:T(8,128)(2,1)S(1)} %get-tuple-element.71), channel_id=1, source_target_pairs={{0,1},{1,0},{2,3},{3,2},{4,5},{5,4},{6,7},{7,6},{8,9},{9,8},{10,11... | collective-permute-start | bytes 3145736 | tf_op jit(solution)/shard_map/ppermute | solution.py:324
  17.8 15.0 %collective-permute-start.6 = (s16[264,1024]{1,0:T(8,128)(2,1)S(1)}, s16[264,1024]{1,0:T(8,128)(2,1)S(1)}, u32[]{:S(2)}, u32[]{:S(2)}) collective-permute-start(s16[264,1024]{1,0:T(8,128)(2,1)S(1)} %get-tuple-element.69), channel_id=1, source_target_pairs={{0,24},{8,0},{16,8},{24,16},{1,25},{9,1},{17,9},{25,17},{2,26},{10... | collective-permute-start | bytes 1622024 | tf_op jit(solution)/shard_map/ppermute | solution.py:321
  19.1 17.7 %collective-permute-start.8 = (s16[264,1024]{1,0:T(8,128)(2,1)S(1)}, s16[264,1024]{1,0:T(8,128)(2,1)S(1)}, u32[]{:S(2)}, u32[]{:S(2)}) collective-permute-start(s16[264,1024]{1,0:T(8,128)(2,1)S(1)} %get-tuple-element.72), channel_id=1, source_target_pairs={{0,2},{2,4},{4,6},{6,0},{1,3},{3,5},{5,7},{7,1},{8,10},{10,12},{12... | collective-permute-start | bytes 1622024 | tf_op jit(solution)/shard_map/ppermute | solution.py:321
  29.2 14.4 %collective-permute-start.9 = (s16[264,1024]{1,0:T(8,128)(2,1)S(1)}, s16[264,1024]{1,0:T(8,128)(2,1)S(1)}, u32[]{:S(2)}, u32[]{:S(2)}) collective-permute-start(s16[264,1024]{1,0:T(8,128)(2,1)S(1)} %get-tuple-element.73), channel_id=1, source_target_pairs={{0,6},{2,0},{4,2},{6,4},{1,7},{3,1},{5,3},{7,5},{8,14},{10,8},{12,... | collective-permute-start | bytes 1622024 | tf_op jit(solution)/shard_map/ppermute | solution.py:321
  32.8 15.6 %collective-permute-start.12 = (s16[264,1024]{1,0:T(8,128)(2,1)S(1)}, s16[264,1024]{1,0:T(8,128)(2,1)S(1)}, u32[]{:S(2)}, u32[]{:S(2)}) collective-permute-start(s16[264,1024]{1,0:T(8,128)(2,1)S(1)} %get-tuple-element.78), channel_id=1, source_target_pairs={{0,8},{8,16},{16,24},{24,0},{1,9},{9,17},{17,25},{25,1},{2,10},{10... | collective-permute-start | bytes 1622024 | tf_op jit(solution)/shard_map/ppermute | solution.py:321
  32.8 32.7 %copy-start = (s32[1,256,1024]{2,1,0:T(8,128)S(1)}, s32[1,256,1024]{2,1,0:T(8,128)}, u32[]{:S(2)}) copy-start(s32[1,256,1024]{2,1,0:T(8,128)} %refs_8_.1) | copy-start | bytes 3145732
  32.8 32.7 %copy-start.1 = (s32[1,256,1024]{2,1,0:T(8,128)S(1)}, s32[1,256,1024]{2,1,0:T(8,128)}, u32[]{:S(2)}) copy-start(s32[1,256,1024]{2,1,0:T(8,128)} %refs_11_.1) | copy-start | bytes 3145732
  32.8 32.7 %copy-start.2 = (f32[1,1024]{1,0:T(1,128)S(1)}, f32[1,1024]{1,0:T(1,128)}, u32[]{:S(2)}) copy-start(f32[1,1024]{1,0:T(1,128)} %refs_10_.1) | copy-start | bytes 12292
  32.8 32.7 %copy-start.3 = (f32[1,1024]{1,0:T(1,128)S(1)}, f32[1,1024]{1,0:T(1,128)}, u32[]{:S(2)}) copy-start(f32[1,1024]{1,0:T(1,128)} %refs_13_.1) | copy-start | bytes 12292
  32.9 32.7 %copy-start.4 = (f32[1,256]{1,0:T(1,128)S(1)}, f32[1,256]{1,0:T(1,128)}, u32[]{:S(2)}) copy-start(f32[1,256]{1,0:T(1,128)} %refs_9_.1) | copy-start | bytes 3076
  32.9 32.7 %copy-start.5 = (f32[1,256]{1,0:T(1,128)S(1)}, f32[1,256]{1,0:T(1,128)}, u32[]{:S(2)}) copy-start(f32[1,256]{1,0:T(1,128)} %refs_12_.1) | copy-start | bytes 3076
  35.3 27.5 %collective-permute-start.10 = (bf16[2,2,128,1024]{3,2,1,0:T(8,128)(2,1)S(1)}, bf16[2,2,128,1024]{3,2,1,0:T(8,128)(2,1)S(1)}, u32[]{:S(2)}, u32[]{:S(2)}) collective-permute-start(bf16[2,2,128,1024]{3,2,1,0:T(8,128)(2,1)S(1)} %get-tuple-element.76), channel_id=1, source_target_pairs={{0,1},{1,0},{2,3},{3,2},{4,5},{5,4},{6,7},{7,6},{8,9},{9,8},{10,11... | collective-permute-start | bytes 3145736 | tf_op jit(solution)/shard_map/ppermute | solution.py:324
  36.8 14.5 %collective-permute-start.13 = (s16[264,1024]{1,0:T(8,128)(2,1)S(1)}, s16[264,1024]{1,0:T(8,128)(2,1)S(1)}, u32[]{:S(2)}, u32[]{:S(2)}) collective-permute-start(s16[264,1024]{1,0:T(8,128)(2,1)S(1)} %get-tuple-element.79), channel_id=1, source_target_pairs={{0,24},{8,0},{16,8},{24,16},{1,25},{9,1},{17,9},{25,17},{2,26},{10... | collective-permute-start | bytes 1622024 | tf_op jit(solution)/shard_map/ppermute | solution.py:321
  43.6 14.3 %collective-permute-start.14 = (s16[264,1024]{1,0:T(8,128)(2,1)S(1)}, s16[264,1024]{1,0:T(8,128)(2,1)S(1)}, u32[]{:S(2)}, u32[]{:S(2)}) collective-permute-start(s16[264,1024]{1,0:T(8,128)(2,1)S(1)} %get-tuple-element.80), channel_id=1, source_target_pairs={{0,2},{2,4},{4,6},{6,0},{1,3},{3,5},{5,7},{7,1},{8,10},{10,12},{12... | collective-permute-start | bytes 1622024 | tf_op jit(solution)/shard_map/ppermute | solution.py:321
  46.5 19.0 %collective-permute-start.11 = (bf16[2,2,128,1024]{3,2,1,0:T(8,128)(2,1)S(1)}, bf16[2,2,128,1024]{3,2,1,0:T(8,128)(2,1)S(1)}, u32[]{:S(2)}, u32[]{:S(2)}) collective-permute-start(bf16[2,2,128,1024]{3,2,1,0:T(8,128)(2,1)S(1)} %get-tuple-element.77), channel_id=1, source_target_pairs={{0,1},{1,0},{2,3},{3,2},{4,5},{5,4},{6,7},{7,6},{8,9},{9,8},{10,11... | collective-permute-start | bytes 3145736 | tf_op jit(solution)/shard_map/ppermute | solution.py:324
  48.4 14.4 %collective-permute-start.15 = (s16[264,1024]{1,0:T(8,128)(2,1)S(1)}, s16[264,1024]{1,0:T(8,128)(2,1)S(1)}, u32[]{:S(2)}, u32[]{:S(2)}) collective-permute-start(s16[264,1024]{1,0:T(8,128)(2,1)S(1)} %get-tuple-element.81), channel_id=1, source_target_pairs={{0,6},{2,0},{4,2},{6,4},{1,7},{3,1},{5,3},{7,5},{8,14},{10,8},{12,... | collective-permute-start | bytes 1622024 | tf_op jit(solution)/shard_map/ppermute | solution.py:321
  51.3 18.2 %collective-permute-start.21 = (s16[264,1024]{1,0:T(8,128)(2,1)S(1)}, s16[264,1024]{1,0:T(8,128)(2,1)S(1)}, u32[]{:S(2)}, u32[]{:S(2)}) collective-permute-start(s16[264,1024]{1,0:T(8,128)(2,1)S(1)} %get-tuple-element.89), channel_id=1, source_target_pairs={{0,2},{2,4},{4,6},{6,0},{1,3},{3,5},{5,7},{7,1},{8,10},{10,12},{12... | collective-permute-start | bytes 1622024 | tf_op jit(solution)/shard_map/ppermute | solution.py:321
  57.9 15.6 %collective-permute-start.22 = (s16[264,1024]{1,0:T(8,128)(2,1)S(1)}, s16[264,1024]{1,0:T(8,128)(2,1)S(1)}, u32[]{:S(2)}, u32[]{:S(2)}) collective-permute-start(s16[264,1024]{1,0:T(8,128)(2,1)S(1)} %get-tuple-element.90), channel_id=1, source_target_pairs={{0,6},{2,0},{4,2},{6,4},{1,7},{3,1},{5,3},{7,5},{8,14},{10,8},{12,... | collective-permute-start | bytes 1622024 | tf_op jit(solution)/shard_map/ppermute | solution.py:321
  62.8 16.4 %collective-permute-start.16 = (s16[264,1024]{1,0:T(8,128)(2,1)S(1)}, s16[264,1024]{1,0:T(8,128)(2,1)S(1)}, u32[]{:S(2)}, u32[]{:S(2)}) collective-permute-start(s16[264,1024]{1,0:T(8,128)(2,1)S(1)} %get-tuple-element.83), channel_id=1, source_target_pairs={{0,8},{8,16},{16,24},{24,0},{1,9},{9,17},{17,25},{25,1},{2,10},{10... | collective-permute-start | bytes 1622024 | tf_op jit(solution)/shard_map/ppermute | solution.py:321
  62.8 16.3 %collective-permute-start.17 = (s16[264,1024]{1,0:T(8,128)(2,1)S(1)}, s16[264,1024]{1,0:T(8,128)(2,1)S(1)}, u32[]{:S(2)}, u32[]{:S(2)}) collective-permute-start(s16[264,1024]{1,0:T(8,128)(2,1)S(1)} %get-tuple-element.84), channel_id=1, source_target_pairs={{0,24},{8,0},{16,8},{24,16},{1,25},{9,1},{17,9},{25,17},{2,26},{10... | collective-permute-start | bytes 1622024 | tf_op jit(solution)/shard_map/ppermute | solution.py:321
  74.8 10.3 %collective-permute-start.23 = (s16[136,1024]{1,0:T(8,128)(2,1)S(1)}, s16[136,1024]{1,0:T(8,128)(2,1)S(1)}, u32[]{:S(2)}, u32[]{:S(2)}) collective-permute-start(s16[136,1024]{1,0:T(8,128)(2,1)S(1)} %get-tuple-element.92), channel_id=1, source_target_pairs={{0,16},{8,24},{16,0},{24,8},{1,17},{9,25},{17,1},{25,9},{2,18},{10... | collective-permute-start | bytes 835592 | tf_op jit(solution)/shard_map/ppermute | solution.py:321
  76.5 14.4 %collective-permute-start.24 = (s16[136,1024]{1,0:T(8,128)(2,1)S(1)}, s16[136,1024]{1,0:T(8,128)(2,1)S(1)}, u32[]{:S(2)}, u32[]{:S(2)}) collective-permute-start(s16[136,1024]{1,0:T(8,128)(2,1)S(1)} %get-tuple-element.93), channel_id=1, source_target_pairs={{0,8},{8,16},{16,24},{24,0},{1,9},{9,17},{17,25},{25,1},{2,10},{10... | collective-permute-start | bytes 835592 | tf_op jit(solution)/shard_map/ppermute | solution.py:321
  76.9 14.1 %collective-permute-start.25 = (s16[136,1024]{1,0:T(8,128)(2,1)S(1)}, s16[136,1024]{1,0:T(8,128)(2,1)S(1)}, u32[]{:S(2)}, u32[]{:S(2)}) collective-permute-start(s16[136,1024]{1,0:T(8,128)(2,1)S(1)} %get-tuple-element.94), channel_id=1, source_target_pairs={{0,24},{8,0},{16,8},{24,16},{1,25},{9,1},{17,9},{25,17},{2,26},{10... | collective-permute-start | bytes 835592 | tf_op jit(solution)/shard_map/ppermute | solution.py:321
  80.5 10.4 %collective-permute-start.18 = (s16[136,1024]{1,0:T(8,128)(2,1)S(1)}, s16[136,1024]{1,0:T(8,128)(2,1)S(1)}, u32[]{:S(2)}, u32[]{:S(2)}) collective-permute-start(s16[136,1024]{1,0:T(8,128)(2,1)S(1)} %get-tuple-element.86), channel_id=1, source_target_pairs={{0,4},{2,6},{4,0},{6,2},{1,5},{3,7},{5,1},{7,3},{8,12},{10,14},{12... | collective-permute-start | bytes 835592 | tf_op jit(solution)/shard_map/ppermute | solution.py:321
  85.1 12.5 %collective-permute-start.19 = (s16[136,1024]{1,0:T(8,128)(2,1)S(1)}, s16[136,1024]{1,0:T(8,128)(2,1)S(1)}, u32[]{:S(2)}, u32[]{:S(2)}) collective-permute-start(s16[136,1024]{1,0:T(8,128)(2,1)S(1)} %get-tuple-element.87), channel_id=1, source_target_pairs={{0,2},{2,4},{4,6},{6,0},{1,3},{3,5},{5,7},{7,1},{8,10},{10,12},{12... | collective-permute-start | bytes 835592 | tf_op jit(solution)/shard_map/ppermute | solution.py:321
  85.1 12.5 %collective-permute-start.20 = (s16[136,1024]{1,0:T(8,128)(2,1)S(1)}, s16[136,1024]{1,0:T(8,128)(2,1)S(1)}, u32[]{:S(2)}, u32[]{:S(2)}) collective-permute-start(s16[136,1024]{1,0:T(8,128)(2,1)S(1)} %get-tuple-element.88), channel_id=1, source_target_pairs={{0,6},{2,0},{4,2},{6,4},{1,7},{3,1},{5,3},{7,5},{8,14},{10,8},{12,... | collective-permute-start | bytes 835592 | tf_op jit(solution)/shard_map/ppermute | solution.py:321
  116.9 13.8 %all-to-all-start.1 = ((f32[32,16,128]{2,1,0:T(8,128)}), f32[32,16,128]{2,1,0:T(8,128)S(1)}, u32[]{:S(2)}, u32[]{:S(2)}) async-start(f32[32,16,128]{2,1,0:T(8,128)} %get-tuple-element.102), calls=%async_computation.1 | async-start | bytes 524288 | tf_op jit(solution)/shard_map/all_to_all | solution.py:485

commit v3 on v2

--- a/solution.py
+++ b/solution.py
@@ -25,7 +25,7 @@
 LEAST = 1e-18
 SIDE = 8
 STEP = 64
-VMEM_LIMIT = 20 * 1024 * 1024
+VMEM_LIMIT = 8 * 1024 * 1024
 F32, I16 = jnp.float32, jnp.int16
 VMEM = pltpu.VMEM
 
@@ -83,48 +83,39 @@
     return pltpu.with_memory_space_constraint(value, VMEM)
 
 
-def gather_copies(wanted, where, parts, outs, sem):
+def block_at(where, job, i):
+    half, delta, low = job
+    j = lax.rem(where[1 - half] + ORDER[low + i], RING)
+    far = lax.rem(where[half] + delta, RING)
+    return far * RING + j if half == 0 else j * RING + far
+
+
+def gather_body(wanted, where, parts, *refs):
+    outs, sem = refs[:-1], refs[-1]
     copies = []
     for (jobs, mine), out in zip(wanted, outs):
         core = where[2] if mine else 1 - where[2]
-        for q, (half, delta, low) in enumerate(jobs):
+        for q, job in enumerate(jobs):
             for i in range(2):
-                j = lax.rem(where[1 - half] + ORDER[low + i], RING)
-                far = lax.rem(where[half] + delta, RING)
-                at = far * RING + j if half == 0 else j * RING + far
-                copies.append(
-                    pltpu.make_async_copy(
-                        parts.at[at, core, half], out.at[q, i], sem.at[len(copies)]
-                    )
-                )
-    return copies
-
-
-def gather_body(wanted, where, parts, *refs):
-    copies = gather_copies(wanted, where, parts, refs[:-1], refs[-1])
+                source = parts.at[block_at(where, job, i), core, job[0]]
+                copies.append(pltpu.make_async_copy(source, out.at[q, i], sem.at[len(copies)]))
     for copy in copies:
         copy.start()
     for copy in copies:
         copy.wait()
 
 
-def gather_specs():
-    return [pl.BlockSpec(memory_space=pltpu.SMEM), pl.BlockSpec(memory_space=pltpu.HBM)]
-
-
-def gather_outs(parts, wanted):
+def gather(where, parts, wanted):
     rows, cols = parts.shape[3:]
-    return (
-        tuple(VMEM((2, 2, rows, cols), parts.dtype) for _ in wanted),
-        pltpu.SemaphoreType.DMA((4 * len(wanted),)),
-        16 * len(wanted) * rows * cols,
-    )
-
-
-def gather(where, parts, wanted):
-    outs, sem, moved = gather_outs(parts, wanted)
-    body = functools.partial(gather_body, wanted)
-    return call(body, outs, [sem], moved // 4, moved, gather_specs())(where, parts)
+    size = 2 * rows * cols * sum(len(jobs) for jobs, _ in wanted)
+    return call(
+        functools.partial(gather_body, wanted),
+        tuple(VMEM((len(jobs), 2, rows, cols), parts.dtype) for jobs, _ in wanted),
+        [pltpu.SemaphoreType.DMA((2 * sum(len(jobs) for jobs, _ in wanted),))],
+        size,
+        4 * size,
+        [pl.BlockSpec(memory_space=pltpu.SMEM), pl.BlockSpec(memory_space=pltpu.HBM)],
+    )(where, pltpu.with_memory_space_constraint(parts, pltpu.HBM))
 
 
 def chunks(rows, step, carry):
@@ -155,24 +146,26 @@
         )
 
 
-def pair_body(relays, wanted, *refs):
-    own, came = refs[:2]
-    relayed, refs = refs[2 : 2 + relays], refs[2 + relays :]
-    copies = []
-    if wanted:
-        (where, parts), refs = refs[:2], refs[2:]
-        copies = gather_copies(wanted, where, parts, refs[2 : 2 + len(wanted)], refs[-1])
-    for copy in copies:
-        copy.start()
-    outs, total = refs[:2], refs[2 + len(wanted)]
-    rows, cols = own.shape[2:]
+def pair_body(jobs, at_came, first, relays, sends, *refs):
+    (where, parts, came), refs = refs[:3], refs[3:]
+    relayed, refs = refs[:relays], refs[relays:]
+    outs, total = refs[: len(jobs)], refs[-1]
+    rows, cols = came.shape[2:]
+    core = where[2]
+    for out, wanted in zip(refs[len(jobs) : -1], sends):
+        for q, job in enumerate(wanted):
+            for i in range(2):
+                at = block_at(where, job, i)
+                for r in range(0, rows, STEP):
+                    out[q, i, r : r + STEP, :] = parts[at, 1 - core, job[0], r : r + STEP, :]
     peaks = []
-    for q in range(2):
+    for q, job in enumerate(jobs):
         by = came_factor(relayed[q].at[2 * rows : 2 * rows + SIDE]) if relayed else None
         for i in range(2):
-
-            def step(r, peak, q=q, i=i, by=by):
-                value = own[q, i, pl.ds(r, STEP), :].astype(F32) + came[q, i, pl.ds(r, STEP), :].astype(F32)
+            at = (q, i) if first else (block_at(where, job, i), core, job[0])
+
+            def step(r, peak, q=q, i=i, by=by, at=at):
+                value = parts[(*at, pl.ds(r, STEP))].astype(F32) + came[at_came + q, i, pl.ds(r, STEP), :].astype(F32)
                 if relayed:
                     value = value + decode(relayed[q][pl.ds(i * rows + r, STEP), :], by[i : i + 1])
                 total[2 * q + i, pl.ds(r, STEP), :] = value
@@ -181,22 +174,21 @@
             peak = chunks(rows, step, jnp.zeros((8, cols), F32))
             peaks.append(jnp.max(peak, axis=0, keepdims=True))
     send_blocks(total, outs, peaks, rows, 2)
-    for copy in copies:
-        copy.wait()
-
-
-def pair(own, came, relayed=(), where=None, parts=None, wanted=()):
-    rows, cols = own.shape[2:]
-    outs, scratch = (VMEM((2 * rows + SIDE, cols), I16),) * 2, [VMEM((4, rows, cols), F32)]
-    specs, args = in_vmem(2 + len(relayed)), [own, held(came), *[held(r) for r in relayed]]
-    if wanted:
-        more, sem, _ = gather_outs(parts, wanted)
-        outs, scratch = outs + more, scratch + [sem]
-        specs, args = specs + gather_specs(), args + [where, parts]
+
+
+def pair(where, parts, came, jobs, first=False, relayed=(), sends=()):
+    rows, cols = came.shape[2:]
+    at_came = len(jobs) * jobs[0][0] if came.shape[0] > len(jobs) else 0
     got = call(
-        functools.partial(pair_body, len(relayed), wanted), outs, scratch, 200 * rows * cols, 24 * rows * cols, specs
-    )(*args)
-    return got[:2], got[2:]
+        functools.partial(pair_body, jobs, at_came, first, len(relayed), sends),
+        (VMEM((2 * rows + SIDE, cols), I16),) * len(jobs)
+        + tuple(VMEM((len(wanted), 2, rows, cols), came.dtype) for wanted in sends),
+        [VMEM((2 * len(jobs), rows, cols), F32)],
+        100 * len(jobs) * rows * cols,
+        12 * len(jobs) * rows * cols,
+        [pl.BlockSpec(memory_space=pltpu.SMEM), *in_vmem(2 + len(relayed))],
+    )(where, parts, held(came), *[held(r) for r in relayed])
+    return got[: len(jobs)], got[len(jobs) :]
 
 
 def column_of(row):
@@ -209,18 +201,19 @@
     return jnp.transpose(jnp.broadcast_to(column, (n, 128)))[0:1, :]
 
 
-def keep_body(*refs):
-    owns, cames, got, old = refs[:2], refs[2:4], refs[4:8], refs[8:14]
-    total, first_old, second_old = refs[14:]
-    rows = owns[0].shape[2]
+def keep_body(jobs, where, parts, came, *refs):
+    got, old = refs[:4], refs[4:10]
+    total, first_old, second_old = refs[10:]
+    rows = came.shape[2]
     for half in range(2):
         for i in range(RING):
             ref = got[2 * half + (1 if i < 2 else 0)]
             by = came_factor(ref.at[2 * rows : 2 * rows + SIDE])[i % 2 : i % 2 + 1]
-
-            def step(r, _, ref=ref, by=by, half=half, i=i, own=owns[half], came=cames[half]):
-                at = (i // 2, i % 2, pl.ds(r, STEP))
-                value = own[at].astype(F32) + came[at].astype(F32)
+            q = 2 * half + i // 2
+            at = (block_at(where, jobs[q], i % 2), where[2], half)
+
+            def step(r, _, ref=ref, by=by, half=half, i=i, q=q, at=at):
+                value = parts[(*at, pl.ds(r, STEP))].astype(F32) + came[q, i % 2, pl.ds(r, STEP), :].astype(F32)
                 total[half, i, pl.ds(r, STEP), :] = value + decode(ref[pl.ds(i % 2 * rows + r, STEP), :], by)
 
             chunks(rows, step, None)
@@ -234,12 +227,17 @@
             out[r : r + STEP, :] = codes[0, r : r + STEP, :].astype(F32) * (beta / levels) * bound
 
 
-def keep(own, came, got, old):
-    rows, cols = own[0].shape[2:]
+def keep(where, parts, came, jobs, got, old):
+    rows, cols = came.shape[2:]
     each = VMEM((2 * rows, cols), F32)
     return call(
-        keep_body, (VMEM((2, RING, rows, cols), F32), each, each), [], 300 * rows * cols, 100 * rows * cols, in_vmem(14)
-    )(*own, *[held(c) for c in came], *[held(g) for g in got], *old)
+        functools.partial(keep_body, jobs),
+        (VMEM((2, RING, rows, cols), F32), each, each),
+        [],
+        300 * rows * cols,
+        100 * rows * cols,
+        [pl.BlockSpec(memory_space=pltpu.SMEM), *in_vmem(12)],
+    )(where, parts, held(came), *[held(g) for g in got], *old)
 
 
 def middle_body(half, acc, first, second, *refs):
@@ -314,7 +312,7 @@
 
 def reduce_scatter(parts, old, devices):
     where = jnp.stack([lax.axis_index(a) for a in FSDP]).astype(jnp.int32)
-    parts = pltpu.with_memory_space_constraint(parts, pltpu.HBM)
+    resident = held(parts)
     axis = ("y", "z")
 
     def hop(value, name, delta):
@@ -323,40 +321,33 @@
     def swap(value):
         return lax.ppermute(value, "core", [(0, 1), (1, 0)])
 
-    def stage(half, own, came, relayed, wanted):
-        sent, more = pair(own, came, relayed, where, parts, wanted)
+    def stage(half, jobs, came, source=resident, first=False, relayed=(), sends=()):
+        sent, more = pair(where, source, came, jobs, first, relayed, sends)
         got = []
         for value, delta in zip(sent, (1, 3)):
             got.append(hop(value, axis[half], delta))
         return got, more
 
-    def jobs(half, *each):
-        return tuple((half, delta, low) for delta, low in each)
-
-    far, near, join, mine = (
-        [jobs(half, *each) for half in range(2)]
-        for each in (((2, 0), (2, 2)), ((1, 2), (3, 0)), ((1, 0), (3, 2)), ((0, 0), (0, 2)))
-    )
+    def jobs_of(*each):
+        return [tuple((half, delta, low) for delta, low in each) for half in range(2)]
+
+    far, near = jobs_of((2, 0), (2, 2)), jobs_of((1, 2), (3, 0))
+    join, mine = jobs_of((1, 0), (3, 2)), jobs_of((0, 0), (0, 2))
     (out,) = gather(where, parts, ((far[0], False),))
     came_far_0 = swap(out)
     out, own_far_0 = gather(where, parts, ((far[1], False), (far[0], True)))
     came_far_1 = swap(out)
-    far_0, (out, own_far_1) = stage(0, own_far_0, came_far_0, (), ((near[0], False), (far[1], True)))
-    came_near_0 = swap(out)
-    far_1, (out, own_near_0) = stage(1, own_far_1, came_far_1, (), ((near[1], False), (near[0], True)))
-    came_near_1 = swap(out)
-    near_0, (out, own_near_1) = stage(0, own_near_0, came_near_0, (), ((join[0], False), (near[1], True)))
-    came_join_0 = swap(out)
-    near_1, (out, own_join_0) = stage(1, own_near_1, came_near_1, (), ((join[1], False), (join[0], True)))
-    came_join_1 = swap(out)
-    join_0, (out, own_join_1) = stage(0, own_join_0, came_join_0, far_0, ((mine[0], False), (join[1], True)))
-    came_mine_0 = swap(out)
-    join_1, (out, own_mine_0, own_mine_1) = stage(
-        1, own_join_1, came_join_1, far_1, ((mine[1], False), (mine[0], True), (mine[1], True))
-    )
-    came_mine_1 = swap(out)
+    far_0, _ = stage(0, far[0], came_far_0, own_far_0, True)
+    far_1, out = stage(1, far[1], came_far_1, sends=near)
+    came_near = [swap(o) for o in out]
+    near_0, (out,) = stage(0, near[0], came_near[0], sends=(join[0] + join[1],))
+    came_join = swap(out)
+    near_1, (out,) = stage(1, near[1], came_near[1], sends=(mine[0] + mine[1],))
+    came_mine = swap(out)
+    join_0, _ = stage(0, join[0], came_join, relayed=far_0)
+    join_1, _ = stage(1, join[1], came_join, relayed=far_1)
     acc, first_old, second_old = keep(
-        (own_mine_0, own_mine_1), (came_mine_0, came_mine_1), (*near_0, *near_1), old
+        where, resident, came_mine, mine[0] + mine[1], (*near_0, *near_1), old
     )
     halves = []
     for half, joined in enumerate((join_0, join_1)):

time: 133 us -> 132 us (level)
  starting transfers between devices: 41.7 us -> 38.7 us
  blocking collectives: 17 us -> 18.4 us
    ppermute x8 -> x6, waiting for transfers between devices: 0.08 us -> 2.3 us  [swap(): return lax.ppermute(value, 'core', [(0, 1), (1, 0)])]
    ppermute x8 -> x6, starting transfers between devices: 6.62 us -> 5.12 us  [swap(): return lax.ppermute(value, 'core', [(0, 1), (1, 0)])]
    ppermute x18, waiting for transfers between devices: 37.7 us -> 36.3 us  [hop(): lax.ppermute(value, name, [(i, (i + delta) % RING) for i in range(RING)])]
    ppermute x18, starting transfers between devices: 30.3 us -> 28.9 us  [hop(): lax.ppermute(value, name, [(i, (i + delta) % RING) for i in range(RING)])]
    all_to_all x1, blocking collectives: 17 us -> 18.4 us  [exchange(): return lax.all_to_all(value, axes, split_axis=0, concat_axis=0, tiled=True)]
  transfers between devices with their start and end apart: 27 -> 25, of which waited for: 10 -> 8; matrix products, arithmetic and copies ran while one was open for 0% -> 0% of each run, Pallas kernels for 16% -> 14%
where the time goes in v3:
time: 132 us
  waiting for transfers between devices  46.3 us (35%)
  starting transfers between devices  38.7 us (29%)
  Pallas kernels  27.3 us (21%)
  blocking collectives  18.4 us (14%)
    ppermute x18, waiting for transfers between devices, hop(): lax.ppermute(value, name, [(i, (i + delta) % RING) for i in range(RING)])  36.3 us
    ppermute x18, starting transfers between devices, hop(): lax.ppermute(value, name, [(i, (i + delta) % RING) for i in range(RING)])  28.9 us
    all_to_all x1, blocking collectives, exchange(): return lax.all_to_all(value, axes, split_axis=0, concat_axis=0, tiled=True)  18.4 us
    pallas_call x6, Pallas kernels, pair(): call(functools.partial(pair_body, jobs, at_came, first, len(relayed), sen...  11.7 us
    all_to_all x1, waiting for transfers between devices, exchange(): return lax.all_to_all(value, axes, split_axis=0, concat_axis=0, tiled=True)  7.72 us
    ppermute x6, starting transfers between devices, swap(): return lax.ppermute(value, 'core', [(0, 1), (1, 0)])  5.12 us
    all_to_all x1, starting transfers between devices, exchange(): return lax.all_to_all(value, axes, split_axis=0, concat_axis=0, tiled=True)  4.75 us
    pallas_call x2, Pallas kernels, gather(): call(functools.partial(gather_body, wanted), tuple((VMEM((len(jobs), 2, r...  4.73 us
  transfers between devices with their start and end apart: 25, of which 8 were waited for; matrix products, arithmetic and copies ran while one was open for 0% of the time, Pallas kernels for 14%

profile of v3, /device:TPU:1, one launch (start us, length us, event | category | flops | bytes accessed | tf_op | source)
XLA Modules:
  0.0 132.1 jit_solution(6826793316151572747)
XLA Ops:
  0.6 0.1 pad_add_fusion.where.refs_0_
  0.7 2.3 %shard_map.126 = (bf16[2,2,128,1024]{3,2,1,0:T(8,128)(2,1)S(1)}, bf16[2,2,128,1024]{3,2,1,0:T(8,128)(2,1)S(1)}) custom-call(s32[3]{0:T(128)S(1)} %pad_add_fusion.where.refs_0_, bf16[16,2,2,128,1024]{4,3,2,1,0:T(8,128)(2,1)} %bitcast.8), custom_call_target="tpu_custom_call" | custom-call | flops 1048576 | bytes 4194304 | tf_op jit(solution)/shard_map/pallas_call | solution.py:111
  3.1 1.5 %collective-permute-start = (bf16[2,2,128,1024]{3,2,1,0:T(8,128)(2,1)S(1)}, bf16[2,2,128,1024]{3,2,1,0:T(8,128)(2,1)S(1)}, u32[]{:S(2)}, u32[]{:S(2)}) collective-permute-start(bf16[2,2,128,1024]{3,2,1,0:T(8,128)(2,1)S(1)} %get-tuple-element.50), channel_id=1, source_target_pairs={{0,1},{1,0},{2,3},{3,2},{4,5},{5,4},{6,7},{7,6},{8,9},{9,8},{10,11... | collective-permute-start | bytes 3145736 | tf_op jit(solution)/shard_map/ppermute | solution.py:322
  4.5 2.3 %collective-permute-done.refs_2_ = bf16[2,2,128,1024]{3,2,1,0:T(8,128)(2,1)S(1)} collective-permute-done((bf16[2,2,128,1024]{3,2,1,0:T(8,128)(2,1)S(1)}, bf16[2,2,128,1024]{3,2,1,0:T(8,128)(2,1)S(1)}, u32[]{:S(2)}, u32[]{:S(2)}) %collective-permute-start) | collective-permute-done | bytes 1048608 | tf_op jit(solution)/shard_map/ppermute | solution.py:322
  6.8 0.3 copy-done
  7.1 1.8 %shard_map.127 = (s16[264,1024]{1,0:T(8,128)(2,1)S(1)}, s16[264,1024]{1,0:T(8,128)(2,1)S(1)}, bf16[2,2,128,1024]{3,2,1,0:T(8,128)(2,1)S(1)}, bf16[2,2,128,1024]{3,2,1,0:T(8,128)(2,1)S(1)}) custom-call(s32[3]{0:T(128)S(1)} %pad_add_fusion.where.refs_0_, bf16[16,2,2,128,1024]{4,3,2,1,0:T(8,128)(2,1)S(1)} %bitcast.10, ...), custom_call_target="tpu_custom_call" | custom-call | flops 26214400 | bytes 3145728 | tf_op jit(solution)/shard_map/pallas_call | solution.py:182
  9.0 1.5 %collective-permute-start.3 = (bf16[2,2,128,1024]{3,2,1,0:T(8,128)(2,1)S(1)}, bf16[2,2,128,1024]{3,2,1,0:T(8,128)(2,1)S(1)}, u32[]{:S(2)}, u32[]{:S(2)}) collective-permute-start(bf16[2,2,128,1024]{3,2,1,0:T(8,128)(2,1)S(1)} %get-tuple-element.53), channel_id=1, source_target_pairs={{0,1},{1,0},{2,3},{3,2},{4,5},{5,4},{6,7},{7,6},{8,9},{9,8},{10,11... | collective-permute-start | bytes 3145736 | tf_op jit(solution)/shard_map/ppermute | solution.py:322
  10.4 0.1 collective-permute-start.1
  10.5 2.4 %shard_map.131 = bf16[2,2,128,1024]{3,2,1,0:T(8,128)(2,1)S(1)} custom-call(s32[3]{0:T(128)S(1)} %pad_add_fusion.where.refs_0_, bf16[16,2,2,128,1024]{4,3,2,1,0:T(8,128)(2,1)} %bitcast.9), custom_call_target="tpu_custom_call" | custom-call | flops 524288 | bytes 2097152 | tf_op jit(solution)/shard_map/pallas_call | solution.py:111
  12.9 0.6 collective-permute-start.9
  13.6 1.8 %shard_map.129 = (s16[264,1024]{1,0:T(8,128)(2,1)S(1)}, s16[264,1024]{1,0:T(8,128)(2,1)S(1)}, bf16[4,2,128,1024]{3,2,1,0:T(8,128)(2,1)S(1)}) custom-call(s32[3]{0:T(128)S(1)} %pad_add_fusion.where.refs_0_, bf16[16,2,2,128,1024]{4,3,2,1,0:T(8,128)(2,1)S(1)} %bitcast.13, bf16[2,2,128,1024]{3,2,1,0:T(8,128)(2,1)S(1)} %collective-permute-done.3.refs_2_), custom_call_target="tpu_custom_call" | custom-call | flops 26214400 | bytes 3145728 | tf_op jit(solution)/shard_map/pallas_call | solution.py:182
  15.4 1.4 %collective-permute-start.8 = (bf16[4,2,128,1024]{3,2,1,0:T(8,128)(2,1)S(1)}, bf16[4,2,128,1024]{3,2,1,0:T(8,128)(2,1)S(1)}, u32[]{:S(2)}, u32[]{:S(2)}) collective-permute-start(bf16[4,2,128,1024]{3,2,1,0:T(8,128)(2,1)S(1)} %get-tuple-element.59), channel_id=1, source_target_pairs={{0,1},{1,0},{2,3},{3,2},{4,5},{5,4},{6,7},{7,6},{8,9},{9,8},{10,11... | collective-permute-start | bytes 6291464 | tf_op jit(solution)/shard_map/ppermute | solution.py:322
  16.8 1.8 %shard_map.128 = (s16[264,1024]{1,0:T(8,128)(2,1)S(1)}, s16[264,1024]{1,0:T(8,128)(2,1)S(1)}, bf16[4,2,128,1024]{3,2,1,0:T(8,128)(2,1)S(1)}) custom-call(s32[3]{0:T(128)S(1)} %pad_add_fusion.where.refs_0_, bf16[16,2,2,128,1024]{4,3,2,1,0:T(8,128)(2,1)S(1)} %bitcast.14, bf16[2,2,128,1024]{3,2,1,0:T(8,128)(2,1)S(1)} %collective-permute-done.1.refs_2_), custom_call_target="tpu_custom_call" | custom-call | flops 26214400 | bytes 3145728 | tf_op jit(solution)/shard_map/pallas_call | solution.py:182
  18.6 0.1 collective-permute-start.2
  18.7 1.7 %shard_map.132 = (s16[264,1024]{1,0:T(8,128)(2,1)S(1)}, s16[264,1024]{1,0:T(8,128)(2,1)S(1)}) custom-call(s32[3]{0:T(128)S(1)} %pad_add_fusion.where.refs_0_, bf16[2,2,128,1024]{3,2,1,0:T(8,128)(2,1)S(1)} %get-tuple-element.60.refs_1_, bf16[2,2,128,1024]{3,2,1,0:T(8,128)(2,1)S(1)} %collective-permute-done.9.refs_2_), custom_call_target="tpu_custom_call" | custom-call | flops 26214400 | bytes 3145728 | tf_op jit(solution)/shard_map/pallas_call | solution.py:182
  20.4 1.5 %collective-permute-start.10 = (s16[264,1024]{1,0:T(8,128)(2,1)S(1)}, s16[264,1024]{1,0:T(8,128)(2,1)S(1)}, u32[]{:S(2)}, u32[]{:S(2)}) collective-permute-start(s16[264,1024]{1,0:T(8,128)(2,1)S(1)} %get-tuple-element.61), channel_id=1, source_target_pairs={{0,8},{8,16},{16,24},{24,0},{1,9},{9,17},{17,25},{25,1},{2,10},{10... | collective-permute-start | bytes 1622024 | tf_op jit(solution)/shard_map/ppermute | solution.py:319
  21.9 1.5 %collective-permute-start.11 = (s16[264,1024]{1,0:T(8,128)(2,1)S(1)}, s16[264,1024]{1,0:T(8,128)(2,1)S(1)}, u32[]{:S(2)}, u32[]{:S(2)}) collective-permute-start(s16[264,1024]{1,0:T(8,128)(2,1)S(1)} %get-tuple-element.62), channel_id=1, source_target_pairs={{0,24},{8,0},{16,8},{24,16},{1,25},{9,1},{17,9},{25,17},{2,26},{10... | collective-permute-start | bytes 1622024 | tf_op jit(solution)/shard_map/ppermute | solution.py:319
  23.4 1.6 %collective-permute-start.17 = (s16[264,1024]{1,0:T(8,128)(2,1)S(1)}, s16[264,1024]{1,0:T(8,128)(2,1)S(1)}, u32[]{:S(2)}, u32[]{:S(2)}) collective-permute-start(s16[264,1024]{1,0:T(8,128)(2,1)S(1)} %get-tuple-element.69), channel_id=1, source_target_pairs={{0,2},{2,4},{4,6},{6,0},{1,3},{3,5},{5,7},{7,1},{8,10},{10,12},{12... | collective-permute-start | bytes 1622024 | tf_op jit(solution)/shard_map/ppermute | solution.py:319
  25.0 10.3 %collective-permute-done.10.refs_3_ = s16[264,1024]{1,0:T(8,128)(2,1)S(1)} collective-permute-done((s16[264,1024]{1,0:T(8,128)(2,1)S(1)}, s16[264,1024]{1,0:T(8,128)(2,1)S(1)}, u32[]{:S(2)}, u32[]{:S(2)}) %collective-permute-start.10) | collective-permute-done | bytes 540704 | tf_op jit(solution)/shard_map/ppermute | solution.py:319
  35.4 3.6 %collective-permute-start.18 = (s16[264,1024]{1,0:T(8,128)(2,1)S(1)}, s16[264,1024]{1,0:T(8,128)(2,1)S(1)}, u32[]{:S(2)}, u32[]{:S(2)}) collective-permute-start(s16[264,1024]{1,0:T(8,128)(2,1)S(1)} %get-tuple-element.70), channel_id=1, source_target_pairs={{0,6},{2,0},{4,2},{6,4},{1,7},{3,1},{5,3},{7,5},{8,14},{10,8},{12,... | collective-permute-start | bytes 1622024 | tf_op jit(solution)/shard_map/ppermute | solution.py:319
  39.0 2.7 %collective-permute-start.5 = (s16[264,1024]{1,0:T(8,128)(2,1)S(1)}, s16[264,1024]{1,0:T(8,128)(2,1)S(1)}, u32[]{:S(2)}, u32[]{:S(2)}) collective-permute-start(s16[264,1024]{1,0:T(8,128)(2,1)S(1)} %get-tuple-element.55), channel_id=1, source_target_pairs={{0,24},{8,0},{16,8},{24,16},{1,25},{9,1},{17,9},{25,17},{2,26},{10... | collective-permute-start | bytes 1622024 | tf_op jit(solution)/shard_map/ppermute | solution.py:319
  41.7 7.7 %collective-permute-done.18.refs_4_ = s16[264,1024]{1,0:T(8,128)(2,1)S(1)} collective-permute-done((s16[264,1024]{1,0:T(8,128)(2,1)S(1)}, s16[264,1024]{1,0:T(8,128)(2,1)S(1)}, u32[]{:S(2)}, u32[]{:S(2)}) %collective-permute-start.18) | collective-permute-done | bytes 540704 | tf_op jit(solution)/shard_map/ppermute | solution.py:319
  49.4 0.4 collective-permute-start.6
  49.8 3.0 %collective-permute-start.7 = (s16[264,1024]{1,0:T(8,128)(2,1)S(1)}, s16[264,1024]{1,0:T(8,128)(2,1)S(1)}, u32[]{:S(2)}, u32[]{:S(2)}) collective-permute-start(s16[264,1024]{1,0:T(8,128)(2,1)S(1)} %get-tuple-element.57), channel_id=1, source_target_pairs={{0,6},{2,0},{4,2},{6,4},{1,7},{3,1},{5,3},{7,5},{8,14},{10,8},{12,... | collective-permute-start | bytes 1622024 | tf_op jit(solution)/shard_map/ppermute | solution.py:319
  52.8 2.3 %shard_map.135 = (s16[264,1024]{1,0:T(8,128)(2,1)S(1)}, s16[264,1024]{1,0:T(8,128)(2,1)S(1)}) custom-call(s32[3]{0:T(128)S(1)} %pad_add_fusion.where.refs_0_, bf16[16,2,2,128,1024]{4,3,2,1,0:T(8,128)(2,1)S(1)} %bitcast.15, bf16[4,2,128,1024]{3,2,1,0:T(8,128)(2,1)S(1)} %collective-permute-done.8.refs_2_, ...), custom_call_target="tpu_custom_call" | custom-call | flops 26214400 | bytes 3145728 | tf_op jit(solution)/shard_map/pallas_call | solution.py:182
  55.3 2.7 %collective-permute-start.20 = (s16[264,1024]{1,0:T(8,128)(2,1)S(1)}, s16[264,1024]{1,0:T(8,128)(2,1)S(1)}, u32[]{:S(2)}, u32[]{:S(2)}) collective-permute-start(s16[264,1024]{1,0:T(8,128)(2,1)S(1)} %get-tuple-element.72), channel_id=1, source_target_pairs={{0,6},{2,0},{4,2},{6,4},{1,7},{3,1},{5,3},{7,5},{8,14},{10,8},{12,... | collective-permute-start | bytes 1622024 | tf_op jit(solution)/shard_map/ppermute | solution.py:319
  58.0 2.3 %shard_map.133 = (s16[264,1024]{1,0:T(8,128)(2,1)S(1)}, s16[264,1024]{1,0:T(8,128)(2,1)S(1)}) custom-call(s32[3]{0:T(128)S(1)} %pad_add_fusion.where.refs_0_, bf16[16,2,2,128,1024]{4,3,2,1,0:T(8,128)(2,1)S(1)} %bitcast.16, bf16[4,2,128,1024]{3,2,1,0:T(8,128)(2,1)S(1)} %collective-permute-done.8.refs_2_, ...), custom_call_target="tpu_custom_call" | custom-call | flops 26214400 | bytes 3145728 | tf_op jit(solution)/shard_map/pallas_call | solution.py:182
  60.3 3.0 %collective-permute-done.6.refs_2_ = s16[264,1024]{1,0:T(8,128)(2,1)S(1)} collective-permute-done((s16[264,1024]{1,0:T(8,128)(2,1)S(1)}, s16[264,1024]{1,0:T(8,128)(2,1)S(1)}, u32[]{:S(2)}, u32[]{:S(2)}) %collective-permute-start.6) | collective-permute-done | bytes 540704 | tf_op jit(solution)/shard_map/ppermute | solution.py:319
  63.3 2.7 %collective-permute-start.13 = (s16[264,1024]{1,0:T(8,128)(2,1)S(1)}, s16[264,1024]{1,0:T(8,128)(2,1)S(1)}, u32[]{:S(2)}, u32[]{:S(2)}) collective-permute-start(s16[264,1024]{1,0:T(8,128)(2,1)S(1)} %get-tuple-element.64), channel_id=1, source_target_pairs={{0,24},{8,0},{16,8},{24,16},{1,25},{9,1},{17,9},{25,17},{2,26},{10... | collective-permute-start | bytes 1622024 | tf_op jit(solution)/shard_map/ppermute | solution.py:319
  66.0 2.6 %shard_map.130 = (f32[2,4,128,1024]{3,2,1,0:T(8,128)S(1)}, f32[256,1024]{1,0:T(8,128)S(1)}, f32[256,1024]{1,0:T(8,128)S(1)}) custom-call(s32[3]{0:T(128)S(1)} %pad_add_fusion.where.refs_0_, bf16[16,2,2,128,1024]{4,3,2,1,0:T(8,128)(2,1)S(1)} %bitcast.17, bf16[4,2,128,1024]{3,2,1,0:T(8,128)(2,1)S(1)} %collective-permute-done.2.came, ...), custom_call_target="tpu_custom_call" | custom-call | flops 39321600 | bytes 13107200 | tf_op jit(solution)/shard_map/pallas_call | solution.py:233
  68.7 6.2 %collective-permute-done.19.first = s16[264,1024]{1,0:T(8,128)(2,1)S(1)} collective-permute-done((s16[264,1024]{1,0:T(8,128)(2,1)S(1)}, s16[264,1024]{1,0:T(8,128)(2,1)S(1)}, u32[]{:S(2)}, u32[]{:S(2)}) %collective-permute-start.19) | collective-permute-done | bytes 540704 | tf_op jit(solution)/shard_map/ppermute | solution.py:319
  74.9 1.3 %shard_map.136 = (s16[136,1024]{1,0:T(8,128)(2,1)S(1)}, s16[136,1024]{1,0:T(8,128)(2,1)S(1)}, s16[136,1024]{1,0:T(8,128)(2,1)S(1)}, f32[128,1024]{1,0:T(8,128)S(1)}) custom-call(f32[2,4,128,1024]{3,2,1,0:T(8,128)S(1)} %get-tuple-element.58.acc, s16[264,1024]{1,0:T(8,128)(2,1)S(1)} %collective-permute-done.19.first, ...), custom_call_target="tpu_custom_call" | custom-call | flops 26214400 | bytes 4194304 | tf_op jit(solution)/shard_map/pallas_call | solution.py:268
  76.2 1.5 %collective-permute-start.21 = (s16[136,1024]{1,0:T(8,128)(2,1)S(1)}, s16[136,1024]{1,0:T(8,128)(2,1)S(1)}, u32[]{:S(2)}, u32[]{:S(2)}) collective-permute-start(s16[136,1024]{1,0:T(8,128)(2,1)S(1)} %get-tuple-element.74), channel_id=1, source_target_pairs={{0,16},{8,24},{16,0},{24,8},{1,17},{9,25},{17,1},{25,9},{2,18},{10... | collective-permute-start | bytes 835592 | tf_op jit(solution)/shard_map/ppermute | solution.py:319
  77.8 0.4 collective-permute-start.22
  78.2 2.3 %collective-permute-start.23 = (s16[136,1024]{1,0:T(8,128)(2,1)S(1)}, s16[136,1024]{1,0:T(8,128)(2,1)S(1)}, u32[]{:S(2)}, u32[]{:S(2)}) collective-permute-start(s16[136,1024]{1,0:T(8,128)(2,1)S(1)} %get-tuple-element.76), channel_id=1, source_target_pairs={{0,24},{8,0},{16,8},{24,16},{1,25},{9,1},{17,9},{25,17},{2,26},{10... | collective-permute-start | bytes 835592 | tf_op jit(solution)/shard_map/ppermute | solution.py:319
  80.4 1.3 %shard_map.134 = (s16[136,1024]{1,0:T(8,128)(2,1)S(1)}, s16[136,1024]{1,0:T(8,128)(2,1)S(1)}, s16[136,1024]{1,0:T(8,128)(2,1)S(1)}, f32[128,1024]{1,0:T(8,128)S(1)}) custom-call(f32[2,4,128,1024]{3,2,1,0:T(8,128)S(1)} %get-tuple-element.58.acc, s16[264,1024]{1,0:T(8,128)(2,1)S(1)} %collective-permute-done.12.first, ...), custom_call_target="tpu_custom_call" | custom-call | flops 26214400 | bytes 4194304 | tf_op jit(solution)/shard_map/pallas_call | solution.py:268
  81.8 2.2 %collective-permute-start.14 = (s16[136,1024]{1,0:T(8,128)(2,1)S(1)}, s16[136,1024]{1,0:T(8,128)(2,1)S(1)}, u32[]{:S(2)}, u32[]{:S(2)}) collective-permute-start(s16[136,1024]{1,0:T(8,128)(2,1)S(1)} %get-tuple-element.66), channel_id=1, source_target_pairs={{0,4},{2,6},{4,0},{6,2},{1,5},{3,7},{5,1},{7,3},{8,12},{10,14},{12... | collective-permute-start | bytes 835592 | tf_op jit(solution)/shard_map/ppermute | solution.py:319
  83.9 0.9 collective-permute-start.15
  84.8 1.8 %collective-permute-start.16 = (s16[136,1024]{1,0:T(8,128)(2,1)S(1)}, s16[136,1024]{1,0:T(8,128)(2,1)S(1)}, u32[]{:S(2)}, u32[]{:S(2)}) collective-permute-start(s16[136,1024]{1,0:T(8,128)(2,1)S(1)} %get-tuple-element.68), channel_id=1, source_target_pairs={{0,6},{2,0},{4,2},{6,4},{1,7},{3,1},{5,3},{7,5},{8,14},{10,8},{12,... | collective-permute-start | bytes 835592 | tf_op jit(solution)/shard_map/ppermute | solution.py:319
  86.6 4.9 %collective-permute-done.22.refs_6_ = s16[136,1024]{1,0:T(8,128)(2,1)S(1)} collective-permute-done((s16[136,1024]{1,0:T(8,128)(2,1)S(1)}, s16[136,1024]{1,0:T(8,128)(2,1)S(1)}, u32[]{:S(2)}, u32[]{:S(2)}) %collective-permute-start.22) | collective-permute-done | bytes 278560 | tf_op jit(solution)/shard_map/ppermute | solution.py:319
  91.5 4.1 %collective-permute-done.15.refs_2_ = s16[136,1024]{1,0:T(8,128)(2,1)S(1)} collective-permute-done((s16[136,1024]{1,0:T(8,128)(2,1)S(1)}, s16[136,1024]{1,0:T(8,128)(2,1)S(1)}, u32[]{:S(2)}, u32[]{:S(2)}) %collective-permute-start.15) | collective-permute-done | bytes 278560 | tf_op jit(solution)/shard_map/ppermute | solution.py:319
  95.6 1.0 shard_map.137
  96.6 18.4 %all_to_all.16 = f32[128,1,128]{2,1,0:T(1,128)S(1)} all-to-all(f32[128,1,128]{2,1,0:T(1,128)S(1)} %bitcast.19), channel_id=1, replica_groups=mesh['section'=4,'y'=4,'z'=4,'core'=2] {'section','y','z','core'}, dimensions={0} | all-to-all | bytes 131072 | tf_op jit(solution)/shard_map/all_to_all | solution.py:476
  115.0 1.3 shard_map.138
  116.3 4.7 %all-to-all-start.1 = ((f32[32,16,128]{2,1,0:T(8,128)}), f32[32,16,128]{2,1,0:T(8,128)S(1)}, u32[]{:S(2)}, u32[]{:S(2)}) async-start(f32[32,16,128]{2,1,0:T(8,128)} %get-tuple-element.84), calls=%async_computation.1 | async-start | bytes 524288 | tf_op jit(solution)/shard_map/all_to_all | solution.py:476
  121.1 1.3 %row_outputs.1 = (f32[1,256,1024]{2,1,0:T(8,128)}, f32[1,256]{1,0:T(1,128)}, f32[1,256]{1,0:T(1,128)}, f32[256,128]{1,0:T(8,128)S(1)}, f32[256,128]{1,0:T(8,128)S(1)}) custom-call(f32[256,1024]{1,0:T(8,128)S(1)} %get-tuple-element.81.first_new, f32[256,1024]{1,0:T(8,128)S(1)} %get-tuple-element.82.second_new), custom_call_target="tpu_custom_call" | custom-call | flops 10485760 | bytes 3145728 | tf_op jit(solution)/shard_map/row_outputs/pallas_call | solution.py:419
  122.4 7.7 %all-to-all-done.1.peaks = f32[32,16,128]{2,1,0:T(8,128)S(1)} async-done(((f32[32,16,128]{2,1,0:T(8,128)}), f32[32,16,128]{2,1,0:T(8,128)S(1)}, u32[]{:S(2)}, u32[]{:S(2)}) %all-to-all-start.1) | async-done | bytes 262176 | tf_op jit(solution)/shard_map/all_to_all | solution.py:476
  130.1 2.0 %scaled_outputs.1 = (f32[1,256,1024]{2,1,0:T(8,128)}, f32[1,256,1024]{2,1,0:T(8,128)}, f32[1,1024]{1,0:T(1,128)}, f32[1,1024]{1,0:T(1,128)}) custom-call(f32[32,16,128]{2,1,0:T(8,128)S(1)} %all-to-all-done.1.peaks, f32[256,1024]{1,0:T(8,128)S(1)} %get-tuple-element.81.first_new, f32[256,1024]{1,0:T(8,128)S(1)} %get-tuple-element.82.second_new, ...), custom_call_target="tpu_custom_call" | custom-call | flops 2097152 | bytes 4194304 | tf_op jit(solution)/shard_map/scaled_outputs/pallas_call | solution.py:462
  (42 shorter events, 0.2 us)
Async XLA Ops:
  0.7 6.4 %copy-start = (bf16[1,1,8192,1024]{3,2,1,0:T(8,128)(2,1)S(1)}, bf16[1,1,8192,1024]{3,2,1,0:T(8,128)(2,1)}, u32[]{:S(2)}) copy-start(bf16[1,1,8192,1024]{3,2,1,0:T(8,128)(2,1)} %param.7) | copy-start | bytes 50331652
  3.1 3.7 %collective-permute-start = (bf16[2,2,128,1024]{3,2,1,0:T(8,128)(2,1)S(1)}, bf16[2,2,128,1024]{3,2,1,0:T(8,128)(2,1)S(1)}, u32[]{:S(2)}, u32[]{:S(2)}) collective-permute-start(bf16[2,2,128,1024]{3,2,1,0:T(8,128)(2,1)S(1)} %get-tuple-element.50), channel_id=1, source_target_pairs={{0,1},{1,0},{2,3},{3,2},{4,5},{5,4},{6,7},{7,6},{8,9},{9,8},{10,11... | collective-permute-start | bytes 3145736 | tf_op jit(solution)/shard_map/ppermute | solution.py:322
  7.1 6.4 %slice-start = ((s8[16777216]{0:T(1024)(128)(4,1)}), s8[4194304]{0:T(1024)(128)(4,1)S(1)}, s32[]{:S(2)}) async-start(s8[16777216]{0:T(1024)(128)(4,1)} %bitcast.11), calls=%async_computation.2 | async-start | bytes 8388608
  7.1 6.4 %slice-start.1 = ((s8[16777216]{0:T(1024)(128)(4,1)}), s8[4194304]{0:T(1024)(128)(4,1)S(1)}, s32[]{:S(2)}) async-start(s8[16777216]{0:T(1024)(128)(4,1)} %bitcast.11), calls=%async_computation.3 | async-start | bytes 8388608
  8.9 4.6 %slice-start.2 = ((s8[16777216]{0:T(1024)(128)(4,1)}), s8[4194304]{0:T(1024)(128)(4,1)S(1)}, s32[]{:S(2)}) async-start(s8[16777216]{0:T(1024)(128)(4,1)} %bitcast.11), calls=%async_computation.4 | async-start | bytes 8388608
  9.0 4.6 %collective-permute-start.3 = (bf16[2,2,128,1024]{3,2,1,0:T(8,128)(2,1)S(1)}, bf16[2,2,128,1024]{3,2,1,0:T(8,128)(2,1)S(1)}, u32[]{:S(2)}, u32[]{:S(2)}) collective-permute-start(bf16[2,2,128,1024]{3,2,1,0:T(8,128)(2,1)S(1)} %get-tuple-element.53), channel_id=1, source_target_pairs={{0,1},{1,0},{2,3},{3,2},{4,5},{5,4},{6,7},{7,6},{8,9},{9,8},{10,11... | collective-permute-start | bytes 3145736 | tf_op jit(solution)/shard_map/ppermute | solution.py:322
  10.4 3.2 %slice-start.3 = ((s8[16777216]{0:T(1024)(128)(4,1)}), s8[4194304]{0:T(1024)(128)(4,1)S(1)}, s32[]{:S(2)}) async-start(s8[16777216]{0:T(1024)(128)(4,1)} %bitcast.11), calls=%async_computation.5 | async-start | bytes 8388608
  10.4 6.4 %collective-permute-start.1 = (bf16[2,2,128,1024]{3,2,1,0:T(8,128)(2,1)S(1)}, bf16[2,2,128,1024]{3,2,1,0:T(8,128)(2,1)S(1)}, u32[]{:S(2)}, u32[]{:S(2)}) collective-permute-start(bf16[2,2,128,1024]{3,2,1,0:T(8,128)(2,1)S(1)} %get-tuple-element.51), channel_id=1, source_target_pairs={{0,1},{1,0},{2,3},{3,2},{4,5},{5,4},{6,7},{7,6},{8,9},{9,8},{10,11... | collective-permute-start | bytes 3145736 | tf_op jit(solution)/shard_map/ppermute | solution.py:322
  12.9 5.8 %collective-permute-start.9 = (bf16[2,2,128,1024]{3,2,1,0:T(8,128)(2,1)S(1)}, bf16[2,2,128,1024]{3,2,1,0:T(8,128)(2,1)S(1)}, u32[]{:S(2)}, u32[]{:S(2)}) collective-permute-start(bf16[2,2,128,1024]{3,2,1,0:T(8,128)(2,1)S(1)} %shard_map.131), channel_id=1, source_target_pairs={{0,1},{1,0},{2,3},{3,2},{4,5},{5,4},{6,7},{7,6},{8,9},{9,8},{10,11... | collective-permute-start | bytes 3145736 | tf_op jit(solution)/shard_map/ppermute | solution.py:322
  15.4 34.4 %collective-permute-start.8 = (bf16[4,2,128,1024]{3,2,1,0:T(8,128)(2,1)S(1)}, bf16[4,2,128,1024]{3,2,1,0:T(8,128)(2,1)S(1)}, u32[]{:S(2)}, u32[]{:S(2)}) collective-permute-start(bf16[4,2,128,1024]{3,2,1,0:T(8,128)(2,1)S(1)} %get-tuple-element.59), channel_id=1, source_target_pairs={{0,1},{1,0},{2,3},{3,2},{4,5},{5,4},{6,7},{7,6},{8,9},{9,8},{10,11... | collective-permute-start | bytes 6291464 | tf_op jit(solution)/shard_map/ppermute | solution.py:322
  18.6 47.4 %collective-permute-start.2 = (bf16[4,2,128,1024]{3,2,1,0:T(8,128)(2,1)S(1)}, bf16[4,2,128,1024]{3,2,1,0:T(8,128)(2,1)S(1)}, u32[]{:S(2)}, u32[]{:S(2)}) collective-permute-start(bf16[4,2,128,1024]{3,2,1,0:T(8,128)(2,1)S(1)} %get-tuple-element.52), channel_id=1, source_target_pairs={{0,1},{1,0},{2,3},{3,2},{4,5},{5,4},{6,7},{7,6},{8,9},{9,8},{10,11... | collective-permute-start | bytes 6291464 | tf_op jit(solution)/shard_map/ppermute | solution.py:322
  20.4 15.0 %collective-permute-start.10 = (s16[264,1024]{1,0:T(8,128)(2,1)S(1)}, s16[264,1024]{1,0:T(8,128)(2,1)S(1)}, u32[]{:S(2)}, u32[]{:S(2)}) collective-permute-start(s16[264,1024]{1,0:T(8,128)(2,1)S(1)} %get-tuple-element.61), channel_id=1, source_target_pairs={{0,8},{8,16},{16,24},{24,0},{1,9},{9,17},{17,25},{25,1},{2,10},{10... | collective-permute-start | bytes 1622024 | tf_op jit(solution)/shard_map/ppermute | solution.py:319
  21.9 17.1 %collective-permute-start.11 = (s16[264,1024]{1,0:T(8,128)(2,1)S(1)}, s16[264,1024]{1,0:T(8,128)(2,1)S(1)}, u32[]{:S(2)}, u32[]{:S(2)}) collective-permute-start(s16[264,1024]{1,0:T(8,128)(2,1)S(1)} %get-tuple-element.62), channel_id=1, source_target_pairs={{0,24},{8,0},{16,8},{24,16},{1,25},{9,1},{17,9},{25,17},{2,26},{10... | collective-permute-start | bytes 1622024 | tf_op jit(solution)/shard_map/ppermute | solution.py:319
  23.4 15.6 %collective-permute-start.17 = (s16[264,1024]{1,0:T(8,128)(2,1)S(1)}, s16[264,1024]{1,0:T(8,128)(2,1)S(1)}, u32[]{:S(2)}, u32[]{:S(2)}) collective-permute-start(s16[264,1024]{1,0:T(8,128)(2,1)S(1)} %get-tuple-element.69), channel_id=1, source_target_pairs={{0,2},{2,4},{4,6},{6,0},{1,3},{3,5},{5,7},{7,1},{8,10},{10,12},{12... | collective-permute-start | bytes 1622024 | tf_op jit(solution)/shard_map/ppermute | solution.py:319
  35.4 14.0 %collective-permute-start.18 = (s16[264,1024]{1,0:T(8,128)(2,1)S(1)}, s16[264,1024]{1,0:T(8,128)(2,1)S(1)}, u32[]{:S(2)}, u32[]{:S(2)}) collective-permute-start(s16[264,1024]{1,0:T(8,128)(2,1)S(1)} %get-tuple-element.70), channel_id=1, source_target_pairs={{0,6},{2,0},{4,2},{6,4},{1,7},{3,1},{5,3},{7,5},{8,14},{10,8},{12,... | collective-permute-start | bytes 1622024 | tf_op jit(solution)/shard_map/ppermute | solution.py:319
  39.0 16.1 %collective-permute-start.4 = (s16[264,1024]{1,0:T(8,128)(2,1)S(1)}, s16[264,1024]{1,0:T(8,128)(2,1)S(1)}, u32[]{:S(2)}, u32[]{:S(2)}) collective-permute-start(s16[264,1024]{1,0:T(8,128)(2,1)S(1)} %get-tuple-element.54), channel_id=1, source_target_pairs={{0,8},{8,16},{16,24},{24,0},{1,9},{9,17},{17,25},{25,1},{2,10},{10... | collective-permute-start | bytes 1622024 | tf_op jit(solution)/shard_map/ppermute | solution.py:319
  39.0 16.2 %collective-permute-start.5 = (s16[264,1024]{1,0:T(8,128)(2,1)S(1)}, s16[264,1024]{1,0:T(8,128)(2,1)S(1)}, u32[]{:S(2)}, u32[]{:S(2)}) collective-permute-start(s16[264,1024]{1,0:T(8,128)(2,1)S(1)} %get-tuple-element.55), channel_id=1, source_target_pairs={{0,24},{8,0},{16,8},{24,16},{1,25},{9,1},{17,9},{25,17},{2,26},{10... | collective-permute-start | bytes 1622024 | tf_op jit(solution)/shard_map/ppermute | solution.py:319
  49.4 13.9 %collective-permute-start.6 = (s16[264,1024]{1,0:T(8,128)(2,1)S(1)}, s16[264,1024]{1,0:T(8,128)(2,1)S(1)}, u32[]{:S(2)}, u32[]{:S(2)}) collective-permute-start(s16[264,1024]{1,0:T(8,128)(2,1)S(1)} %get-tuple-element.56), channel_id=1, source_target_pairs={{0,2},{2,4},{4,6},{6,0},{1,3},{3,5},{5,7},{7,1},{8,10},{10,12},{12... | collective-permute-start | bytes 1622024 | tf_op jit(solution)/shard_map/ppermute | solution.py:319
  49.8 13.5 %collective-permute-start.7 = (s16[264,1024]{1,0:T(8,128)(2,1)S(1)}, s16[264,1024]{1,0:T(8,128)(2,1)S(1)}, u32[]{:S(2)}, u32[]{:S(2)}) collective-permute-start(s16[264,1024]{1,0:T(8,128)(2,1)S(1)} %get-tuple-element.57), channel_id=1, source_target_pairs={{0,6},{2,0},{4,2},{6,4},{1,7},{3,1},{5,3},{7,5},{8,14},{10,8},{12,... | collective-permute-start | bytes 1622024 | tf_op jit(solution)/shard_map/ppermute | solution.py:319
  55.1 19.8 %collective-permute-start.19 = (s16[264,1024]{1,0:T(8,128)(2,1)S(1)}, s16[264,1024]{1,0:T(8,128)(2,1)S(1)}, u32[]{:S(2)}, u32[]{:S(2)}) collective-permute-start(s16[264,1024]{1,0:T(8,128)(2,1)S(1)} %get-tuple-element.71), channel_id=1, source_target_pairs={{0,2},{2,4},{4,6},{6,0},{1,3},{3,5},{5,7},{7,1},{8,10},{10,12},{12... | collective-permute-start | bytes 1622024 | tf_op jit(solution)/shard_map/ppermute | solution.py:319
  55.2 10.8 %copy-start.1 = (s32[1,256,1024]{2,1,0:T(8,128)S(1)}, s32[1,256,1024]{2,1,0:T(8,128)}, u32[]{:S(2)}) copy-start(s32[1,256,1024]{2,1,0:T(8,128)} %refs_4_.1) | copy-start | bytes 3145732
  55.2 10.8 %copy-start.2 = (s32[1,256,1024]{2,1,0:T(8,128)S(1)}, s32[1,256,1024]{2,1,0:T(8,128)}, u32[]{:S(2)}) copy-start(s32[1,256,1024]{2,1,0:T(8,128)} %refs_7_.1) | copy-start | bytes 3145732
  55.2 10.8 %copy-start.3 = (f32[1,1024]{1,0:T(1,128)S(1)}, f32[1,1024]{1,0:T(1,128)}, u32[]{:S(2)}) copy-start(f32[1,1024]{1,0:T(1,128)} %refs_6_.1) | copy-start | bytes 12292
  55.2 10.8 %copy-start.4 = (f32[1,1024]{1,0:T(1,128)S(1)}, f32[1,1024]{1,0:T(1,128)}, u32[]{:S(2)}) copy-start(f32[1,1024]{1,0:T(1,128)} %refs_9_.1) | copy-start | bytes 12292
  55.2 10.8 %copy-start.5 = (f32[1,256]{1,0:T(1,128)S(1)}, f32[1,256]{1,0:T(1,128)}, u32[]{:S(2)}) copy-start(f32[1,256]{1,0:T(1,128)} %refs_5_.1) | copy-start | bytes 3076
  55.3 10.8 %copy-start.6 = (f32[1,256]{1,0:T(1,128)S(1)}, f32[1,256]{1,0:T(1,128)}, u32[]{:S(2)}) copy-start(f32[1,256]{1,0:T(1,128)} %refs_8_.1) | copy-start | bytes 3076
  55.3 19.6 %collective-permute-start.20 = (s16[264,1024]{1,0:T(8,128)(2,1)S(1)}, s16[264,1024]{1,0:T(8,128)(2,1)S(1)}, u32[]{:S(2)}, u32[]{:S(2)}) collective-permute-start(s16[264,1024]{1,0:T(8,128)(2,1)S(1)} %get-tuple-element.72), channel_id=1, source_target_pairs={{0,6},{2,0},{4,2},{6,4},{1,7},{3,1},{5,3},{7,5},{8,14},{10,8},{12,... | collective-permute-start | bytes 1622024 | tf_op jit(solution)/shard_map/ppermute | solution.py:319
  63.3 17.1 %collective-permute-start.12 = (s16[264,1024]{1,0:T(8,128)(2,1)S(1)}, s16[264,1024]{1,0:T(8,128)(2,1)S(1)}, u32[]{:S(2)}, u32[]{:S(2)}) collective-permute-start(s16[264,1024]{1,0:T(8,128)(2,1)S(1)} %get-tuple-element.63), channel_id=1, source_target_pairs={{0,8},{8,16},{16,24},{24,0},{1,9},{9,17},{17,25},{25,1},{2,10},{10... | collective-permute-start | bytes 1622024 | tf_op jit(solution)/shard_map/ppermute | solution.py:319
  63.3 17.1 %collective-permute-start.13 = (s16[264,1024]{1,0:T(8,128)(2,1)S(1)}, s16[264,1024]{1,0:T(8,128)(2,1)S(1)}, u32[]{:S(2)}, u32[]{:S(2)}) collective-permute-start(s16[264,1024]{1,0:T(8,128)(2,1)S(1)} %get-tuple-element.64), channel_id=1, source_target_pairs={{0,24},{8,0},{16,8},{24,16},{1,25},{9,1},{17,9},{25,17},{2,26},{10... | collective-permute-start | bytes 1622024 | tf_op jit(solution)/shard_map/ppermute | solution.py:319
  76.2 8.6 %collective-permute-start.21 = (s16[136,1024]{1,0:T(8,128)(2,1)S(1)}, s16[136,1024]{1,0:T(8,128)(2,1)S(1)}, u32[]{:S(2)}, u32[]{:S(2)}) collective-permute-start(s16[136,1024]{1,0:T(8,128)(2,1)S(1)} %get-tuple-element.74), channel_id=1, source_target_pairs={{0,16},{8,24},{16,0},{24,8},{1,17},{9,25},{17,1},{25,9},{2,18},{10... | collective-permute-start | bytes 835592 | tf_op jit(solution)/shard_map/ppermute | solution.py:319
  77.8 13.7 %collective-permute-start.22 = (s16[136,1024]{1,0:T(8,128)(2,1)S(1)}, s16[136,1024]{1,0:T(8,128)(2,1)S(1)}, u32[]{:S(2)}, u32[]{:S(2)}) collective-permute-start(s16[136,1024]{1,0:T(8,128)(2,1)S(1)} %get-tuple-element.75), channel_id=1, source_target_pairs={{0,8},{8,16},{16,24},{24,0},{1,9},{9,17},{17,25},{25,1},{2,10},{10... | collective-permute-start | bytes 835592 | tf_op jit(solution)/shard_map/ppermute | solution.py:319
  78.2 13.4 %collective-permute-start.23 = (s16[136,1024]{1,0:T(8,128)(2,1)S(1)}, s16[136,1024]{1,0:T(8,128)(2,1)S(1)}, u32[]{:S(2)}, u32[]{:S(2)}) collective-permute-start(s16[136,1024]{1,0:T(8,128)(2,1)S(1)} %get-tuple-element.76), channel_id=1, source_target_pairs={{0,24},{8,0},{16,8},{24,16},{1,25},{9,1},{17,9},{25,17},{2,26},{10... | collective-permute-start | bytes 835592 | tf_op jit(solution)/shard_map/ppermute | solution.py:319
  81.8 9.7 %collective-permute-start.14 = (s16[136,1024]{1,0:T(8,128)(2,1)S(1)}, s16[136,1024]{1,0:T(8,128)(2,1)S(1)}, u32[]{:S(2)}, u32[]{:S(2)}) collective-permute-start(s16[136,1024]{1,0:T(8,128)(2,1)S(1)} %get-tuple-element.66), channel_id=1, source_target_pairs={{0,4},{2,6},{4,0},{6,2},{1,5},{3,7},{5,1},{7,3},{8,12},{10,14},{12... | collective-permute-start | bytes 835592 | tf_op jit(solution)/shard_map/ppermute | solution.py:319
  83.9 11.7 %collective-permute-start.15 = (s16[136,1024]{1,0:T(8,128)(2,1)S(1)}, s16[136,1024]{1,0:T(8,128)(2,1)S(1)}, u32[]{:S(2)}, u32[]{:S(2)}) collective-permute-start(s16[136,1024]{1,0:T(8,128)(2,1)S(1)} %get-tuple-element.67), channel_id=1, source_target_pairs={{0,2},{2,4},{4,6},{6,0},{1,3},{3,5},{5,7},{7,1},{8,10},{10,12},{12... | collective-permute-start | bytes 835592 | tf_op jit(solution)/shard_map/ppermute | solution.py:319
  84.8 10.8 %collective-permute-start.16 = (s16[136,1024]{1,0:T(8,128)(2,1)S(1)}, s16[136,1024]{1,0:T(8,128)(2,1)S(1)}, u32[]{:S(2)}, u32[]{:S(2)}) collective-permute-start(s16[136,1024]{1,0:T(8,128)(2,1)S(1)} %get-tuple-element.68), channel_id=1, source_target_pairs={{0,6},{2,0},{4,2},{6,4},{1,7},{3,1},{5,3},{7,5},{8,14},{10,8},{12,... | collective-permute-start | bytes 835592 | tf_op jit(solution)/shard_map/ppermute | solution.py:319
  116.3 13.8 %all-to-all-start.1 = ((f32[32,16,128]{2,1,0:T(8,128)}), f32[32,16,128]{2,1,0:T(8,128)S(1)}, u32[]{:S(2)}, u32[]{:S(2)}) async-start(f32[32,16,128]{2,1,0:T(8,128)} %get-tuple-element.84), calls=%async_computation.1 | async-start | bytes 524288 | tf_op jit(solution)/shard_map/all_to_all | solution.py:476

commit v4 on v3

--- a/solution.py
+++ b/solution.py
@@ -146,49 +146,50 @@
         )
 
 
-def pair_body(jobs, at_came, first, relays, sends, *refs):
+def pair_body(messages, first, relays, sends, *refs):
     (where, parts, came), refs = refs[:3], refs[3:]
     relayed, refs = refs[:relays], refs[relays:]
-    outs, total = refs[: len(jobs)], refs[-1]
+    outs, total = refs[: len(messages)], refs[-1]
     rows, cols = came.shape[2:]
     core = where[2]
-    for out, wanted in zip(refs[len(jobs) : -1], sends):
+    for out, wanted in zip(refs[len(messages) : -1], sends):
         for q, job in enumerate(wanted):
             for i in range(2):
                 at = block_at(where, job, i)
                 for r in range(0, rows, STEP):
                     out[q, i, r : r + STEP, :] = parts[at, 1 - core, job[0], r : r + STEP, :]
-    peaks = []
-    for q, job in enumerate(jobs):
-        by = came_factor(relayed[q].at[2 * rows : 2 * rows + SIDE]) if relayed else None
-        for i in range(2):
+    peaks, line = [], 0
+    for m, blocks in enumerate(messages):
+        by = came_factor(relayed[m].at[2 * rows : 2 * rows + SIDE]) if relayed else None
+        for job, q, i in blocks:
             at = (q, i) if first else (block_at(where, job, i), core, job[0])
 
-            def step(r, peak, q=q, i=i, by=by, at=at):
-                value = parts[(*at, pl.ds(r, STEP))].astype(F32) + came[at_came + q, i, pl.ds(r, STEP), :].astype(F32)
+            def step(r, peak, m=m, q=q, i=i, by=by, at=at, line=line):
+                value = parts[(*at, pl.ds(r, STEP))].astype(F32) + came[q, i, pl.ds(r, STEP), :].astype(F32)
                 if relayed:
-                    value = value + decode(relayed[q][pl.ds(i * rows + r, STEP), :], by[i : i + 1])
-                total[2 * q + i, pl.ds(r, STEP), :] = value
+                    value = value + decode(relayed[m][pl.ds(i * rows + r, STEP), :], by[i : i + 1])
+                total[line, pl.ds(r, STEP), :] = value
                 return jnp.maximum(peak, fold(jnp.abs(value), jnp.maximum))
 
             peak = chunks(rows, step, jnp.zeros((8, cols), F32))
             peaks.append(jnp.max(peak, axis=0, keepdims=True))
-    send_blocks(total, outs, peaks, rows, 2)
-
-
-def pair(where, parts, came, jobs, first=False, relayed=(), sends=()):
+            line += 1
+    send_blocks(total, outs, peaks, rows, len(messages[0]))
+
+
+def pair(where, parts, came, messages, first=False, relayed=(), sends=()):
     rows, cols = came.shape[2:]
-    at_came = len(jobs) * jobs[0][0] if came.shape[0] > len(jobs) else 0
+    each, n = len(messages[0]), len(messages)
     got = call(
-        functools.partial(pair_body, jobs, at_came, first, len(relayed), sends),
-        (VMEM((2 * rows + SIDE, cols), I16),) * len(jobs)
+        functools.partial(pair_body, messages, first, len(relayed), sends),
+        (VMEM((each * rows + SIDE, cols), I16),) * n
         + tuple(VMEM((len(wanted), 2, rows, cols), came.dtype) for wanted in sends),
-        [VMEM((2 * len(jobs), rows, cols), F32)],
-        100 * len(jobs) * rows * cols,
-        12 * len(jobs) * rows * cols,
+        [VMEM((each * n, rows, cols), F32)],
+        50 * each * n * rows * cols,
+        6 * each * n * rows * cols,
         [pl.BlockSpec(memory_space=pltpu.SMEM), *in_vmem(2 + len(relayed))],
     )(where, parts, held(came), *[held(r) for r in relayed])
-    return got[: len(jobs)], got[len(jobs) :]
+    return got[:n], got[n:]
 
 
 def column_of(row):
@@ -202,8 +203,7 @@
 
 
 def keep_body(jobs, where, parts, came, *refs):
-    got, old = refs[:4], refs[4:10]
-    total, first_old, second_old = refs[10:]
+    got, total = refs[:4], refs[4]
     rows = came.shape[2]
     for half in range(2):
         for i in range(RING):
@@ -217,9 +217,24 @@
                 total[half, i, pl.ds(r, STEP), :] = value + decode(ref[pl.ds(i % 2 * rows + r, STEP), :], by)
 
             chunks(rows, step, None)
-    for (codes, row, column), levels, beta, out in (
-        (old[:3], 7.0, beta_first, first_old),
-        (old[3:], 15.0, beta_second, second_old),
+
+
+def keep(where, parts, came, jobs, got):
+    rows, cols = came.shape[2:]
+    return call(
+        functools.partial(keep_body, jobs),
+        (VMEM((2, RING, rows, cols), F32),),
+        [],
+        200 * rows * cols,
+        80 * rows * cols,
+        [pl.BlockSpec(memory_space=pltpu.SMEM), *in_vmem(6)],
+    )(where, parts, held(came), *[held(g) for g in got])[0]
+
+
+def old_body(*refs):
+    for (codes, row, column, out), levels, beta in (
+        ((*refs[:3], refs[6]), 7.0, beta_first),
+        ((*refs[3:6], refs[7]), 15.0, beta_second),
     ):
         tall, wide = column_of(row[...]), column[...]
         for r in range(0, out.shape[0], STEP):
@@ -227,52 +242,43 @@
             out[r : r + STEP, :] = codes[0, r : r + STEP, :].astype(F32) * (beta / levels) * bound
 
 
-def keep(where, parts, came, jobs, got, old):
-    rows, cols = came.shape[2:]
-    each = VMEM((2 * rows, cols), F32)
+def old_moments(old):
+    _, rows, cols = old[0].shape
+    each = VMEM((rows, cols), F32)
+    return call(old_body, (each, each), [], 10 * rows * cols, 16 * rows * cols, in_vmem(6))(*old)
+
+
+def middle_body(half, blocks, sent, acc, first, second, *refs):
+    outs, total = refs[:-1], refs[-1]
+    rows, cols = acc.shape[2:]
+    peaks = []
+    for n, (i, ref) in enumerate(zip(blocks, (first, second))):
+        by = came_factor(ref.at[rows : rows + SIDE])[0:1]
+
+        def step(r, peak, ref=ref, by=by, i=i, n=n):
+            value = acc[half, i, pl.ds(r, STEP), :] + decode(ref[pl.ds(r, STEP), :], by)
+            if n >= sent:
+                outs[n][pl.ds(r, STEP), :] = value
+                return peak
+            total[n, pl.ds(r, STEP), :] = value
+            return jnp.maximum(peak, fold(jnp.abs(value), jnp.maximum))
+
+        peak = chunks(rows, step, jnp.zeros((8, cols), F32))
+        if n < sent:
+            peaks.append(jnp.max(peak, axis=0, keepdims=True))
+    send_blocks(total, outs[:sent], peaks, rows, 1)
+
+
+def middle(acc, got, half, blocks, sent):
+    rows, cols = acc.shape[2:]
     return call(
-        functools.partial(keep_body, jobs),
-        (VMEM((2, RING, rows, cols), F32), each, each),
-        [],
-        300 * rows * cols,
+        functools.partial(middle_body, half, blocks, sent),
+        tuple(VMEM((rows + SIDE, cols), I16) if n < sent else VMEM((rows, cols), F32) for n in range(2)),
+        [VMEM((sent, rows, cols), F32)],
         100 * rows * cols,
-        [pl.BlockSpec(memory_space=pltpu.SMEM), *in_vmem(12)],
-    )(where, parts, held(came), *[held(g) for g in got], *old)
-
-
-def middle_body(half, acc, first, second, *refs):
-    outs, kept, total = refs[:3], refs[3], refs[4]
-    rows, cols = kept.shape
-    peaks = []
-    for i in range(RING):
-        ref = first if i < 2 else second
-        by = came_factor(ref.at[2 * rows : 2 * rows + SIDE])[i % 2 : i % 2 + 1]
-
-        def step(r, peak, ref=ref, by=by, i=i):
-            value = acc[half, i, pl.ds(r, STEP), :] + decode(ref[pl.ds(i % 2 * rows + r, STEP), :], by)
-            if i == 3:
-                kept[pl.ds(r, STEP), :] = value
-                return peak
-            total[i, pl.ds(r, STEP), :] = value
-            return jnp.maximum(peak, fold(jnp.abs(value), jnp.maximum))
-
-        peak = chunks(rows, step, jnp.zeros((8, cols), F32))
-        if i < 3:
-            peaks.append(jnp.max(peak, axis=0, keepdims=True))
-    send_blocks(total, outs, peaks, rows, 1)
-
-
-def middle(acc, first, second, half):
-    rows, cols = acc.shape[2:]
-    sent = VMEM((rows + SIDE, cols), I16)
-    return call(
-        functools.partial(middle_body, half),
-        (sent, sent, sent, VMEM((rows, cols), F32)),
-        [VMEM((3, rows, cols), F32)],
-        200 * rows * cols,
-        32 * rows * cols,
+        16 * rows * cols,
         in_vmem(3),
-    )(acc, held(first), held(second))
+    )(acc, *[held(g) for g in got])
 
 
 def last_body(*refs):
@@ -310,7 +316,7 @@
     )(*flat)
 
 
-def reduce_scatter(parts, old, devices):
+def reduce_scatter(parts, devices):
     where = jnp.stack([lax.axis_index(a) for a in FSDP]).astype(jnp.int32)
     resident = held(parts)
     axis = ("y", "z")
@@ -321,8 +327,8 @@
     def swap(value):
         return lax.ppermute(value, "core", [(0, 1), (1, 0)])
 
-    def stage(half, jobs, came, source=resident, first=False, relayed=(), sends=()):
-        sent, more = pair(where, source, came, jobs, first, relayed, sends)
+    def stage(half, messages, came, source=resident, first=False, relayed=(), sends=()):
+        sent, more = pair(where, source, came, messages, first, relayed, sends)
         got = []
         for value, delta in zip(sent, (1, 3)):
             got.append(hop(value, axis[half], delta))
@@ -330,6 +336,9 @@
 
     def jobs_of(*each):
         return [tuple((half, delta, low) for delta, low in each) for half in range(2)]
+
+    def blocks_of(jobs, base=0, only=(0, 1)):
+        return tuple(tuple((job, base + q, i) for i in only) for q, job in enumerate(jobs))
 
     far, near = jobs_of((2, 0), (2, 2)), jobs_of((1, 2), (3, 0))
     join, mine = jobs_of((1, 0), (3, 2)), jobs_of((0, 0), (0, 2))
@@ -337,26 +346,28 @@
     came_far_0 = swap(out)
     out, own_far_0 = gather(where, parts, ((far[1], False), (far[0], True)))
     came_far_1 = swap(out)
-    far_0, _ = stage(0, far[0], came_far_0, own_far_0, True)
-    far_1, out = stage(1, far[1], came_far_1, sends=near)
+    far_0, _ = stage(0, blocks_of(far[0]), came_far_0, own_far_0, True)
+    far_1, out = stage(1, blocks_of(far[1]), came_far_1, sends=near)
     came_near = [swap(o) for o in out]
-    near_0, (out,) = stage(0, near[0], came_near[0], sends=(join[0] + join[1],))
+    near_0, (out,) = stage(0, blocks_of(near[0]), came_near[0], sends=(join[0] + join[1],))
     came_join = swap(out)
-    near_1, (out,) = stage(1, near[1], came_near[1], sends=(mine[0] + mine[1],))
+    near_1, (out,) = stage(1, blocks_of(near[1]), came_near[1], sends=(mine[0] + mine[1],))
     came_mine = swap(out)
-    join_0, _ = stage(0, join[0], came_join, relayed=far_0)
-    join_1, _ = stage(1, join[1], came_join, relayed=far_1)
-    acc, first_old, second_old = keep(
-        where, resident, came_mine, mine[0] + mine[1], (*near_0, *near_1), old
-    )
+    joined = {}
+    for only in range(2):
+        for half, relayed in enumerate((far_0, far_1)):
+            messages = blocks_of(join[half], 2 * half, (only,))
+            joined[only, half], _ = stage(half, messages, came_join, relayed=relayed)
+    acc = keep(where, resident, came_mine, mine[0] + mine[1], (*near_0, *near_1))
     halves = []
-    for half, joined in enumerate((join_0, join_1)):
-        *out, kept = middle(acc, *joined, half)
+    for half in range(2):
+        near_out, far_out = middle(acc, joined[0, half], half, (0, 2), 2)
+        back_out, kept = middle(acc, joined[1, half], half, (1, 3), 1)
         got = []
-        for k, delta in ((2, 2), (0, 1), (1, 3)):
-            got.append(hop(out[k], axis[1 - half], delta))
+        for out, delta in ((far_out, 2), (near_out, 1), (back_out, 3)):
+            got.append(hop(out, axis[1 - half], delta))
         halves.append([kept] + got)
-    return *last(halves, devices), first_old, second_old
+    return last(halves, devices)
 
 
 def clip_body(limit, squares, grad, first_old, second_old, first_new, second_new, peaks):
@@ -447,23 +458,24 @@
             out[...] = wide
             inverse[k : k + 1, :] = 1.0 / wide
 
+    step = first_scaled.shape[1]
+    rows = pl.ds(pl.multiple_of(pl.program_id(0) * step, step), step)
     for k, (values, by, out) in enumerate(
         ((first_new, by_first, first_scaled), (second_new, by_second, second_scaled))
     ):
-        out[0] = values[...] * jnp.maximum(by[:, 0:1], inverse[k : k + 1, :])
+        out[0] = values[rows, :] * jnp.maximum(by[rows, 0:1], inverse[k : k + 1, :])
 
 
 def scaled_outputs(peaks, first_new, second_new, by_first, by_second):
     rows, cols = first_new.shape
     step = min(rows, 64)
-    whole, side = pl.BlockSpec((step, cols), lambda r: (r, 0)), pl.BlockSpec((step, 128), lambda r: (r, 0))
     out, line = pl.BlockSpec((1, step, cols), lambda r: (0, r, 0)), pl.BlockSpec((1, cols), lambda r: (0, 0))
     big, wide = jax.ShapeDtypeStruct((1, rows, cols), F32), jax.ShapeDtypeStruct((1, cols), F32)
     return pl.pallas_call(
         scaled_body,
         grid=(rows // step,),
         out_shape=(big, big, wide, wide),
-        in_specs=[pl.BlockSpec(memory_space=VMEM), whole, whole, side, side],
+        in_specs=in_vmem(5),
         out_specs=(out, out, line, line),
         scratch_shapes=[VMEM((8, cols), F32)],
         compiler_params=pltpu.CompilerParams(vmem_limit_bytes=VMEM_LIMIT),
@@ -484,7 +496,8 @@
     devices, group = lax.axis_size(AXES), lax.axis_size(FSDP)
     parts = grad_parts.reshape(RING * RING, 2, 2, -1, col_count)
     old = (first_codes, first_rows, first_columns, second_codes, second_rows, second_columns)
-    gradient, squares, first_old, second_old = reduce_scatter(parts, old, devices)
+    gradient, squares = reduce_scatter(parts, devices)
+    first_old, second_old = old_moments(old)
     squares = exchange(squares, AXES)
     clip_limit = clip_rms * math.sqrt(entries)
     first_new, second_new, peaks = clip(squares, gradient, first_old, second_old, clip_limit, group)

time: 132 us -> 143 us (1.083)
  blocking collectives: 18.4 us -> 0 us
  starting transfers between devices: 38.7 us -> 57.1 us
  waiting for transfers between devices: 46.3 us -> 51 us
  local copies, waits for them, and re-layouts: 0.35 us -> 4.73 us
  Pallas kernels: 27.3 us -> 29.1 us
    all_to_all x1 -> x0, blocking collectives: 18.4 us -> none  [exchange(): return lax.all_to_all(value, axes, split_axis=0, concat_axis=0, tiled=True)]
    all_to_all x1 -> x2, starting transfers between devices: 4.75 us -> 23 us  [exchange(): return lax.all_to_all(value, axes, split_axis=0, concat_axis=0, tiled=True)]
    all_to_all x1 -> x2, waiting for transfers between devices: 7.72 us -> 14.6 us  [exchange(): return lax.all_to_all(value, axes, split_axis=0, concat_axis=0, tiled=True)]
    unnamed x22 -> x30, local copies, waits for them, and re-layouts: 0.35 us -> 4.73 us
    ppermute x18 -> x22, waiting for transfers between devices: 36.3 us -> 34.1 us  [hop(): lax.ppermute(value, name, [(i, (i + delta) % RING) for i in range(RING)])]
    pallas_call x8 -> x13, Pallas kernels: 14.4 us -> 16 us  [the longest x8 12.9 us: pair(): call(functools.partial(pair_body, messages, first, len(relayed), sends),...]
    ppermute x18 -> x22, starting transfers between devices: 28.9 us -> 29 us  [hop(): lax.ppermute(value, name, [(i, (i + delta) % RING) for i in range(RING)])]
  transfers between devices with their start and end apart: 25 -> 30, of which waited for: 8 -> 10; matrix products, arithmetic and copies ran while one was open for 0% -> 0% of each run, Pallas kernels for 14% -> 14%
where the time goes in v4:
time: 143 us
  starting transfers between devices  57.1 us (40%)
  waiting for transfers between devices  51 us (36%)
  Pallas kernels  29.1 us (20%)
  local copies, waits for them, and re-layouts  4.73 us (3%)
    ppermute x22, waiting for transfers between devices, hop(): lax.ppermute(value, name, [(i, (i + delta) % RING) for i in range(RING)])  34.1 us
    ppermute x22, starting transfers between devices, hop(): lax.ppermute(value, name, [(i, (i + delta) % RING) for i in range(RING)])  29 us
    all_to_all x2, starting transfers between devices, exchange(): return lax.all_to_all(value, axes, split_axis=0, concat_axis=0, tiled=True)  23 us
    all_to_all x2, waiting for transfers between devices, exchange(): return lax.all_to_all(value, axes, split_axis=0, concat_axis=0, tiled=True)  14.6 us
    pallas_call x8, Pallas kernels, pair(): call(functools.partial(pair_body, messages, first, len(relayed), sends),...  12.9 us
    ppermute x6, starting transfers between devices, swap(): return lax.ppermute(value, 'core', [(0, 1), (1, 0)])  5.12 us
    unnamed x30, local copies, waits for them, and re-layouts  4.73 us
    pallas_call x2, Pallas kernels, gather(): call(functools.partial(gather_body, wanted), tuple((VMEM((len(jobs), 2, r...  4.73 us
  transfers between devices with their start and end apart: 30, of which 10 were waited for; matrix products, arithmetic and copies ran while one was open for 0% of the time, Pallas kernels for 14%

profile of v4, /device:TPU:1, one launch (start us, length us, event | category | flops | bytes accessed | tf_op | source)
XLA Modules:
  0.0 143.1 jit_solution(12589932319827769956)
XLA Ops:
  0.7 2.3 %shard_map.126 = (bf16[2,2,128,1024]{3,2,1,0:T(8,128)(2,1)S(1)}, bf16[2,2,128,1024]{3,2,1,0:T(8,128)(2,1)S(1)}) custom-call(s32[3]{0:T(128)S(1)} %pad_add_fusion.where.refs_0_, bf16[16,2,2,128,1024]{4,3,2,1,0:T(8,128)(2,1)} %bitcast.8), custom_call_target="tpu_custom_call" | custom-call | flops 1048576 | bytes 4194304 | tf_op jit(solution)/shard_map/pallas_call | solution.py:111
  3.1 1.5 %collective-permute-start = (bf16[2,2,128,1024]{3,2,1,0:T(8,128)(2,1)S(1)}, bf16[2,2,128,1024]{3,2,1,0:T(8,128)(2,1)S(1)}, u32[]{:S(2)}, u32[]{:S(2)}) collective-permute-start(bf16[2,2,128,1024]{3,2,1,0:T(8,128)(2,1)S(1)} %get-tuple-element.53), channel_id=1, source_target_pairs={{0,1},{1,0},{2,3},{3,2},{4,5},{5,4},{6,7},{7,6},{8,9},{9,8},{10,11... | collective-permute-start | bytes 3145736 | tf_op jit(solution)/shard_map/ppermute | solution.py:328
  4.5 2.3 %collective-permute-done.refs_2_ = bf16[2,2,128,1024]{3,2,1,0:T(8,128)(2,1)S(1)} collective-permute-done((bf16[2,2,128,1024]{3,2,1,0:T(8,128)(2,1)S(1)}, bf16[2,2,128,1024]{3,2,1,0:T(8,128)(2,1)S(1)}, u32[]{:S(2)}, u32[]{:S(2)}) %collective-permute-start) | collective-permute-done | bytes 1048608 | tf_op jit(solution)/shard_map/ppermute | solution.py:328
  7.1 1.8 %shard_map.127 = (s16[264,1024]{1,0:T(8,128)(2,1)S(1)}, s16[264,1024]{1,0:T(8,128)(2,1)S(1)}, bf16[2,2,128,1024]{3,2,1,0:T(8,128)(2,1)S(1)}, bf16[2,2,128,1024]{3,2,1,0:T(8,128)(2,1)S(1)}) custom-call(s32[3]{0:T(128)S(1)} %pad_add_fusion.where.refs_0_, bf16[16,2,2,128,1024]{4,3,2,1,0:T(8,128)(2,1)S(1)} %bitcast.10, ...), custom_call_target="tpu_custom_call" | custom-call | flops 26214400 | bytes 3145728 | tf_op jit(solution)/shard_map/pallas_call | solution.py:183
  9.0 1.5 %collective-permute-start.3 = (bf16[2,2,128,1024]{3,2,1,0:T(8,128)(2,1)S(1)}, bf16[2,2,128,1024]{3,2,1,0:T(8,128)(2,1)S(1)}, u32[]{:S(2)}, u32[]{:S(2)}) collective-permute-start(bf16[2,2,128,1024]{3,2,1,0:T(8,128)(2,1)S(1)} %get-tuple-element.56), channel_id=1, source_target_pairs={{0,1},{1,0},{2,3},{3,2},{4,5},{5,4},{6,7},{7,6},{8,9},{9,8},{10,11... | collective-permute-start | bytes 3145736 | tf_op jit(solution)/shard_map/ppermute | solution.py:328
  10.5 2.4 %shard_map.131 = bf16[2,2,128,1024]{3,2,1,0:T(8,128)(2,1)S(1)} custom-call(s32[3]{0:T(128)S(1)} %pad_add_fusion.where.refs_0_, bf16[16,2,2,128,1024]{4,3,2,1,0:T(8,128)(2,1)} %bitcast.9), custom_call_target="tpu_custom_call" | custom-call | flops 524288 | bytes 2097152 | tf_op jit(solution)/shard_map/pallas_call | solution.py:111
  13.6 1.8 %shard_map.129 = (s16[264,1024]{1,0:T(8,128)(2,1)S(1)}, s16[264,1024]{1,0:T(8,128)(2,1)S(1)}, bf16[4,2,128,1024]{3,2,1,0:T(8,128)(2,1)S(1)}) custom-call(s32[3]{0:T(128)S(1)} %pad_add_fusion.where.refs_0_, bf16[16,2,2,128,1024]{4,3,2,1,0:T(8,128)(2,1)S(1)} %bitcast.13, bf16[2,2,128,1024]{3,2,1,0:T(8,128)(2,1)S(1)} %collective-permute-done.3.refs_2_), custom_call_target="tpu_custom_call" | custom-call | flops 26214400 | bytes 3145728 | tf_op jit(solution)/shard_map/pallas_call | solution.py:183
  15.4 1.4 collective-permute-start.8
  16.8 1.8 %shard_map.128 = (s16[264,1024]{1,0:T(8,128)(2,1)S(1)}, s16[264,1024]{1,0:T(8,128)(2,1)S(1)}, bf16[4,2,128,1024]{3,2,1,0:T(8,128)(2,1)S(1)}) custom-call(s32[3]{0:T(128)S(1)} %pad_add_fusion.where.refs_0_, bf16[16,2,2,128,1024]{4,3,2,1,0:T(8,128)(2,1)S(1)} %bitcast.14, bf16[2,2,128,1024]{3,2,1,0:T(8,128)(2,1)S(1)} %collective-permute-done.1.refs_2_), custom_call_target="tpu_custom_call" | custom-call | flops 26214400 | bytes 3145728 | tf_op jit(solution)/shard_map/pallas_call | solution.py:183
  18.7 1.7 %shard_map.132 = (s16[264,1024]{1,0:T(8,128)(2,1)S(1)}, s16[264,1024]{1,0:T(8,128)(2,1)S(1)}) custom-call(s32[3]{0:T(128)S(1)} %pad_add_fusion.where.refs_0_, bf16[2,2,128,1024]{3,2,1,0:T(8,128)(2,1)S(1)} %get-tuple-element.62.refs_1_, bf16[2,2,128,1024]{3,2,1,0:T(8,128)(2,1)S(1)} %collective-permute-done.9.refs_2_), custom_call_target="tpu_custom_call" | custom-call | flops 26214400 | bytes 3145728 | tf_op jit(solution)/shard_map/pallas_call | solution.py:183
  20.4 1.5 %collective-permute-start.10 = (s16[264,1024]{1,0:T(8,128)(2,1)S(1)}, s16[264,1024]{1,0:T(8,128)(2,1)S(1)}, u32[]{:S(2)}, u32[]{:S(2)}) collective-permute-start(s16[264,1024]{1,0:T(8,128)(2,1)S(1)} %get-tuple-element.63), channel_id=1, source_target_pairs={{0,8},{8,16},{16,24},{24,0},{1,9},{9,17},{17,25},{25,1},{2,10},{10... | collective-permute-start | bytes 1622024 | tf_op jit(solution)/shard_map/ppermute | solution.py:325
  21.9 1.5 %collective-permute-start.11 = (s16[264,1024]{1,0:T(8,128)(2,1)S(1)}, s16[264,1024]{1,0:T(8,128)(2,1)S(1)}, u32[]{:S(2)}, u32[]{:S(2)}) collective-permute-start(s16[264,1024]{1,0:T(8,128)(2,1)S(1)} %get-tuple-element.64), channel_id=1, source_target_pairs={{0,24},{8,0},{16,8},{24,16},{1,25},{9,1},{17,9},{25,17},{2,26},{10... | collective-permute-start | bytes 1622024 | tf_op jit(solution)/shard_map/ppermute | solution.py:325
  23.4 1.6 %collective-permute-start.19 = (s16[264,1024]{1,0:T(8,128)(2,1)S(1)}, s16[264,1024]{1,0:T(8,128)(2,1)S(1)}, u32[]{:S(2)}, u32[]{:S(2)}) collective-permute-start(s16[264,1024]{1,0:T(8,128)(2,1)S(1)} %get-tuple-element.73), channel_id=1, source_target_pairs={{0,2},{2,4},{4,6},{6,0},{1,3},{3,5},{5,7},{7,1},{8,10},{10,12},{12... | collective-permute-start | bytes 1622024 | tf_op jit(solution)/shard_map/ppermute | solution.py:325
  25.0 10.3 %collective-permute-done.10.refs_3_ = s16[264,1024]{1,0:T(8,128)(2,1)S(1)} collective-permute-done((s16[264,1024]{1,0:T(8,128)(2,1)S(1)}, s16[264,1024]{1,0:T(8,128)(2,1)S(1)}, u32[]{:S(2)}, u32[]{:S(2)}) %collective-permute-start.10) | collective-permute-done | bytes 540704 | tf_op jit(solution)/shard_map/ppermute | solution.py:325
  35.4 3.6 %collective-permute-start.20 = (s16[264,1024]{1,0:T(8,128)(2,1)S(1)}, s16[264,1024]{1,0:T(8,128)(2,1)S(1)}, u32[]{:S(2)}, u32[]{:S(2)}) collective-permute-start(s16[264,1024]{1,0:T(8,128)(2,1)S(1)} %get-tuple-element.74), channel_id=1, source_target_pairs={{0,6},{2,0},{4,2},{6,4},{1,7},{3,1},{5,3},{7,5},{8,14},{10,8},{12,... | collective-permute-start | bytes 1622024 | tf_op jit(solution)/shard_map/ppermute | solution.py:325
  39.0 2.7 %collective-permute-start.5 = (s16[264,1024]{1,0:T(8,128)(2,1)S(1)}, s16[264,1024]{1,0:T(8,128)(2,1)S(1)}, u32[]{:S(2)}, u32[]{:S(2)}) collective-permute-start(s16[264,1024]{1,0:T(8,128)(2,1)S(1)} %get-tuple-element.58), channel_id=1, source_target_pairs={{0,24},{8,0},{16,8},{24,16},{1,25},{9,1},{17,9},{25,17},{2,26},{10... | collective-permute-start | bytes 1622024 | tf_op jit(solution)/shard_map/ppermute | solution.py:325
  41.7 7.7 %collective-permute-done.20.refs_4_ = s16[264,1024]{1,0:T(8,128)(2,1)S(1)} collective-permute-done((s16[264,1024]{1,0:T(8,128)(2,1)S(1)}, s16[264,1024]{1,0:T(8,128)(2,1)S(1)}, u32[]{:S(2)}, u32[]{:S(2)}) %collective-permute-start.20) | collective-permute-done | bytes 540704 | tf_op jit(solution)/shard_map/ppermute | solution.py:325
  49.8 3.0 %collective-permute-start.7 = (s16[264,1024]{1,0:T(8,128)(2,1)S(1)}, s16[264,1024]{1,0:T(8,128)(2,1)S(1)}, u32[]{:S(2)}, u32[]{:S(2)}) collective-permute-start(s16[264,1024]{1,0:T(8,128)(2,1)S(1)} %get-tuple-element.60), channel_id=1, source_target_pairs={{0,6},{2,0},{4,2},{6,4},{1,7},{3,1},{5,3},{7,5},{8,14},{10,8},{12,... | collective-permute-start | bytes 1622024 | tf_op jit(solution)/shard_map/ppermute | solution.py:325
  52.8 1.4 %shard_map.133 = (s16[136,1024]{1,0:T(8,128)(2,1)S(1)}, s16[136,1024]{1,0:T(8,128)(2,1)S(1)}) custom-call(s32[3]{0:T(128)S(1)} %pad_add_fusion.where.refs_0_, bf16[16,2,2,128,1024]{4,3,2,1,0:T(8,128)(2,1)S(1)} %bitcast.15, bf16[4,2,128,1024]{3,2,1,0:T(8,128)(2,1)S(1)} %collective-permute-done.8.refs_2_, ...), custom_call_target="tpu_custom_call" | custom-call | flops 13107200 | bytes 1572864 | tf_op jit(solution)/shard_map/pallas_call | solution.py:183
  54.3 1.4 %shard_map.135 = (s16[136,1024]{1,0:T(8,128)(2,1)S(1)}, s16[136,1024]{1,0:T(8,128)(2,1)S(1)}) custom-call(s32[3]{0:T(128)S(1)} %pad_add_fusion.where.refs_0_, bf16[16,2,2,128,1024]{4,3,2,1,0:T(8,128)(2,1)S(1)} %bitcast.16, bf16[4,2,128,1024]{3,2,1,0:T(8,128)(2,1)S(1)} %collective-permute-done.8.refs_2_, ...), custom_call_target="tpu_custom_call" | custom-call | flops 13107200 | bytes 1572864 | tf_op jit(solution)/shard_map/pallas_call | solution.py:183
  55.8 1.3 collective-permute-start.14
  57.0 6.3 %collective-permute-done.6.refs_2_ = s16[264,1024]{1,0:T(8,128)(2,1)S(1)} collective-permute-done((s16[264,1024]{1,0:T(8,128)(2,1)S(1)}, s16[264,1024]{1,0:T(8,128)(2,1)S(1)}, u32[]{:S(2)}, u32[]{:S(2)}) %collective-permute-start.6) | collective-permute-done | bytes 540704 | tf_op jit(solution)/shard_map/ppermute | solution.py:325
  63.3 1.3 collective-permute-start.15
  65.0 1.4 %shard_map.139 = (s16[136,1024]{1,0:T(8,128)(2,1)S(1)}, s16[136,1024]{1,0:T(8,128)(2,1)S(1)}) custom-call(s32[3]{0:T(128)S(1)} %pad_add_fusion.where.refs_0_, bf16[16,2,2,128,1024]{4,3,2,1,0:T(8,128)(2,1)S(1)} %bitcast.17, bf16[4,2,128,1024]{3,2,1,0:T(8,128)(2,1)S(1)} %collective-permute-done.8.refs_2_, ...), custom_call_target="tpu_custom_call" | custom-call | flops 13107200 | bytes 1572864 | tf_op jit(solution)/shard_map/pallas_call | solution.py:183
  66.9 2.2 %shard_map.130.acc = f32[2,4,128,1024]{3,2,1,0:T(8,128)S(1)} custom-call(s32[3]{0:T(128)S(1)} %pad_add_fusion.where.refs_0_, bf16[16,2,2,128,1024]{4,3,2,1,0:T(8,128)(2,1)S(1)} %bitcast.18, bf16[4,2,128,1024]{3,2,1,0:T(8,128)(2,1)S(1)} %collective-permute-done.2.came, s16[264,1024]{1,0:T(8,128)(2,1)S(1)} %collective-permute-done.4.refs_0_, ...), custom_call_target="tpu_custom_call" | custom-call | flops 26214400 | bytes 10485760 | tf_op jit(solution)/shard_map/pallas_call | solution.py:224
  69.1 2.6 %collective-permute-start.24 = (s16[136,1024]{1,0:T(8,128)(2,1)S(1)}, s16[136,1024]{1,0:T(8,128)(2,1)S(1)}, u32[]{:S(2)}, u32[]{:S(2)}) collective-permute-start(s16[136,1024]{1,0:T(8,128)(2,1)S(1)} %get-tuple-element.79), channel_id=1, source_target_pairs={{0,6},{2,0},{4,2},{6,4},{1,7},{3,1},{5,3},{7,5},{8,14},{10,8},{12,... | collective-permute-start | bytes 835592 | tf_op jit(solution)/shard_map/ppermute | solution.py:325
  71.7 1.4 %shard_map.137 = (s16[136,1024]{1,0:T(8,128)(2,1)S(1)}, s16[136,1024]{1,0:T(8,128)(2,1)S(1)}) custom-call(s32[3]{0:T(128)S(1)} %pad_add_fusion.where.refs_0_, bf16[16,2,2,128,1024]{4,3,2,1,0:T(8,128)(2,1)S(1)} %bitcast.19, bf16[4,2,128,1024]{3,2,1,0:T(8,128)(2,1)S(1)} %collective-permute-done.8.refs_2_, ...), custom_call_target="tpu_custom_call" | custom-call | flops 13107200 | bytes 1572864 | tf_op jit(solution)/shard_map/pallas_call | solution.py:183
  73.3 2.7 %collective-permute-start.22 = (s16[136,1024]{1,0:T(8,128)(2,1)S(1)}, s16[136,1024]{1,0:T(8,128)(2,1)S(1)}, u32[]{:S(2)}, u32[]{:S(2)}) collective-permute-start(s16[136,1024]{1,0:T(8,128)(2,1)S(1)} %get-tuple-element.76), channel_id=1, source_target_pairs={{0,6},{2,0},{4,2},{6,4},{1,7},{3,1},{5,3},{7,5},{8,14},{10,8},{12,... | collective-permute-start | bytes 835592 | tf_op jit(solution)/shard_map/ppermute | solution.py:325
  76.0 0.8 shard_map.136
  78.0 2.1 %collective-permute-start.18 = (s16[136,1024]{1,0:T(8,128)(2,1)S(1)}, s16[136,1024]{1,0:T(8,128)(2,1)S(1)}, u32[]{:S(2)}, u32[]{:S(2)}) collective-permute-start(s16[136,1024]{1,0:T(8,128)(2,1)S(1)} %get-tuple-element.72), channel_id=1, source_target_pairs={{0,6},{2,0},{4,2},{6,4},{1,7},{3,1},{5,3},{7,5},{8,14},{10,8},{12,... | collective-permute-start | bytes 835592 | tf_op jit(solution)/shard_map/ppermute | solution.py:325
  80.9 1.6 %collective-permute-start.25 = (s16[136,1024]{1,0:T(8,128)(2,1)S(1)}, s16[136,1024]{1,0:T(8,128)(2,1)S(1)}, u32[]{:S(2)}, u32[]{:S(2)}) collective-permute-start(s16[136,1024]{1,0:T(8,128)(2,1)S(1)} %get-tuple-element.80), channel_id=1, source_target_pairs={{0,16},{8,24},{16,0},{24,8},{1,17},{9,25},{17,1},{25,9},{2,18},{10... | collective-permute-start | bytes 835592 | tf_op jit(solution)/shard_map/ppermute | solution.py:325
  82.5 0.9 collective-permute-done.22.second
  83.4 1.0 collective-permute-start.26
  85.1 1.9 %collective-permute-done.16.refs_1_ = s16[136,1024]{1,0:T(8,128)(2,1)S(1)} collective-permute-done((s16[136,1024]{1,0:T(8,128)(2,1)S(1)}, s16[136,1024]{1,0:T(8,128)(2,1)S(1)}, u32[]{:S(2)}, u32[]{:S(2)}) %collective-permute-start.16) | collective-permute-done | bytes 278560 | tf_op jit(solution)/shard_map/ppermute | solution.py:325
  87.4 5.7 %collective-permute-done.17.refs_2_ = s16[136,1024]{1,0:T(8,128)(2,1)S(1)} collective-permute-done((s16[136,1024]{1,0:T(8,128)(2,1)S(1)}, s16[136,1024]{1,0:T(8,128)(2,1)S(1)}, u32[]{:S(2)}, u32[]{:S(2)}) %collective-permute-start.17) | collective-permute-done | bytes 278560 | tf_op jit(solution)/shard_map/ppermute | solution.py:325
  93.1 1.3 collective-permute-done.18.refs_3_
  94.4 1.6 %shard_map.141 = (f32[256,1024]{1,0:T(8,128)S(1)}, f32[128,128]{1,0:T(8,128)}) custom-call(f32[128,1024]{1,0:T(8,128)S(1)} %get-tuple-element.67.refs_0_, s16[136,1024]{1,0:T(8,128)(2,1)S(1)} %collective-permute-done.16.refs_1_, s16[136,1024]{1,0:T(8,128)(2,1)S(1)} %collective-permute-done.17.refs_2_, s16[136,1024]{1,0:T(8,128)(2,1)S(1)} %collective-permute-done.18.refs_3_, ...), custom_call_target="tpu_custom_call" | custom-call | flops 13107200 | bytes 4194304 | tf_op jit(solution)/shard_map/pallas_call | solution.py:309
  96.0 18.3 %all-to-all-start = ((f32[128,1,128]{2,1,0:T(1,128)}), f32[128,1,128]{2,1,0:T(1,128)S(1)}, u32[]{:S(2)}, u32[]{:S(2)}) async-start(f32[128,1,128]{2,1,0:T(1,128)} %bitcast.5), calls=%async_computation | async-start | bytes 131072 | tf_op jit(solution)/shard_map/all_to_all | solution.py:488
  114.8 1.0 copy-done.1
  115.7 1.0 copy-done.3
  116.7 6.9 %all-to-all-done = f32[128,1,128]{2,1,0:T(1,128)S(1)} async-done(((f32[128,1,128]{2,1,0:T(1,128)}), f32[128,1,128]{2,1,0:T(1,128)S(1)}, u32[]{:S(2)}, u32[]{:S(2)}) %all-to-all-start) | async-done | bytes 65568 | tf_op jit(solution)/shard_map/all_to_all | solution.py:488
  123.6 1.2 copy-done.2
  124.8 1.2 copy-done.4
  126.1 1.2 shard_map.143
  127.3 4.7 %all-to-all-start.1 = ((f32[32,16,128]{2,1,0:T(8,128)}), f32[32,16,128]{2,1,0:T(8,128)S(1)}, u32[]{:S(2)}, u32[]{:S(2)}) async-start(f32[32,16,128]{2,1,0:T(8,128)} %get-tuple-element.90), calls=%async_computation.1 | async-start | bytes 524288 | tf_op jit(solution)/shard_map/all_to_all | solution.py:488
  132.1 1.3 row_outputs.1
  133.4 7.7 %all-to-all-done.1.peaks = f32[32,16,128]{2,1,0:T(8,128)S(1)} async-done(((f32[32,16,128]{2,1,0:T(8,128)}), f32[32,16,128]{2,1,0:T(8,128)S(1)}, u32[]{:S(2)}, u32[]{:S(2)}) %all-to-all-start.1) | async-done | bytes 262176 | tf_op jit(solution)/shard_map/all_to_all | solution.py:488
  141.1 2.0 %scaled_outputs.1 = (f32[1,256,1024]{2,1,0:T(8,128)}, f32[1,256,1024]{2,1,0:T(8,128)}, f32[1,1024]{1,0:T(1,128)}, f32[1,1024]{1,0:T(1,128)}) custom-call(f32[32,16,128]{2,1,0:T(8,128)S(1)} %all-to-all-done.1.peaks, f32[256,1024]{1,0:T(8,128)S(1)} %get-tuple-element.87.first_new, f32[256,1024]{1,0:T(8,128)S(1)} %get-tuple-element.88.second_new, ...), custom_call_target="tpu_custom_call" | custom-call | flops 2097152 | bytes 4194304 | tf_op jit(solution)/shard_map/scaled_outputs/pallas_call | solution.py:474
  (64 shorter events, 6.1 us)
Async XLA Ops:
  0.7 6.4 %copy-start = (bf16[1,1,8192,1024]{3,2,1,0:T(8,128)(2,1)S(1)}, bf16[1,1,8192,1024]{3,2,1,0:T(8,128)(2,1)}, u32[]{:S(2)}) copy-start(bf16[1,1,8192,1024]{3,2,1,0:T(8,128)(2,1)} %param.7) | copy-start | bytes 50331652
  3.1 3.7 %collective-permute-start = (bf16[2,2,128,1024]{3,2,1,0:T(8,128)(2,1)S(1)}, bf16[2,2,128,1024]{3,2,1,0:T(8,128)(2,1)S(1)}, u32[]{:S(2)}, u32[]{:S(2)}) collective-permute-start(bf16[2,2,128,1024]{3,2,1,0:T(8,128)(2,1)S(1)} %get-tuple-element.53), channel_id=1, source_target_pairs={{0,1},{1,0},{2,3},{3,2},{4,5},{5,4},{6,7},{7,6},{8,9},{9,8},{10,11... | collective-permute-start | bytes 3145736 | tf_op jit(solution)/shard_map/ppermute | solution.py:328
  7.1 6.4 %slice-start = ((s8[16777216]{0:T(1024)(128)(4,1)}), s8[4194304]{0:T(1024)(128)(4,1)S(1)}, s32[]{:S(2)}) async-start(s8[16777216]{0:T(1024)(128)(4,1)} %bitcast.11), calls=%async_computation.2 | async-start | bytes 8388608
  7.1 6.4 %slice-start.1 = ((s8[16777216]{0:T(1024)(128)(4,1)}), s8[4194304]{0:T(1024)(128)(4,1)S(1)}, s32[]{:S(2)}) async-start(s8[16777216]{0:T(1024)(128)(4,1)} %bitcast.11), calls=%async_computation.3 | async-start | bytes 8388608
  8.9 4.6 %slice-start.2 = ((s8[16777216]{0:T(1024)(128)(4,1)}), s8[4194304]{0:T(1024)(128)(4,1)S(1)}, s32[]{:S(2)}) async-start(s8[16777216]{0:T(1024)(128)(4,1)} %bitcast.11), calls=%async_computation.4 | async-start | bytes 8388608
  9.0 4.6 %collective-permute-start.3 = (bf16[2,2,128,1024]{3,2,1,0:T(8,128)(2,1)S(1)}, bf16[2,2,128,1024]{3,2,1,0:T(8,128)(2,1)S(1)}, u32[]{:S(2)}, u32[]{:S(2)}) collective-permute-start(bf16[2,2,128,1024]{3,2,1,0:T(8,128)(2,1)S(1)} %get-tuple-element.56), channel_id=1, source_target_pairs={{0,1},{1,0},{2,3},{3,2},{4,5},{5,4},{6,7},{7,6},{8,9},{9,8},{10,11... | collective-permute-start | bytes 3145736 | tf_op jit(solution)/shard_map/ppermute | solution.py:328
  10.4 3.2 %slice-start.3 = ((s8[16777216]{0:T(1024)(128)(4,1)}), s8[4194304]{0:T(1024)(128)(4,1)S(1)}, s32[]{:S(2)}) async-start(s8[16777216]{0:T(1024)(128)(4,1)} %bitcast.11), calls=%async_computation.5 | async-start | bytes 8388608
  10.4 6.4 %collective-permute-start.1 = (bf16[2,2,128,1024]{3,2,1,0:T(8,128)(2,1)S(1)}, bf16[2,2,128,1024]{3,2,1,0:T(8,128)(2,1)S(1)}, u32[]{:S(2)}, u32[]{:S(2)}) collective-permute-start(bf16[2,2,128,1024]{3,2,1,0:T(8,128)(2,1)S(1)} %get-tuple-element.54), channel_id=1, source_target_pairs={{0,1},{1,0},{2,3},{3,2},{4,5},{5,4},{6,7},{7,6},{8,9},{9,8},{10,11... | collective-permute-start | bytes 3145736 | tf_op jit(solution)/shard_map/ppermute | solution.py:328
  12.9 5.8 %collective-permute-start.9 = (bf16[2,2,128,1024]{3,2,1,0:T(8,128)(2,1)S(1)}, bf16[2,2,128,1024]{3,2,1,0:T(8,128)(2,1)S(1)}, u32[]{:S(2)}, u32[]{:S(2)}) collective-permute-start(bf16[2,2,128,1024]{3,2,1,0:T(8,128)(2,1)S(1)} %shard_map.131), channel_id=1, source_target_pairs={{0,1},{1,0},{2,3},{3,2},{4,5},{5,4},{6,7},{7,6},{8,9},{9,8},{10,11... | collective-permute-start | bytes 3145736 | tf_op jit(solution)/shard_map/ppermute | solution.py:328
  15.4 34.4 %collective-permute-start.8 = (bf16[4,2,128,1024]{3,2,1,0:T(8,128)(2,1)S(1)}, bf16[4,2,128,1024]{3,2,1,0:T(8,128)(2,1)S(1)}, u32[]{:S(2)}, u32[]{:S(2)}) collective-permute-start(bf16[4,2,128,1024]{3,2,1,0:T(8,128)(2,1)S(1)} %get-tuple-element.61), channel_id=1, source_target_pairs={{0,1},{1,0},{2,3},{3,2},{4,5},{5,4},{6,7},{7,6},{8,9},{9,8},{10,11... | collective-permute-start | bytes 6291464 | tf_op jit(solution)/shard_map/ppermute | solution.py:328
  18.6 47.9 %collective-permute-start.2 = (bf16[4,2,128,1024]{3,2,1,0:T(8,128)(2,1)S(1)}, bf16[4,2,128,1024]{3,2,1,0:T(8,128)(2,1)S(1)}, u32[]{:S(2)}, u32[]{:S(2)}) collective-permute-start(bf16[4,2,128,1024]{3,2,1,0:T(8,128)(2,1)S(1)} %get-tuple-element.55), channel_id=1, source_target_pairs={{0,1},{1,0},{2,3},{3,2},{4,5},{5,4},{6,7},{7,6},{8,9},{9,8},{10,11... | collective-permute-start | bytes 6291464 | tf_op jit(solution)/shard_map/ppermute | solution.py:328
  20.4 15.0 %collective-permute-start.10 = (s16[264,1024]{1,0:T(8,128)(2,1)S(1)}, s16[264,1024]{1,0:T(8,128)(2,1)S(1)}, u32[]{:S(2)}, u32[]{:S(2)}) collective-permute-start(s16[264,1024]{1,0:T(8,128)(2,1)S(1)} %get-tuple-element.63), channel_id=1, source_target_pairs={{0,8},{8,16},{16,24},{24,0},{1,9},{9,17},{17,25},{25,1},{2,10},{10... | collective-permute-start | bytes 1622024 | tf_op jit(solution)/shard_map/ppermute | solution.py:325
  21.9 17.1 %collective-permute-start.11 = (s16[264,1024]{1,0:T(8,128)(2,1)S(1)}, s16[264,1024]{1,0:T(8,128)(2,1)S(1)}, u32[]{:S(2)}, u32[]{:S(2)}) collective-permute-start(s16[264,1024]{1,0:T(8,128)(2,1)S(1)} %get-tuple-element.64), channel_id=1, source_target_pairs={{0,24},{8,0},{16,8},{24,16},{1,25},{9,1},{17,9},{25,17},{2,26},{10... | collective-permute-start | bytes 1622024 | tf_op jit(solution)/shard_map/ppermute | solution.py:325
  23.4 15.6 %collective-permute-start.19 = (s16[264,1024]{1,0:T(8,128)(2,1)S(1)}, s16[264,1024]{1,0:T(8,128)(2,1)S(1)}, u32[]{:S(2)}, u32[]{:S(2)}) collective-permute-start(s16[264,1024]{1,0:T(8,128)(2,1)S(1)} %get-tuple-element.73), channel_id=1, source_target_pairs={{0,2},{2,4},{4,6},{6,0},{1,3},{3,5},{5,7},{7,1},{8,10},{10,12},{12... | collective-permute-start | bytes 1622024 | tf_op jit(solution)/shard_map/ppermute | solution.py:325
  35.4 14.0 %collective-permute-start.20 = (s16[264,1024]{1,0:T(8,128)(2,1)S(1)}, s16[264,1024]{1,0:T(8,128)(2,1)S(1)}, u32[]{:S(2)}, u32[]{:S(2)}) collective-permute-start(s16[264,1024]{1,0:T(8,128)(2,1)S(1)} %get-tuple-element.74), channel_id=1, source_target_pairs={{0,6},{2,0},{4,2},{6,4},{1,7},{3,1},{5,3},{7,5},{8,14},{10,8},{12,... | collective-permute-start | bytes 1622024 | tf_op jit(solution)/shard_map/ppermute | solution.py:325
  39.0 15.2 %collective-permute-start.4 = (s16[264,1024]{1,0:T(8,128)(2,1)S(1)}, s16[264,1024]{1,0:T(8,128)(2,1)S(1)}, u32[]{:S(2)}, u32[]{:S(2)}) collective-permute-start(s16[264,1024]{1,0:T(8,128)(2,1)S(1)} %get-tuple-element.57), channel_id=1, source_target_pairs={{0,8},{8,16},{16,24},{24,0},{1,9},{9,17},{17,25},{25,1},{2,10},{10... | collective-permute-start | bytes 1622024 | tf_op jit(solution)/shard_map/ppermute | solution.py:325
  39.0 16.7 %collective-permute-start.5 = (s16[264,1024]{1,0:T(8,128)(2,1)S(1)}, s16[264,1024]{1,0:T(8,128)(2,1)S(1)}, u32[]{:S(2)}, u32[]{:S(2)}) collective-permute-start(s16[264,1024]{1,0:T(8,128)(2,1)S(1)} %get-tuple-element.58), channel_id=1, source_target_pairs={{0,24},{8,0},{16,8},{24,16},{1,25},{9,1},{17,9},{25,17},{2,26},{10... | collective-permute-start | bytes 1622024 | tf_op jit(solution)/shard_map/ppermute | solution.py:325
  49.4 13.9 %collective-permute-start.6 = (s16[264,1024]{1,0:T(8,128)(2,1)S(1)}, s16[264,1024]{1,0:T(8,128)(2,1)S(1)}, u32[]{:S(2)}, u32[]{:S(2)}) collective-permute-start(s16[264,1024]{1,0:T(8,128)(2,1)S(1)} %get-tuple-element.59), channel_id=1, source_target_pairs={{0,2},{2,4},{4,6},{6,0},{1,3},{3,5},{5,7},{7,1},{8,10},{10,12},{12... | collective-permute-start | bytes 1622024 | tf_op jit(solution)/shard_map/ppermute | solution.py:325
  49.8 14.8 %collective-permute-start.7 = (s16[264,1024]{1,0:T(8,128)(2,1)S(1)}, s16[264,1024]{1,0:T(8,128)(2,1)S(1)}, u32[]{:S(2)}, u32[]{:S(2)}) collective-permute-start(s16[264,1024]{1,0:T(8,128)(2,1)S(1)} %get-tuple-element.60), channel_id=1, source_target_pairs={{0,6},{2,0},{4,2},{6,4},{1,7},{3,1},{5,3},{7,5},{8,14},{10,8},{12,... | collective-permute-start | bytes 1622024 | tf_op jit(solution)/shard_map/ppermute | solution.py:325
  54.2 14.9 %collective-permute-start.12 = (s16[136,1024]{1,0:T(8,128)(2,1)S(1)}, s16[136,1024]{1,0:T(8,128)(2,1)S(1)}, u32[]{:S(2)}, u32[]{:S(2)}) collective-permute-start(s16[136,1024]{1,0:T(8,128)(2,1)S(1)} %get-tuple-element.65), channel_id=1, source_target_pairs={{0,8},{8,16},{16,24},{24,0},{1,9},{9,17},{17,25},{25,1},{2,10},{10... | collective-permute-start | bytes 835592 | tf_op jit(solution)/shard_map/ppermute | solution.py:325
  55.8 17.4 %collective-permute-start.14 = (s16[136,1024]{1,0:T(8,128)(2,1)S(1)}, s16[136,1024]{1,0:T(8,128)(2,1)S(1)}, u32[]{:S(2)}, u32[]{:S(2)}) collective-permute-start(s16[136,1024]{1,0:T(8,128)(2,1)S(1)} %get-tuple-element.68), channel_id=1, source_target_pairs={{0,8},{8,16},{16,24},{24,0},{1,9},{9,17},{17,25},{25,1},{2,10},{10... | collective-permute-start | bytes 835592 | tf_op jit(solution)/shard_map/ppermute | solution.py:325
  63.3 10.0 %collective-permute-start.15 = (s16[136,1024]{1,0:T(8,128)(2,1)S(1)}, s16[136,1024]{1,0:T(8,128)(2,1)S(1)}, u32[]{:S(2)}, u32[]{:S(2)}) collective-permute-start(s16[136,1024]{1,0:T(8,128)(2,1)S(1)} %get-tuple-element.69), channel_id=1, source_target_pairs={{0,24},{8,0},{16,8},{24,16},{1,25},{9,1},{17,9},{25,17},{2,26},{10... | collective-permute-start | bytes 835592 | tf_op jit(solution)/shard_map/ppermute | solution.py:325
  64.6 12.2 %collective-permute-start.13 = (s16[136,1024]{1,0:T(8,128)(2,1)S(1)}, s16[136,1024]{1,0:T(8,128)(2,1)S(1)}, u32[]{:S(2)}, u32[]{:S(2)}) collective-permute-start(s16[136,1024]{1,0:T(8,128)(2,1)S(1)} %get-tuple-element.66), channel_id=1, source_target_pairs={{0,24},{8,0},{16,8},{24,16},{1,25},{9,1},{17,9},{25,17},{2,26},{10... | collective-permute-start | bytes 835592 | tf_op jit(solution)/shard_map/ppermute | solution.py:325
  66.5 10.9 %collective-permute-start.23 = (s16[136,1024]{1,0:T(8,128)(2,1)S(1)}, s16[136,1024]{1,0:T(8,128)(2,1)S(1)}, u32[]{:S(2)}, u32[]{:S(2)}) collective-permute-start(s16[136,1024]{1,0:T(8,128)(2,1)S(1)} %get-tuple-element.78), channel_id=1, source_target_pairs={{0,2},{2,4},{4,6},{6,0},{1,3},{3,5},{5,7},{7,1},{8,10},{10,12},{12... | collective-permute-start | bytes 835592 | tf_op jit(solution)/shard_map/ppermute | solution.py:325
  69.1 8.9 %collective-permute-start.24 = (s16[136,1024]{1,0:T(8,128)(2,1)S(1)}, s16[136,1024]{1,0:T(8,128)(2,1)S(1)}, u32[]{:S(2)}, u32[]{:S(2)}) collective-permute-start(s16[136,1024]{1,0:T(8,128)(2,1)S(1)} %get-tuple-element.79), channel_id=1, source_target_pairs={{0,6},{2,0},{4,2},{6,4},{1,7},{3,1},{5,3},{7,5},{8,14},{10,8},{12,... | collective-permute-start | bytes 835592 | tf_op jit(solution)/shard_map/ppermute | solution.py:325
  73.2 7.7 %collective-permute-start.21 = (s16[136,1024]{1,0:T(8,128)(2,1)S(1)}, s16[136,1024]{1,0:T(8,128)(2,1)S(1)}, u32[]{:S(2)}, u32[]{:S(2)}) collective-permute-start(s16[136,1024]{1,0:T(8,128)(2,1)S(1)} %get-tuple-element.75), channel_id=1, source_target_pairs={{0,2},{2,4},{4,6},{6,0},{1,3},{3,5},{5,7},{7,1},{8,10},{10,12},{12... | collective-permute-start | bytes 835592 | tf_op jit(solution)/shard_map/ppermute | solution.py:325
  73.3 10.1 %collective-permute-start.22 = (s16[136,1024]{1,0:T(8,128)(2,1)S(1)}, s16[136,1024]{1,0:T(8,128)(2,1)S(1)}, u32[]{:S(2)}, u32[]{:S(2)}) collective-permute-start(s16[136,1024]{1,0:T(8,128)(2,1)S(1)} %get-tuple-element.76), channel_id=1, source_target_pairs={{0,6},{2,0},{4,2},{6,4},{1,7},{3,1},{5,3},{7,5},{8,14},{10,8},{12,... | collective-permute-start | bytes 835592 | tf_op jit(solution)/shard_map/ppermute | solution.py:325
  76.7 10.3 %collective-permute-start.16 = (s16[136,1024]{1,0:T(8,128)(2,1)S(1)}, s16[136,1024]{1,0:T(8,128)(2,1)S(1)}, u32[]{:S(2)}, u32[]{:S(2)}) collective-permute-start(s16[136,1024]{1,0:T(8,128)(2,1)S(1)} %get-tuple-element.70), channel_id=1, source_target_pairs={{0,4},{2,6},{4,0},{6,2},{1,5},{3,7},{5,1},{7,3},{8,12},{10,14},{12... | collective-permute-start | bytes 835592 | tf_op jit(solution)/shard_map/ppermute | solution.py:325
  77.4 15.7 %collective-permute-start.17 = (s16[136,1024]{1,0:T(8,128)(2,1)S(1)}, s16[136,1024]{1,0:T(8,128)(2,1)S(1)}, u32[]{:S(2)}, u32[]{:S(2)}) collective-permute-start(s16[136,1024]{1,0:T(8,128)(2,1)S(1)} %get-tuple-element.71), channel_id=1, source_target_pairs={{0,2},{2,4},{4,6},{6,0},{1,3},{3,5},{5,7},{7,1},{8,10},{10,12},{12... | collective-permute-start | bytes 835592 | tf_op jit(solution)/shard_map/ppermute | solution.py:325
  78.0 16.3 %collective-permute-start.18 = (s16[136,1024]{1,0:T(8,128)(2,1)S(1)}, s16[136,1024]{1,0:T(8,128)(2,1)S(1)}, u32[]{:S(2)}, u32[]{:S(2)}) collective-permute-start(s16[136,1024]{1,0:T(8,128)(2,1)S(1)} %get-tuple-element.72), channel_id=1, source_target_pairs={{0,6},{2,0},{4,2},{6,4},{1,7},{3,1},{5,3},{7,5},{8,14},{10,8},{12,... | collective-permute-start | bytes 835592 | tf_op jit(solution)/shard_map/ppermute | solution.py:325
  80.9 13.4 %collective-permute-start.25 = (s16[136,1024]{1,0:T(8,128)(2,1)S(1)}, s16[136,1024]{1,0:T(8,128)(2,1)S(1)}, u32[]{:S(2)}, u32[]{:S(2)}) collective-permute-start(s16[136,1024]{1,0:T(8,128)(2,1)S(1)} %get-tuple-element.80), channel_id=1, source_target_pairs={{0,16},{8,24},{16,0},{24,8},{1,17},{9,25},{17,1},{25,9},{2,18},{10... | collective-permute-start | bytes 835592 | tf_op jit(solution)/shard_map/ppermute | solution.py:325
  83.4 11.0 %collective-permute-start.26 = (s16[136,1024]{1,0:T(8,128)(2,1)S(1)}, s16[136,1024]{1,0:T(8,128)(2,1)S(1)}, u32[]{:S(2)}, u32[]{:S(2)}) collective-permute-start(s16[136,1024]{1,0:T(8,128)(2,1)S(1)} %get-tuple-element.81), channel_id=1, source_target_pairs={{0,8},{8,16},{16,24},{24,0},{1,9},{9,17},{17,25},{25,1},{2,10},{10... | collective-permute-start | bytes 835592 | tf_op jit(solution)/shard_map/ppermute | solution.py:325
  85.0 29.3 %copy-start.5 = (s32[1,256,1024]{2,1,0:T(8,128)S(1)}, s32[1,256,1024]{2,1,0:T(8,128)}, u32[]{:S(2)}) copy-start(s32[1,256,1024]{2,1,0:T(8,128)} %refs_0_.1) | copy-start | bytes 3145732
  85.0 29.3 %copy-start.6 = (s32[1,256,1024]{2,1,0:T(8,128)S(1)}, s32[1,256,1024]{2,1,0:T(8,128)}, u32[]{:S(2)}) copy-start(s32[1,256,1024]{2,1,0:T(8,128)} %refs_3_.1) | copy-start | bytes 3145732
  85.0 29.3 %copy-start.7 = (f32[1,1024]{1,0:T(1,128)S(1)}, f32[1,1024]{1,0:T(1,128)}, u32[]{:S(2)}) copy-start(f32[1,1024]{1,0:T(1,128)} %refs_2_.1) | copy-start | bytes 12292
  85.0 29.3 %copy-start.8 = (f32[1,1024]{1,0:T(1,128)S(1)}, f32[1,1024]{1,0:T(1,128)}, u32[]{:S(2)}) copy-start(f32[1,1024]{1,0:T(1,128)} %refs_5_.1) | copy-start | bytes 12292
  85.0 29.3 %copy-start.9 = (f32[1,256]{1,0:T(1,128)S(1)}, f32[1,256]{1,0:T(1,128)}, u32[]{:S(2)}) copy-start(f32[1,256]{1,0:T(1,128)} %refs_1_.1) | copy-start | bytes 3076
  85.1 29.3 %copy-start.10 = (f32[1,256]{1,0:T(1,128)S(1)}, f32[1,256]{1,0:T(1,128)}, u32[]{:S(2)}) copy-start(f32[1,256]{1,0:T(1,128)} %refs_4_.1) | copy-start | bytes 3076
  87.0 7.4 %collective-permute-start.27 = (s16[136,1024]{1,0:T(8,128)(2,1)S(1)}, s16[136,1024]{1,0:T(8,128)(2,1)S(1)}, u32[]{:S(2)}, u32[]{:S(2)}) collective-permute-start(s16[136,1024]{1,0:T(8,128)(2,1)S(1)} %get-tuple-element.82), channel_id=1, source_target_pairs={{0,24},{8,0},{16,8},{24,16},{1,25},{9,1},{17,9},{25,17},{2,26},{10... | collective-permute-start | bytes 835592 | tf_op jit(solution)/shard_map/ppermute | solution.py:325
  96.0 27.6 %all-to-all-start = ((f32[128,1,128]{2,1,0:T(1,128)}), f32[128,1,128]{2,1,0:T(1,128)S(1)}, u32[]{:S(2)}, u32[]{:S(2)}) async-start(f32[128,1,128]{2,1,0:T(1,128)} %bitcast.5), calls=%async_computation | async-start | bytes 131072 | tf_op jit(solution)/shard_map/all_to_all | solution.py:488
  114.8 1.0 copy-start.1
  115.7 1.0 copy-start.3
  123.6 1.2 copy-start.2
  124.8 1.2 copy-start.4
  127.3 13.8 %all-to-all-start.1 = ((f32[32,16,128]{2,1,0:T(8,128)}), f32[32,16,128]{2,1,0:T(8,128)S(1)}, u32[]{:S(2)}, u32[]{:S(2)}) async-start(f32[32,16,128]{2,1,0:T(8,128)} %get-tuple-element.90), calls=%async_computation.1 | async-start | bytes 524288 | tf_op jit(solution)/shard_map/all_to_all | solution.py:488

commit v5 on v4

--- a/solution.py
+++ b/solution.py
@@ -83,6 +83,10 @@
     return pltpu.with_memory_space_constraint(value, VMEM)
 
 
+def position():
+    return [lax.axis_index(a) for a in FSDP]
+
+
 def block_at(where, job, i):
     half, delta, low = job
     j = lax.rem(where[1 - half] + ORDER[low + i], RING)
@@ -90,8 +94,9 @@
     return far * RING + j if half == 0 else j * RING + far
 
 
-def gather_body(wanted, where, parts, *refs):
+def gather_body(wanted, parts, *refs):
     outs, sem = refs[:-1], refs[-1]
+    where = position()
     copies = []
     for (jobs, mine), out in zip(wanted, outs):
         core = where[2] if mine else 1 - where[2]
@@ -105,7 +110,7 @@
         copy.wait()
 
 
-def gather(where, parts, wanted):
+def gather(parts, wanted):
     rows, cols = parts.shape[3:]
     size = 2 * rows * cols * sum(len(jobs) for jobs, _ in wanted)
     return call(
@@ -114,8 +119,8 @@
         [pltpu.SemaphoreType.DMA((2 * sum(len(jobs) for jobs, _ in wanted),))],
         size,
         4 * size,
-        [pl.BlockSpec(memory_space=pltpu.SMEM), pl.BlockSpec(memory_space=pltpu.HBM)],
-    )(where, pltpu.with_memory_space_constraint(parts, pltpu.HBM))
+        [pl.BlockSpec(memory_space=pltpu.HBM)],
+    )(pltpu.with_memory_space_constraint(parts, pltpu.HBM))
 
 
 def chunks(rows, step, carry):
@@ -147,7 +152,8 @@
 
 
 def pair_body(messages, first, relays, sends, *refs):
-    (where, parts, came), refs = refs[:3], refs[3:]
+    (parts, came), refs = refs[:2], refs[2:]
+    where = position()
     relayed, refs = refs[:relays], refs[relays:]
     outs, total = refs[: len(messages)], refs[-1]
     rows, cols = came.shape[2:]
@@ -177,7 +183,7 @@
     send_blocks(total, outs, peaks, rows, len(messages[0]))
 
 
-def pair(where, parts, came, messages, first=False, relayed=(), sends=()):
+def pair(parts, came, messages, first=False, relayed=(), sends=()):
     rows, cols = came.shape[2:]
     each, n = len(messages[0]), len(messages)
     got = call(
@@ -187,8 +193,8 @@
         [VMEM((each * n, rows, cols), F32)],
         50 * each * n * rows * cols,
         6 * each * n * rows * cols,
-        [pl.BlockSpec(memory_space=pltpu.SMEM), *in_vmem(2 + len(relayed))],
-    )(where, parts, held(came), *[held(r) for r in relayed])
+        in_vmem(2 + len(relayed)),
+    )(parts, held(came), *[held(r) for r in relayed])
     return got[:n], got[n:]
 
 
@@ -202,8 +208,9 @@
     return jnp.transpose(jnp.broadcast_to(column, (n, 128)))[0:1, :]
 
 
-def keep_body(jobs, where, parts, came, *refs):
+def keep_body(jobs, parts, came, *refs):
     got, total = refs[:4], refs[4]
+    where = position()
     rows = came.shape[2]
     for half in range(2):
         for i in range(RING):
@@ -219,7 +226,7 @@
             chunks(rows, step, None)
 
 
-def keep(where, parts, came, jobs, got):
+def keep(parts, came, jobs, got):
     rows, cols = came.shape[2:]
     return call(
         functools.partial(keep_body, jobs),
@@ -227,8 +234,8 @@
         [],
         200 * rows * cols,
         80 * rows * cols,
-        [pl.BlockSpec(memory_space=pltpu.SMEM), *in_vmem(6)],
-    )(where, parts, held(came), *[held(g) for g in got])[0]
+        in_vmem(6),
+    )(parts, held(came), *[held(g) for g in got])[0]
 
 
 def old_body(*refs):
@@ -317,7 +324,6 @@
 
 
 def reduce_scatter(parts, devices):
-    where = jnp.stack([lax.axis_index(a) for a in FSDP]).astype(jnp.int32)
     resident = held(parts)
     axis = ("y", "z")
 
@@ -328,7 +334,7 @@
         return lax.ppermute(value, "core", [(0, 1), (1, 0)])
 
     def stage(half, messages, came, source=resident, first=False, relayed=(), sends=()):
-        sent, more = pair(where, source, came, messages, first, relayed, sends)
+        sent, more = pair(source, came, messages, first, relayed, sends)
         got = []
         for value, delta in zip(sent, (1, 3)):
             got.append(hop(value, axis[half], delta))
@@ -342,9 +348,9 @@
 
     far, near = jobs_of((2, 0), (2, 2)), jobs_of((1, 2), (3, 0))
     join, mine = jobs_of((1, 0), (3, 2)), jobs_of((0, 0), (0, 2))
-    (out,) = gather(where, parts, ((far[0], False),))
+    (out,) = gather(parts, ((far[0], False),))
     came_far_0 = swap(out)
-    out, own_far_0 = gather(where, parts, ((far[1], False), (far[0], True)))
+    out, own_far_0 = gather(parts, ((far[1], False), (far[0], True)))
     came_far_1 = swap(out)
     far_0, _ = stage(0, blocks_of(far[0]), came_far_0, own_far_0, True)
     far_1, out = stage(1, blocks_of(far[1]), came_far_1, sends=near)
@@ -358,7 +364,7 @@
         for half, relayed in enumerate((far_0, far_1)):
             messages = blocks_of(join[half], 2 * half, (only,))
             joined[only, half], _ = stage(half, messages, came_join, relayed=relayed)
-    acc = keep(where, resident, came_mine, mine[0] + mine[1], (*near_0, *near_1))
+    acc = keep(resident, came_mine, mine[0] + mine[1], (*near_0, *near_1))
     halves = []
     for half in range(2):
         near_out, far_out = middle(acc, joined[0, half], half, (0, 2), 2)

time: 143 us -> 146 us (1.021)
  Pallas kernels: 29.1 us -> 23.1 us
  waiting for transfers between devices: 51 us -> 55 us
  local copies, waits for them, and re-layouts: 4.73 us -> 7.82 us
    pallas_call x8, Pallas kernels: 12.9 us -> 8.49 us  [pair(): call(functools.partial(pair_body, messages, first, len(relayed), sends),...]
    unnamed x30, local copies, waits for them, and re-layouts: 4.73 us -> 7.82 us
    ppermute x6, waiting for transfers between devices: 2.3 us -> 4.49 us  [swap(): return lax.ppermute(value, 'core', [(0, 1), (1, 0)])]
    ppermute x22, waiting for transfers between devices: 34.1 us -> 35.9 us  [hop(): lax.ppermute(value, name, [(i, (i + delta) % RING) for i in range(RING)])]
    all_to_all x2, starting transfers between devices: 23 us -> 24.8 us  [exchange(): return lax.all_to_all(value, axes, split_axis=0, concat_axis=0, tiled=True)]
  transfers between devices with their start and end apart: 30 -> 30, of which waited for: 10 -> 13; matrix products, arithmetic and copies ran while one was open for 0% -> 0% of each run, Pallas kernels for 14% -> 11%
where the time goes in v5:
time: 146 us; the launch traced here: 145 us
  starting transfers between devices  58.3 us (40%)
  waiting for transfers between devices  55 us (38%)
  Pallas kernels  23.1 us (16%)
  local copies, waits for them, and re-layouts  7.82 us (5%)
    ppermute x22, waiting for transfers between devices, hop(): lax.ppermute(value, name, [(i, (i + delta) % RING) for i in range(RING)])  35.9 us
    ppermute x22, starting transfers between devices, hop(): lax.ppermute(value, name, [(i, (i + delta) % RING) for i in range(RING)])  29.4 us
    all_to_all x2, starting transfers between devices, exchange(): return lax.all_to_all(value, axes, split_axis=0, concat_axis=0, tiled=True)  24.8 us
    all_to_all x2, waiting for transfers between devices, exchange(): return lax.all_to_all(value, axes, split_axis=0, concat_axis=0, tiled=True)  14.6 us
    pallas_call x8, Pallas kernels, pair(): call(functools.partial(pair_body, messages, first, len(relayed), sends),...  8.49 us
    unnamed x30, local copies, waits for them, and re-layouts  7.82 us
    ppermute x6, waiting for transfers between devices, swap(): return lax.ppermute(value, 'core', [(0, 1), (1, 0)])  4.49 us
    ppermute x6, starting transfers between devices, swap(): return lax.ppermute(value, 'core', [(0, 1), (1, 0)])  4.05 us
  transfers between devices with their start and end apart: 30, of which 13 were waited for; matrix products, arithmetic and copies ran while one was open for 0% of the time, Pallas kernels for 11%

profile of v5, /device:TPU:1, one launch (start us, length us, event | category | flops | bytes accessed | tf_op | source)
XLA Modules:
  0.0 145.3 jit_solution(6505619252097291740)
XLA Ops:
  0.6 1.7 %shard_map.126 = (bf16[2,2,128,1024]{3,2,1,0:T(8,128)(2,1)S(1)}, bf16[2,2,128,1024]{3,2,1,0:T(8,128)(2,1)S(1)}) custom-call(bf16[16,2,2,128,1024]{4,3,2,1,0:T(8,128)(2,1)} %bitcast.5), custom_call_target="tpu_custom_call" | custom-call | flops 1048576 | bytes 4194304 | tf_op jit(solution)/shard_map/pallas_call | solution.py:116
  2.4 1.5 %collective-permute-start = (bf16[2,2,128,1024]{3,2,1,0:T(8,128)(2,1)S(1)}, bf16[2,2,128,1024]{3,2,1,0:T(8,128)(2,1)S(1)}, u32[]{:S(2)}, u32[]{:S(2)}) collective-permute-start(bf16[2,2,128,1024]{3,2,1,0:T(8,128)(2,1)S(1)} %get-tuple-element.53), channel_id=1, source_target_pairs={{0,1},{1,0},{2,3},{3,2},{4,5},{5,4},{6,7},{7,6},{8,9},{9,8},{10,11... | collective-permute-start | bytes 3145736 | tf_op jit(solution)/shard_map/ppermute | solution.py:334
  3.9 2.3 %collective-permute-done.refs_1_ = bf16[2,2,128,1024]{3,2,1,0:T(8,128)(2,1)S(1)} collective-permute-done((bf16[2,2,128,1024]{3,2,1,0:T(8,128)(2,1)S(1)}, bf16[2,2,128,1024]{3,2,1,0:T(8,128)(2,1)S(1)}, u32[]{:S(2)}, u32[]{:S(2)}) %collective-permute-start) | collective-permute-done | bytes 1048608 | tf_op jit(solution)/shard_map/ppermute | solution.py:334
  6.1 0.9 copy-done
  7.0 1.3 shard_map.127
  8.3 1.5 %collective-permute-start.3 = (bf16[2,2,128,1024]{3,2,1,0:T(8,128)(2,1)S(1)}, bf16[2,2,128,1024]{3,2,1,0:T(8,128)(2,1)S(1)}, u32[]{:S(2)}, u32[]{:S(2)}) collective-permute-start(bf16[2,2,128,1024]{3,2,1,0:T(8,128)(2,1)S(1)} %get-tuple-element.56), channel_id=1, source_target_pairs={{0,1},{1,0},{2,3},{3,2},{4,5},{5,4},{6,7},{7,6},{8,9},{9,8},{10,11... | collective-permute-start | bytes 3145736 | tf_op jit(solution)/shard_map/ppermute | solution.py:334
  9.9 2.2 %collective-permute-done.3.refs_1_ = bf16[2,2,128,1024]{3,2,1,0:T(8,128)(2,1)S(1)} collective-permute-done((bf16[2,2,128,1024]{3,2,1,0:T(8,128)(2,1)S(1)}, bf16[2,2,128,1024]{3,2,1,0:T(8,128)(2,1)S(1)}, u32[]{:S(2)}, u32[]{:S(2)}) %collective-permute-start.3) | collective-permute-done | bytes 1048608 | tf_op jit(solution)/shard_map/ppermute | solution.py:334
  12.1 1.3 shard_map.129
  13.8 2.0 %shard_map.131 = bf16[2,2,128,1024]{3,2,1,0:T(8,128)(2,1)S(1)} custom-call(bf16[16,2,2,128,1024]{4,3,2,1,0:T(8,128)(2,1)} %bitcast.6), custom_call_target="tpu_custom_call" | custom-call | flops 524288 | bytes 2097152 | tf_op jit(solution)/shard_map/pallas_call | solution.py:116
  15.9 1.3 slice-done.2
  17.2 1.2 slice-done.3
  18.4 1.3 shard_map.128
  20.2 1.7 %collective-permute-start.19 = (s16[264,1024]{1,0:T(8,128)(2,1)S(1)}, s16[264,1024]{1,0:T(8,128)(2,1)S(1)}, u32[]{:S(2)}, u32[]{:S(2)}) collective-permute-start(s16[264,1024]{1,0:T(8,128)(2,1)S(1)} %get-tuple-element.73), channel_id=1, source_target_pairs={{0,2},{2,4},{4,6},{6,0},{1,3},{3,5},{5,7},{7,1},{8,10},{10,12},{12... | collective-permute-start | bytes 1622024 | tf_op jit(solution)/shard_map/ppermute | solution.py:331
  21.9 2.1 %collective-permute-start.20 = (s16[264,1024]{1,0:T(8,128)(2,1)S(1)}, s16[264,1024]{1,0:T(8,128)(2,1)S(1)}, u32[]{:S(2)}, u32[]{:S(2)}) collective-permute-start(s16[264,1024]{1,0:T(8,128)(2,1)S(1)} %get-tuple-element.74), channel_id=1, source_target_pairs={{0,6},{2,0},{4,2},{6,4},{1,7},{3,1},{5,3},{7,5},{8,14},{10,8},{12,... | collective-permute-start | bytes 1622024 | tf_op jit(solution)/shard_map/ppermute | solution.py:331
  24.0 1.1 shard_map.132
  25.2 1.4 collective-permute-start.10
  26.5 10.0 %collective-permute-done.19.refs_2_ = s16[264,1024]{1,0:T(8,128)(2,1)S(1)} collective-permute-done((s16[264,1024]{1,0:T(8,128)(2,1)S(1)}, s16[264,1024]{1,0:T(8,128)(2,1)S(1)}, u32[]{:S(2)}, u32[]{:S(2)}) %collective-permute-start.19) | collective-permute-done | bytes 540704 | tf_op jit(solution)/shard_map/ppermute | solution.py:331
  36.5 2.7 %collective-permute-start.11 = (s16[264,1024]{1,0:T(8,128)(2,1)S(1)}, s16[264,1024]{1,0:T(8,128)(2,1)S(1)}, u32[]{:S(2)}, u32[]{:S(2)}) collective-permute-start(s16[264,1024]{1,0:T(8,128)(2,1)S(1)} %get-tuple-element.64), channel_id=1, source_target_pairs={{0,24},{8,0},{16,8},{24,16},{1,25},{9,1},{17,9},{25,17},{2,26},{10... | collective-permute-start | bytes 1622024 | tf_op jit(solution)/shard_map/ppermute | solution.py:331
  40.0 2.0 %collective-permute-start.5 = (s16[264,1024]{1,0:T(8,128)(2,1)S(1)}, s16[264,1024]{1,0:T(8,128)(2,1)S(1)}, u32[]{:S(2)}, u32[]{:S(2)}) collective-permute-start(s16[264,1024]{1,0:T(8,128)(2,1)S(1)} %get-tuple-element.58), channel_id=1, source_target_pairs={{0,24},{8,0},{16,8},{24,16},{1,25},{9,1},{17,9},{25,17},{2,26},{10... | collective-permute-start | bytes 1622024 | tf_op jit(solution)/shard_map/ppermute | solution.py:331
  42.0 8.2 %collective-permute-done.11.refs_3_ = s16[264,1024]{1,0:T(8,128)(2,1)S(1)} collective-permute-done((s16[264,1024]{1,0:T(8,128)(2,1)S(1)}, s16[264,1024]{1,0:T(8,128)(2,1)S(1)}, u32[]{:S(2)}, u32[]{:S(2)}) %collective-permute-start.11) | collective-permute-done | bytes 540704 | tf_op jit(solution)/shard_map/ppermute | solution.py:331
  50.2 2.7 %collective-permute-start.7 = (s16[264,1024]{1,0:T(8,128)(2,1)S(1)}, s16[264,1024]{1,0:T(8,128)(2,1)S(1)}, u32[]{:S(2)}, u32[]{:S(2)}) collective-permute-start(s16[264,1024]{1,0:T(8,128)(2,1)S(1)} %get-tuple-element.60), channel_id=1, source_target_pairs={{0,6},{2,0},{4,2},{6,4},{1,7},{3,1},{5,3},{7,5},{8,14},{10,8},{12,... | collective-permute-start | bytes 1622024 | tf_op jit(solution)/shard_map/ppermute | solution.py:331
  52.9 0.9 shard_map.139
  53.9 0.9 shard_map.137
  54.8 7.0 %collective-permute-done.5.refs_1_ = s16[264,1024]{1,0:T(8,128)(2,1)S(1)} collective-permute-done((s16[264,1024]{1,0:T(8,128)(2,1)S(1)}, s16[264,1024]{1,0:T(8,128)(2,1)S(1)}, u32[]{:S(2)}, u32[]{:S(2)}) %collective-permute-start.5) | collective-permute-done | bytes 540704 | tf_op jit(solution)/shard_map/ppermute | solution.py:331
  61.8 0.9 collective-permute-start.24
  63.3 2.1 %collective-permute-start.22 = (s16[136,1024]{1,0:T(8,128)(2,1)S(1)}, s16[136,1024]{1,0:T(8,128)(2,1)S(1)}, u32[]{:S(2)}, u32[]{:S(2)}) collective-permute-start(s16[136,1024]{1,0:T(8,128)(2,1)S(1)} %get-tuple-element.76), channel_id=1, source_target_pairs={{0,6},{2,0},{4,2},{6,4},{1,7},{3,1},{5,3},{7,5},{8,14},{10,8},{12,... | collective-permute-start | bytes 835592 | tf_op jit(solution)/shard_map/ppermute | solution.py:331
  66.3 1.0 collective-permute-start.14
  67.3 1.7 %shard_map.130.acc = f32[2,4,128,1024]{3,2,1,0:T(8,128)S(1)} custom-call(bf16[16,2,2,128,1024]{4,3,2,1,0:T(8,128)(2,1)S(1)} %bitcast.15, bf16[4,2,128,1024]{3,2,1,0:T(8,128)(2,1)S(1)} %collective-permute-done.2.came, s16[264,1024]{1,0:T(8,128)(2,1)S(1)} %collective-permute-done.4.refs_0_, s16[264,1024]{1,0:T(8,128)(2,1)S(1)} %collective-permute-done.5.refs_1_, ...), custom_call_target="tpu_custom_call" | custom-call | flops 26214400 | bytes 10485760 | tf_op jit(solution)/shard_map/pallas_call | solution.py:231
  69.0 2.9 %collective-permute-start.15 = (s16[136,1024]{1,0:T(8,128)(2,1)S(1)}, s16[136,1024]{1,0:T(8,128)(2,1)S(1)}, u32[]{:S(2)}, u32[]{:S(2)}) collective-permute-start(s16[136,1024]{1,0:T(8,128)(2,1)S(1)} %get-tuple-element.69), channel_id=1, source_target_pairs={{0,24},{8,0},{16,8},{24,16},{1,25},{9,1},{17,9},{25,17},{2,26},{10... | collective-permute-start | bytes 835592 | tf_op jit(solution)/shard_map/ppermute | solution.py:331
  72.9 1.6 %collective-permute-done.21.first = s16[136,1024]{1,0:T(8,128)(2,1)S(1)} collective-permute-done((s16[136,1024]{1,0:T(8,128)(2,1)S(1)}, s16[136,1024]{1,0:T(8,128)(2,1)S(1)}, u32[]{:S(2)}, u32[]{:S(2)}) %collective-permute-start.21) | collective-permute-done | bytes 278560 | tf_op jit(solution)/shard_map/ppermute | solution.py:331
  74.4 3.4 %collective-permute-start.13 = (s16[136,1024]{1,0:T(8,128)(2,1)S(1)}, s16[136,1024]{1,0:T(8,128)(2,1)S(1)}, u32[]{:S(2)}, u32[]{:S(2)}) collective-permute-start(s16[136,1024]{1,0:T(8,128)(2,1)S(1)} %get-tuple-element.66), channel_id=1, source_target_pairs={{0,24},{8,0},{16,8},{24,16},{1,25},{9,1},{17,9},{25,17},{2,26},{10... | collective-permute-start | bytes 835592 | tf_op jit(solution)/shard_map/ppermute | solution.py:331
  79.9 2.1 %collective-permute-start.27 = (s16[136,1024]{1,0:T(8,128)(2,1)S(1)}, s16[136,1024]{1,0:T(8,128)(2,1)S(1)}, u32[]{:S(2)}, u32[]{:S(2)}) collective-permute-start(s16[136,1024]{1,0:T(8,128)(2,1)S(1)} %get-tuple-element.82), channel_id=1, source_target_pairs={{0,24},{8,0},{16,8},{24,16},{1,25},{9,1},{17,9},{25,17},{2,26},{10... | collective-permute-start | bytes 835592 | tf_op jit(solution)/shard_map/ppermute | solution.py:331
  83.4 2.4 %collective-permute-done.13.second = s16[136,1024]{1,0:T(8,128)(2,1)S(1)} collective-permute-done((s16[136,1024]{1,0:T(8,128)(2,1)S(1)}, s16[136,1024]{1,0:T(8,128)(2,1)S(1)}, u32[]{:S(2)}, u32[]{:S(2)}) %collective-permute-start.13) | collective-permute-done | bytes 278560 | tf_op jit(solution)/shard_map/ppermute | solution.py:331
  86.8 2.4 %collective-permute-start.18 = (s16[136,1024]{1,0:T(8,128)(2,1)S(1)}, s16[136,1024]{1,0:T(8,128)(2,1)S(1)}, u32[]{:S(2)}, u32[]{:S(2)}) collective-permute-start(s16[136,1024]{1,0:T(8,128)(2,1)S(1)} %get-tuple-element.72), channel_id=1, source_target_pairs={{0,6},{2,0},{4,2},{6,4},{1,7},{3,1},{5,3},{7,5},{8,14},{10,8},{12,... | collective-permute-start | bytes 835592 | tf_op jit(solution)/shard_map/ppermute | solution.py:331
  89.2 3.7 %collective-permute-done.26.refs_6_ = s16[136,1024]{1,0:T(8,128)(2,1)S(1)} collective-permute-done((s16[136,1024]{1,0:T(8,128)(2,1)S(1)}, s16[136,1024]{1,0:T(8,128)(2,1)S(1)}, u32[]{:S(2)}, u32[]{:S(2)}) %collective-permute-start.26) | collective-permute-done | bytes 278560 | tf_op jit(solution)/shard_map/ppermute | solution.py:331
  92.9 1.9 %collective-permute-done.27.refs_7_ = s16[136,1024]{1,0:T(8,128)(2,1)S(1)} collective-permute-done((s16[136,1024]{1,0:T(8,128)(2,1)S(1)}, s16[136,1024]{1,0:T(8,128)(2,1)S(1)}, u32[]{:S(2)}, u32[]{:S(2)}) %collective-permute-start.27) | collective-permute-done | bytes 278560 | tf_op jit(solution)/shard_map/ppermute | solution.py:331
  94.8 1.6 %shard_map.141 = (f32[256,1024]{1,0:T(8,128)S(1)}, f32[128,128]{1,0:T(8,128)}) custom-call(f32[128,1024]{1,0:T(8,128)S(1)} %get-tuple-element.67.refs_0_, s16[136,1024]{1,0:T(8,128)(2,1)S(1)} %collective-permute-done.16.refs_1_, s16[136,1024]{1,0:T(8,128)(2,1)S(1)} %collective-permute-done.17.refs_2_, s16[136,1024]{1,0:T(8,128)(2,1)S(1)} %collective-permute-done.18.refs_3_, ...), custom_call_target="tpu_custom_call" | custom-call | flops 13107200 | bytes 4194304 | tf_op jit(solution)/shard_map/pallas_call | solution.py:316
  96.4 20.0 %all-to-all-start = ((f32[128,1,128]{2,1,0:T(1,128)}), f32[128,1,128]{2,1,0:T(1,128)S(1)}, u32[]{:S(2)}, u32[]{:S(2)}) async-start(f32[128,1,128]{2,1,0:T(1,128)} %bitcast.2), calls=%async_computation | async-start | bytes 131072 | tf_op jit(solution)/shard_map/all_to_all | solution.py:494
  116.9 1.0 copy-done.1
  117.9 1.0 copy-done.3
  118.9 6.9 %all-to-all-done = f32[128,1,128]{2,1,0:T(1,128)S(1)} async-done(((f32[128,1,128]{2,1,0:T(1,128)}), f32[128,1,128]{2,1,0:T(1,128)S(1)}, u32[]{:S(2)}, u32[]{:S(2)}) %all-to-all-start) | async-done | bytes 65568 | tf_op jit(solution)/shard_map/all_to_all | solution.py:494
  125.8 1.2 copy-done.2
  127.0 1.2 copy-done.4
  128.2 1.2 shard_map.143
  129.5 4.7 %all-to-all-start.1 = ((f32[32,16,128]{2,1,0:T(8,128)}), f32[32,16,128]{2,1,0:T(8,128)S(1)}, u32[]{:S(2)}, u32[]{:S(2)}) async-start(f32[32,16,128]{2,1,0:T(8,128)} %get-tuple-element.90), calls=%async_computation.1 | async-start | bytes 524288 | tf_op jit(solution)/shard_map/all_to_all | solution.py:494
  134.2 1.3 row_outputs.1
  135.6 7.7 %all-to-all-done.1.peaks = f32[32,16,128]{2,1,0:T(8,128)S(1)} async-done(((f32[32,16,128]{2,1,0:T(8,128)}), f32[32,16,128]{2,1,0:T(8,128)S(1)}, u32[]{:S(2)}, u32[]{:S(2)}) %all-to-all-start.1) | async-done | bytes 262176 | tf_op jit(solution)/shard_map/all_to_all | solution.py:494
  143.3 2.0 %scaled_outputs.1 = (f32[1,256,1024]{2,1,0:T(8,128)}, f32[1,256,1024]{2,1,0:T(8,128)}, f32[1,1024]{1,0:T(1,128)}, f32[1,1024]{1,0:T(1,128)}) custom-call(f32[32,16,128]{2,1,0:T(8,128)S(1)} %all-to-all-done.1.peaks, f32[256,1024]{1,0:T(8,128)S(1)} %get-tuple-element.87.first_new, f32[256,1024]{1,0:T(8,128)S(1)} %get-tuple-element.88.second_new, ...), custom_call_target="tpu_custom_call" | custom-call | flops 2097152 | bytes 4194304 | tf_op jit(solution)/shard_map/scaled_outputs/pallas_call | solution.py:480
  (63 shorter events, 9.1 us)
Async XLA Ops:
  0.6 6.4 %copy-start = (bf16[1,1,8192,1024]{3,2,1,0:T(8,128)(2,1)S(1)}, bf16[1,1,8192,1024]{3,2,1,0:T(8,128)(2,1)}, u32[]{:S(2)}) copy-start(bf16[1,1,8192,1024]{3,2,1,0:T(8,128)(2,1)} %param.7) | copy-start | bytes 50331652
  2.4 3.7 %collective-permute-start = (bf16[2,2,128,1024]{3,2,1,0:T(8,128)(2,1)S(1)}, bf16[2,2,128,1024]{3,2,1,0:T(8,128)(2,1)S(1)}, u32[]{:S(2)}, u32[]{:S(2)}) collective-permute-start(bf16[2,2,128,1024]{3,2,1,0:T(8,128)(2,1)S(1)} %get-tuple-element.53), channel_id=1, source_target_pairs={{0,1},{1,0},{2,3},{3,2},{4,5},{5,4},{6,7},{7,6},{8,9},{9,8},{10,11... | collective-permute-start | bytes 3145736 | tf_op jit(solution)/shard_map/ppermute | solution.py:334
  8.3 3.7 %collective-permute-start.3 = (bf16[2,2,128,1024]{3,2,1,0:T(8,128)(2,1)S(1)}, bf16[2,2,128,1024]{3,2,1,0:T(8,128)(2,1)S(1)}, u32[]{:S(2)}, u32[]{:S(2)}) collective-permute-start(bf16[2,2,128,1024]{3,2,1,0:T(8,128)(2,1)S(1)} %get-tuple-element.56), channel_id=1, source_target_pairs={{0,1},{1,0},{2,3},{3,2},{4,5},{5,4},{6,7},{7,6},{8,9},{9,8},{10,11... | collective-permute-start | bytes 3145736 | tf_op jit(solution)/shard_map/ppermute | solution.py:334
  9.8 6.2 %collective-permute-start.1 = (bf16[2,2,128,1024]{3,2,1,0:T(8,128)(2,1)S(1)}, bf16[2,2,128,1024]{3,2,1,0:T(8,128)(2,1)S(1)}, u32[]{:S(2)}, u32[]{:S(2)}) collective-permute-start(bf16[2,2,128,1024]{3,2,1,0:T(8,128)(2,1)S(1)} %get-tuple-element.54), channel_id=1, source_target_pairs={{0,1},{1,0},{2,3},{3,2},{4,5},{5,4},{6,7},{7,6},{8,9},{9,8},{10,11... | collective-permute-start | bytes 3145736 | tf_op jit(solution)/shard_map/ppermute | solution.py:334
  12.1 3.9 %slice-start = ((s8[16777216]{0:T(1024)(128)(4,1)}), s8[4194304]{0:T(1024)(128)(4,1)S(1)}, s32[]{:S(2)}) async-start(s8[16777216]{0:T(1024)(128)(4,1)} %bitcast.9), calls=%async_computation.2 | async-start | bytes 8388608
  12.1 3.9 %slice-start.1 = ((s8[16777216]{0:T(1024)(128)(4,1)}), s8[4194304]{0:T(1024)(128)(4,1)S(1)}, s32[]{:S(2)}) async-start(s8[16777216]{0:T(1024)(128)(4,1)} %bitcast.9), calls=%async_computation.3 | async-start | bytes 8388608
  13.3 3.9 %slice-start.2 = ((s8[16777216]{0:T(1024)(128)(4,1)}), s8[4194304]{0:T(1024)(128)(4,1)S(1)}, s32[]{:S(2)}) async-start(s8[16777216]{0:T(1024)(128)(4,1)} %bitcast.9), calls=%async_computation.4 | async-start | bytes 8388608
  13.3 5.1 %slice-start.3 = ((s8[16777216]{0:T(1024)(128)(4,1)}), s8[4194304]{0:T(1024)(128)(4,1)S(1)}, s32[]{:S(2)}) async-start(s8[16777216]{0:T(1024)(128)(4,1)} %bitcast.9), calls=%async_computation.5 | async-start | bytes 8388608
  13.4 36.8 %collective-permute-start.8 = (bf16[4,2,128,1024]{3,2,1,0:T(8,128)(2,1)S(1)}, bf16[4,2,128,1024]{3,2,1,0:T(8,128)(2,1)S(1)}, u32[]{:S(2)}, u32[]{:S(2)}) collective-permute-start(bf16[4,2,128,1024]{3,2,1,0:T(8,128)(2,1)S(1)} %get-tuple-element.61), channel_id=1, source_target_pairs={{0,1},{1,0},{2,3},{3,2},{4,5},{5,4},{6,7},{7,6},{8,9},{9,8},{10,11... | collective-permute-start | bytes 6291464 | tf_op jit(solution)/shard_map/ppermute | solution.py:334
  15.8 8.2 %collective-permute-start.9 = (bf16[2,2,128,1024]{3,2,1,0:T(8,128)(2,1)S(1)}, bf16[2,2,128,1024]{3,2,1,0:T(8,128)(2,1)S(1)}, u32[]{:S(2)}, u32[]{:S(2)}) collective-permute-start(bf16[2,2,128,1024]{3,2,1,0:T(8,128)(2,1)S(1)} %shard_map.131), channel_id=1, source_target_pairs={{0,1},{1,0},{2,3},{3,2},{4,5},{5,4},{6,7},{7,6},{8,9},{9,8},{10,11... | collective-permute-start | bytes 3145736 | tf_op jit(solution)/shard_map/ppermute | solution.py:334
  19.7 46.6 %collective-permute-start.2 = (bf16[4,2,128,1024]{3,2,1,0:T(8,128)(2,1)S(1)}, bf16[4,2,128,1024]{3,2,1,0:T(8,128)(2,1)S(1)}, u32[]{:S(2)}, u32[]{:S(2)}) collective-permute-start(bf16[4,2,128,1024]{3,2,1,0:T(8,128)(2,1)S(1)} %get-tuple-element.55), channel_id=1, source_target_pairs={{0,1},{1,0},{2,3},{3,2},{4,5},{5,4},{6,7},{7,6},{8,9},{9,8},{10,11... | collective-permute-start | bytes 6291464 | tf_op jit(solution)/shard_map/ppermute | solution.py:334
  20.2 16.4 %collective-permute-start.19 = (s16[264,1024]{1,0:T(8,128)(2,1)S(1)}, s16[264,1024]{1,0:T(8,128)(2,1)S(1)}, u32[]{:S(2)}, u32[]{:S(2)}) collective-permute-start(s16[264,1024]{1,0:T(8,128)(2,1)S(1)} %get-tuple-element.73), channel_id=1, source_target_pairs={{0,2},{2,4},{4,6},{6,0},{1,3},{3,5},{5,7},{7,1},{8,10},{10,12},{12... | collective-permute-start | bytes 1622024 | tf_op jit(solution)/shard_map/ppermute | solution.py:331
  21.9 17.4 %collective-permute-start.20 = (s16[264,1024]{1,0:T(8,128)(2,1)S(1)}, s16[264,1024]{1,0:T(8,128)(2,1)S(1)}, u32[]{:S(2)}, u32[]{:S(2)}) collective-permute-start(s16[264,1024]{1,0:T(8,128)(2,1)S(1)} %get-tuple-element.74), channel_id=1, source_target_pairs={{0,6},{2,0},{4,2},{6,4},{1,7},{3,1},{5,3},{7,5},{8,14},{10,8},{12,... | collective-permute-start | bytes 1622024 | tf_op jit(solution)/shard_map/ppermute | solution.py:331
  25.2 14.8 %collective-permute-start.10 = (s16[264,1024]{1,0:T(8,128)(2,1)S(1)}, s16[264,1024]{1,0:T(8,128)(2,1)S(1)}, u32[]{:S(2)}, u32[]{:S(2)}) collective-permute-start(s16[264,1024]{1,0:T(8,128)(2,1)S(1)} %get-tuple-element.63), channel_id=1, source_target_pairs={{0,8},{8,16},{16,24},{24,0},{1,9},{9,17},{17,25},{25,1},{2,10},{10... | collective-permute-start | bytes 1622024 | tf_op jit(solution)/shard_map/ppermute | solution.py:331
  36.5 13.7 %collective-permute-start.11 = (s16[264,1024]{1,0:T(8,128)(2,1)S(1)}, s16[264,1024]{1,0:T(8,128)(2,1)S(1)}, u32[]{:S(2)}, u32[]{:S(2)}) collective-permute-start(s16[264,1024]{1,0:T(8,128)(2,1)S(1)} %get-tuple-element.64), channel_id=1, source_target_pairs={{0,24},{8,0},{16,8},{24,16},{1,25},{9,1},{17,9},{25,17},{2,26},{10... | collective-permute-start | bytes 1622024 | tf_op jit(solution)/shard_map/ppermute | solution.py:331
  39.3 14.5 %collective-permute-start.4 = (s16[264,1024]{1,0:T(8,128)(2,1)S(1)}, s16[264,1024]{1,0:T(8,128)(2,1)S(1)}, u32[]{:S(2)}, u32[]{:S(2)}) collective-permute-start(s16[264,1024]{1,0:T(8,128)(2,1)S(1)} %get-tuple-element.57), channel_id=1, source_target_pairs={{0,8},{8,16},{16,24},{24,0},{1,9},{9,17},{17,25},{25,1},{2,10},{10... | collective-permute-start | bytes 1622024 | tf_op jit(solution)/shard_map/ppermute | solution.py:331
  40.0 21.8 %collective-permute-start.5 = (s16[264,1024]{1,0:T(8,128)(2,1)S(1)}, s16[264,1024]{1,0:T(8,128)(2,1)S(1)}, u32[]{:S(2)}, u32[]{:S(2)}) collective-permute-start(s16[264,1024]{1,0:T(8,128)(2,1)S(1)} %get-tuple-element.58), channel_id=1, source_target_pairs={{0,24},{8,0},{16,8},{24,16},{1,25},{9,1},{17,9},{25,17},{2,26},{10... | collective-permute-start | bytes 1622024 | tf_op jit(solution)/shard_map/ppermute | solution.py:331
  50.2 12.5 %collective-permute-start.6 = (s16[264,1024]{1,0:T(8,128)(2,1)S(1)}, s16[264,1024]{1,0:T(8,128)(2,1)S(1)}, u32[]{:S(2)}, u32[]{:S(2)}) collective-permute-start(s16[264,1024]{1,0:T(8,128)(2,1)S(1)} %get-tuple-element.59), channel_id=1, source_target_pairs={{0,2},{2,4},{4,6},{6,0},{1,3},{3,5},{5,7},{7,1},{8,10},{10,12},{12... | collective-permute-start | bytes 1622024 | tf_op jit(solution)/shard_map/ppermute | solution.py:331
  50.2 13.1 %collective-permute-start.7 = (s16[264,1024]{1,0:T(8,128)(2,1)S(1)}, s16[264,1024]{1,0:T(8,128)(2,1)S(1)}, u32[]{:S(2)}, u32[]{:S(2)}) collective-permute-start(s16[264,1024]{1,0:T(8,128)(2,1)S(1)} %get-tuple-element.60), channel_id=1, source_target_pairs={{0,6},{2,0},{4,2},{6,4},{1,7},{3,1},{5,3},{7,5},{8,14},{10,8},{12,... | collective-permute-start | bytes 1622024 | tf_op jit(solution)/shard_map/ppermute | solution.py:331
  53.8 15.2 %collective-permute-start.23 = (s16[136,1024]{1,0:T(8,128)(2,1)S(1)}, s16[136,1024]{1,0:T(8,128)(2,1)S(1)}, u32[]{:S(2)}, u32[]{:S(2)}) collective-permute-start(s16[136,1024]{1,0:T(8,128)(2,1)S(1)} %get-tuple-element.78), channel_id=1, source_target_pairs={{0,2},{2,4},{4,6},{6,0},{1,3},{3,5},{5,7},{7,1},{8,10},{10,12},{12... | collective-permute-start | bytes 835592 | tf_op jit(solution)/shard_map/ppermute | solution.py:331
  61.8 11.0 %collective-permute-start.24 = (s16[136,1024]{1,0:T(8,128)(2,1)S(1)}, s16[136,1024]{1,0:T(8,128)(2,1)S(1)}, u32[]{:S(2)}, u32[]{:S(2)}) collective-permute-start(s16[136,1024]{1,0:T(8,128)(2,1)S(1)} %get-tuple-element.79), channel_id=1, source_target_pairs={{0,6},{2,0},{4,2},{6,4},{1,7},{3,1},{5,3},{7,5},{8,14},{10,8},{12,... | collective-permute-start | bytes 835592 | tf_op jit(solution)/shard_map/ppermute | solution.py:331
  62.7 11.8 %collective-permute-start.21 = (s16[136,1024]{1,0:T(8,128)(2,1)S(1)}, s16[136,1024]{1,0:T(8,128)(2,1)S(1)}, u32[]{:S(2)}, u32[]{:S(2)}) collective-permute-start(s16[136,1024]{1,0:T(8,128)(2,1)S(1)} %get-tuple-element.75), channel_id=1, source_target_pairs={{0,2},{2,4},{4,6},{6,0},{1,3},{3,5},{5,7},{7,1},{8,10},{10,12},{12... | collective-permute-start | bytes 835592 | tf_op jit(solution)/shard_map/ppermute | solution.py:331
  63.3 15.4 %collective-permute-start.22 = (s16[136,1024]{1,0:T(8,128)(2,1)S(1)}, s16[136,1024]{1,0:T(8,128)(2,1)S(1)}, u32[]{:S(2)}, u32[]{:S(2)}) collective-permute-start(s16[136,1024]{1,0:T(8,128)(2,1)S(1)} %get-tuple-element.76), channel_id=1, source_target_pairs={{0,6},{2,0},{4,2},{6,4},{1,7},{3,1},{5,3},{7,5},{8,14},{10,8},{12,... | collective-permute-start | bytes 835592 | tf_op jit(solution)/shard_map/ppermute | solution.py:331
  66.3 13.0 %collective-permute-start.14 = (s16[136,1024]{1,0:T(8,128)(2,1)S(1)}, s16[136,1024]{1,0:T(8,128)(2,1)S(1)}, u32[]{:S(2)}, u32[]{:S(2)}) collective-permute-start(s16[136,1024]{1,0:T(8,128)(2,1)S(1)} %get-tuple-element.68), channel_id=1, source_target_pairs={{0,8},{8,16},{16,24},{24,0},{1,9},{9,17},{17,25},{25,1},{2,10},{10... | collective-permute-start | bytes 835592 | tf_op jit(solution)/shard_map/ppermute | solution.py:331
  69.0 10.9 %collective-permute-start.15 = (s16[136,1024]{1,0:T(8,128)(2,1)S(1)}, s16[136,1024]{1,0:T(8,128)(2,1)S(1)}, u32[]{:S(2)}, u32[]{:S(2)}) collective-permute-start(s16[136,1024]{1,0:T(8,128)(2,1)S(1)} %get-tuple-element.69), channel_id=1, source_target_pairs={{0,24},{8,0},{16,8},{24,16},{1,25},{9,1},{17,9},{25,17},{2,26},{10... | collective-permute-start | bytes 835592 | tf_op jit(solution)/shard_map/ppermute | solution.py:331
  72.8 10.0 %collective-permute-start.12 = (s16[136,1024]{1,0:T(8,128)(2,1)S(1)}, s16[136,1024]{1,0:T(8,128)(2,1)S(1)}, u32[]{:S(2)}, u32[]{:S(2)}) collective-permute-start(s16[136,1024]{1,0:T(8,128)(2,1)S(1)} %get-tuple-element.65), channel_id=1, source_target_pairs={{0,8},{8,16},{16,24},{24,0},{1,9},{9,17},{17,25},{25,1},{2,10},{10... | collective-permute-start | bytes 835592 | tf_op jit(solution)/shard_map/ppermute | solution.py:331
  74.4 11.4 %collective-permute-start.13 = (s16[136,1024]{1,0:T(8,128)(2,1)S(1)}, s16[136,1024]{1,0:T(8,128)(2,1)S(1)}, u32[]{:S(2)}, u32[]{:S(2)}) collective-permute-start(s16[136,1024]{1,0:T(8,128)(2,1)S(1)} %get-tuple-element.66), channel_id=1, source_target_pairs={{0,24},{8,0},{16,8},{24,16},{1,25},{9,1},{17,9},{25,17},{2,26},{10... | collective-permute-start | bytes 835592 | tf_op jit(solution)/shard_map/ppermute | solution.py:331
  78.6 8.2 %collective-permute-start.25 = (s16[136,1024]{1,0:T(8,128)(2,1)S(1)}, s16[136,1024]{1,0:T(8,128)(2,1)S(1)}, u32[]{:S(2)}, u32[]{:S(2)}) collective-permute-start(s16[136,1024]{1,0:T(8,128)(2,1)S(1)} %get-tuple-element.80), channel_id=1, source_target_pairs={{0,16},{8,24},{16,0},{24,8},{1,17},{9,25},{17,1},{25,9},{2,18},{10... | collective-permute-start | bytes 835592 | tf_op jit(solution)/shard_map/ppermute | solution.py:331
  79.3 13.6 %collective-permute-start.26 = (s16[136,1024]{1,0:T(8,128)(2,1)S(1)}, s16[136,1024]{1,0:T(8,128)(2,1)S(1)}, u32[]{:S(2)}, u32[]{:S(2)}) collective-permute-start(s16[136,1024]{1,0:T(8,128)(2,1)S(1)} %get-tuple-element.81), channel_id=1, source_target_pairs={{0,8},{8,16},{16,24},{24,0},{1,9},{9,17},{17,25},{25,1},{2,10},{10... | collective-permute-start | bytes 835592 | tf_op jit(solution)/shard_map/ppermute | solution.py:331
  79.9 14.8 %collective-permute-start.27 = (s16[136,1024]{1,0:T(8,128)(2,1)S(1)}, s16[136,1024]{1,0:T(8,128)(2,1)S(1)}, u32[]{:S(2)}, u32[]{:S(2)}) collective-permute-start(s16[136,1024]{1,0:T(8,128)(2,1)S(1)} %get-tuple-element.82), channel_id=1, source_target_pairs={{0,24},{8,0},{16,8},{24,16},{1,25},{9,1},{17,9},{25,17},{2,26},{10... | collective-permute-start | bytes 835592 | tf_op jit(solution)/shard_map/ppermute | solution.py:331
  82.8 11.9 %collective-permute-start.16 = (s16[136,1024]{1,0:T(8,128)(2,1)S(1)}, s16[136,1024]{1,0:T(8,128)(2,1)S(1)}, u32[]{:S(2)}, u32[]{:S(2)}) collective-permute-start(s16[136,1024]{1,0:T(8,128)(2,1)S(1)} %get-tuple-element.70), channel_id=1, source_target_pairs={{0,4},{2,6},{4,0},{6,2},{1,5},{3,7},{5,1},{7,3},{8,12},{10,14},{12... | collective-permute-start | bytes 835592 | tf_op jit(solution)/shard_map/ppermute | solution.py:331
  85.8 9.0 %collective-permute-start.17 = (s16[136,1024]{1,0:T(8,128)(2,1)S(1)}, s16[136,1024]{1,0:T(8,128)(2,1)S(1)}, u32[]{:S(2)}, u32[]{:S(2)}) collective-permute-start(s16[136,1024]{1,0:T(8,128)(2,1)S(1)} %get-tuple-element.71), channel_id=1, source_target_pairs={{0,2},{2,4},{4,6},{6,0},{1,3},{3,5},{5,7},{7,1},{8,10},{10,12},{12... | collective-permute-start | bytes 835592 | tf_op jit(solution)/shard_map/ppermute | solution.py:331
  86.4 30.1 %copy-start.5 = (s32[1,256,1024]{2,1,0:T(8,128)S(1)}, s32[1,256,1024]{2,1,0:T(8,128)}, u32[]{:S(2)}) copy-start(s32[1,256,1024]{2,1,0:T(8,128)} %refs_0_.1) | copy-start | bytes 3145732
  86.4 30.1 %copy-start.6 = (s32[1,256,1024]{2,1,0:T(8,128)S(1)}, s32[1,256,1024]{2,1,0:T(8,128)}, u32[]{:S(2)}) copy-start(s32[1,256,1024]{2,1,0:T(8,128)} %refs_3_.1) | copy-start | bytes 3145732
  86.4 30.1 %copy-start.7 = (f32[1,1024]{1,0:T(1,128)S(1)}, f32[1,1024]{1,0:T(1,128)}, u32[]{:S(2)}) copy-start(f32[1,1024]{1,0:T(1,128)} %refs_2_.1) | copy-start | bytes 12292
  86.4 30.1 %copy-start.8 = (f32[1,1024]{1,0:T(1,128)S(1)}, f32[1,1024]{1,0:T(1,128)}, u32[]{:S(2)}) copy-start(f32[1,1024]{1,0:T(1,128)} %refs_5_.1) | copy-start | bytes 12292
  86.4 30.1 %copy-start.9 = (f32[1,256]{1,0:T(1,128)S(1)}, f32[1,256]{1,0:T(1,128)}, u32[]{:S(2)}) copy-start(f32[1,256]{1,0:T(1,128)} %refs_1_.1) | copy-start | bytes 3076
  86.4 30.1 %copy-start.10 = (f32[1,256]{1,0:T(1,128)S(1)}, f32[1,256]{1,0:T(1,128)}, u32[]{:S(2)}) copy-start(f32[1,256]{1,0:T(1,128)} %refs_4_.1) | copy-start | bytes 3076
  86.8 7.9 %collective-permute-start.18 = (s16[136,1024]{1,0:T(8,128)(2,1)S(1)}, s16[136,1024]{1,0:T(8,128)(2,1)S(1)}, u32[]{:S(2)}, u32[]{:S(2)}) collective-permute-start(s16[136,1024]{1,0:T(8,128)(2,1)S(1)} %get-tuple-element.72), channel_id=1, source_target_pairs={{0,6},{2,0},{4,2},{6,4},{1,7},{3,1},{5,3},{7,5},{8,14},{10,8},{12,... | collective-permute-start | bytes 835592 | tf_op jit(solution)/shard_map/ppermute | solution.py:331
  96.4 29.4 %all-to-all-start = ((f32[128,1,128]{2,1,0:T(1,128)}), f32[128,1,128]{2,1,0:T(1,128)S(1)}, u32[]{:S(2)}, u32[]{:S(2)}) async-start(f32[128,1,128]{2,1,0:T(1,128)} %bitcast.2), calls=%async_computation | async-start | bytes 131072 | tf_op jit(solution)/shard_map/all_to_all | solution.py:494
  116.9 1.0 copy-start.1
  117.9 1.0 copy-start.3
  125.8 1.2 copy-start.2
  127.0 1.2 copy-start.4
  129.5 13.8 %all-to-all-start.1 = ((f32[32,16,128]{2,1,0:T(8,128)}), f32[32,16,128]{2,1,0:T(8,128)S(1)}, u32[]{:S(2)}, u32[]{:S(2)}) async-start(f32[32,16,128]{2,1,0:T(8,128)} %get-tuple-element.90), calls=%async_computation.1 | async-start | bytes 524288 | tf_op jit(solution)/shard_map/all_to_all | solution.py:494

commit v6 on v5

--- a/solution.py
+++ b/solution.py
@@ -288,12 +288,30 @@
     )(acc, *[held(g) for g in got])
 
 
+def early_body(*refs):
+    for half in range(2):
+        (kept, far), out = refs[2 * half : 2 * half + 2], refs[4 + half]
+        rows = kept.shape[0]
+        by = came_factor(far.at[rows : rows + SIDE])[0:1]
+
+        def step(r, _, kept=kept, far=far, out=out, by=by):
+            out[pl.ds(r, STEP), :] = kept[pl.ds(r, STEP), :] + decode(far[pl.ds(r, STEP), :], by)
+
+        chunks(rows, step, None)
+
+
+def early(halves):
+    rows, cols = halves[0][0].shape
+    flat = [a for kept, far, *_ in halves for a in (kept, held(far))]
+    return call(early_body, (VMEM((rows, cols), F32),) * 2, [], 40 * rows * cols, 20 * rows * cols, in_vmem(4))(*flat)
+
+
 def last_body(*refs):
-    ins, (grad, squares) = refs[:8], refs[8:]
+    ins, (grad, squares) = refs[:6], refs[6:]
     rows, cols = ins[0].shape
     square = jnp.zeros((8, cols), F32)
     for half in range(2):
-        kept, *got = ins[4 * half : 4 * half + 4]
+        kept, *got = ins[3 * half : 3 * half + 3]
         by = [came_factor(ref.at[rows : rows + SIDE])[0:1] for ref in got]
 
         def step(r, square, half=half, kept=kept, got=got, by=by):
@@ -317,9 +335,9 @@
         last_body,
         (VMEM((2 * rows, cols), F32), VMEM((devices, 128), F32)),
         [],
-        100 * rows * cols,
-        32 * rows * cols,
-        in_vmem(8),
+        80 * rows * cols,
+        24 * rows * cols,
+        in_vmem(6),
     )(*flat)
 
 
@@ -373,7 +391,8 @@
         for out, delta in ((far_out, 2), (near_out, 1), (back_out, 3)):
             got.append(hop(out, axis[1 - half], delta))
         halves.append([kept] + got)
-    return last(halves, devices)
+    sums = early(halves)
+    return last([[total, *got[2:]] for total, got in zip(sums, halves)], devices)
 
 
 def clip_body(limit, squares, grad, first_old, second_old, first_new, second_new, peaks):

time: 146 us -> 140 us (0.959)
  starting transfers between devices: 58.3 us -> 54.5 us
    all_to_all x2, starting transfers between devices: 24.8 us -> 22.4 us  [exchange(): return lax.all_to_all(value, axes, split_axis=0, concat_axis=0, tiled=True)]
where the time goes in v6:
time: 140 us
  starting transfers between devices  54.5 us (39%)
  waiting for transfers between devices  53.6 us (38%)
  Pallas kernels  23.2 us (17%)
  local copies, waits for them, and re-layouts  7.82 us (6%)
    ppermute x22, waiting for transfers between devices, hop(): lax.ppermute(value, name, [(i, (i + delta) % RING) for i in range(RING)])  34.5 us
    ppermute x22, starting transfers between devices, hop(): lax.ppermute(value, name, [(i, (i + delta) % RING) for i in range(RING)])  28 us
    all_to_all x2, starting transfers between devices, exchange(): return lax.all_to_all(value, axes, split_axis=0, concat_axis=0, tiled=True)  22.4 us
    all_to_all x2, waiting for transfers between devices, exchange(): return lax.all_to_all(value, axes, split_axis=0, concat_axis=0, tiled=True)  14.6 us
    pallas_call x8, Pallas kernels, pair(): call(functools.partial(pair_body, messages, first, len(relayed), sends),...  8.5 us
    unnamed x30, local copies, waits for them, and re-layouts  7.82 us
    ppermute x6, waiting for transfers between devices, swap(): return lax.ppermute(value, 'core', [(0, 1), (1, 0)])  4.49 us
    ppermute x6, starting transfers between devices, swap(): return lax.ppermute(value, 'core', [(0, 1), (1, 0)])  4.05 us
  transfers between devices with their start and end apart: 30, of which 13 were waited for; matrix products, arithmetic and copies ran while one was open for 0% of the time, Pallas kernels for 11%

profile of v6, /device:TPU:1, one launch (start us, length us, event | category | flops | bytes accessed | tf_op | source)
XLA Modules:
  0.0 140.1 jit_solution(2878227519271700148)
XLA Ops:
  0.6 1.7 %shard_map.126 = (bf16[2,2,128,1024]{3,2,1,0:T(8,128)(2,1)S(1)}, bf16[2,2,128,1024]{3,2,1,0:T(8,128)(2,1)S(1)}) custom-call(bf16[16,2,2,128,1024]{4,3,2,1,0:T(8,128)(2,1)} %bitcast.5), custom_call_target="tpu_custom_call" | custom-call | flops 1048576 | bytes 4194304 | tf_op jit(solution)/shard_map/pallas_call | solution.py:116
  2.4 1.5 %collective-permute-start = (bf16[2,2,128,1024]{3,2,1,0:T(8,128)(2,1)S(1)}, bf16[2,2,128,1024]{3,2,1,0:T(8,128)(2,1)S(1)}, u32[]{:S(2)}, u32[]{:S(2)}) collective-permute-start(bf16[2,2,128,1024]{3,2,1,0:T(8,128)(2,1)S(1)} %get-tuple-element.55), channel_id=1, source_target_pairs={{0,1},{1,0},{2,3},{3,2},{4,5},{5,4},{6,7},{7,6},{8,9},{9,8},{10,11... | collective-permute-start | bytes 3145736 | tf_op jit(solution)/shard_map/ppermute | solution.py:352
  3.9 2.3 %collective-permute-done.refs_1_ = bf16[2,2,128,1024]{3,2,1,0:T(8,128)(2,1)S(1)} collective-permute-done((bf16[2,2,128,1024]{3,2,1,0:T(8,128)(2,1)S(1)}, bf16[2,2,128,1024]{3,2,1,0:T(8,128)(2,1)S(1)}, u32[]{:S(2)}, u32[]{:S(2)}) %collective-permute-start) | collective-permute-done | bytes 1048608 | tf_op jit(solution)/shard_map/ppermute | solution.py:352
  6.1 0.9 copy-done
  7.0 1.3 shard_map.127
  8.3 1.5 %collective-permute-start.3 = (bf16[2,2,128,1024]{3,2,1,0:T(8,128)(2,1)S(1)}, bf16[2,2,128,1024]{3,2,1,0:T(8,128)(2,1)S(1)}, u32[]{:S(2)}, u32[]{:S(2)}) collective-permute-start(bf16[2,2,128,1024]{3,2,1,0:T(8,128)(2,1)S(1)} %get-tuple-element.58), channel_id=1, source_target_pairs={{0,1},{1,0},{2,3},{3,2},{4,5},{5,4},{6,7},{7,6},{8,9},{9,8},{10,11... | collective-permute-start | bytes 3145736 | tf_op jit(solution)/shard_map/ppermute | solution.py:352
  9.9 2.2 %collective-permute-done.3.refs_1_ = bf16[2,2,128,1024]{3,2,1,0:T(8,128)(2,1)S(1)} collective-permute-done((bf16[2,2,128,1024]{3,2,1,0:T(8,128)(2,1)S(1)}, bf16[2,2,128,1024]{3,2,1,0:T(8,128)(2,1)S(1)}, u32[]{:S(2)}, u32[]{:S(2)}) %collective-permute-start.3) | collective-permute-done | bytes 1048608 | tf_op jit(solution)/shard_map/ppermute | solution.py:352
  12.1 1.3 shard_map.129
  13.8 2.0 %shard_map.131 = bf16[2,2,128,1024]{3,2,1,0:T(8,128)(2,1)S(1)} custom-call(bf16[16,2,2,128,1024]{4,3,2,1,0:T(8,128)(2,1)} %bitcast.6), custom_call_target="tpu_custom_call" | custom-call | flops 524288 | bytes 2097152 | tf_op jit(solution)/shard_map/pallas_call | solution.py:116
  15.9 1.3 slice-done.2
  17.2 1.2 slice-done.3
  18.4 1.3 shard_map.128
  20.2 1.7 %collective-permute-start.17 = (s16[264,1024]{1,0:T(8,128)(2,1)S(1)}, s16[264,1024]{1,0:T(8,128)(2,1)S(1)}, u32[]{:S(2)}, u32[]{:S(2)}) collective-permute-start(s16[264,1024]{1,0:T(8,128)(2,1)S(1)} %get-tuple-element.73), channel_id=1, source_target_pairs={{0,2},{2,4},{4,6},{6,0},{1,3},{3,5},{5,7},{7,1},{8,10},{10,12},{12... | collective-permute-start | bytes 1622024 | tf_op jit(solution)/shard_map/ppermute | solution.py:349
  21.9 2.1 %collective-permute-start.18 = (s16[264,1024]{1,0:T(8,128)(2,1)S(1)}, s16[264,1024]{1,0:T(8,128)(2,1)S(1)}, u32[]{:S(2)}, u32[]{:S(2)}) collective-permute-start(s16[264,1024]{1,0:T(8,128)(2,1)S(1)} %get-tuple-element.74), channel_id=1, source_target_pairs={{0,6},{2,0},{4,2},{6,4},{1,7},{3,1},{5,3},{7,5},{8,14},{10,8},{12,... | collective-permute-start | bytes 1622024 | tf_op jit(solution)/shard_map/ppermute | solution.py:349
  24.0 1.1 shard_map.132
  25.2 1.4 collective-permute-start.10
  26.5 10.0 %collective-permute-done.17.refs_2_ = s16[264,1024]{1,0:T(8,128)(2,1)S(1)} collective-permute-done((s16[264,1024]{1,0:T(8,128)(2,1)S(1)}, s16[264,1024]{1,0:T(8,128)(2,1)S(1)}, u32[]{:S(2)}, u32[]{:S(2)}) %collective-permute-start.17) | collective-permute-done | bytes 540704 | tf_op jit(solution)/shard_map/ppermute | solution.py:349
  36.5 2.7 %collective-permute-start.11 = (s16[264,1024]{1,0:T(8,128)(2,1)S(1)}, s16[264,1024]{1,0:T(8,128)(2,1)S(1)}, u32[]{:S(2)}, u32[]{:S(2)}) collective-permute-start(s16[264,1024]{1,0:T(8,128)(2,1)S(1)} %get-tuple-element.66), channel_id=1, source_target_pairs={{0,24},{8,0},{16,8},{24,16},{1,25},{9,1},{17,9},{25,17},{2,26},{10... | collective-permute-start | bytes 1622024 | tf_op jit(solution)/shard_map/ppermute | solution.py:349
  40.0 2.0 %collective-permute-start.5 = (s16[264,1024]{1,0:T(8,128)(2,1)S(1)}, s16[264,1024]{1,0:T(8,128)(2,1)S(1)}, u32[]{:S(2)}, u32[]{:S(2)}) collective-permute-start(s16[264,1024]{1,0:T(8,128)(2,1)S(1)} %get-tuple-element.60), channel_id=1, source_target_pairs={{0,24},{8,0},{16,8},{24,16},{1,25},{9,1},{17,9},{25,17},{2,26},{10... | collective-permute-start | bytes 1622024 | tf_op jit(solution)/shard_map/ppermute | solution.py:349
  42.0 8.2 %collective-permute-done.11.refs_3_ = s16[264,1024]{1,0:T(8,128)(2,1)S(1)} collective-permute-done((s16[264,1024]{1,0:T(8,128)(2,1)S(1)}, s16[264,1024]{1,0:T(8,128)(2,1)S(1)}, u32[]{:S(2)}, u32[]{:S(2)}) %collective-permute-start.11) | collective-permute-done | bytes 540704 | tf_op jit(solution)/shard_map/ppermute | solution.py:349
  50.2 2.7 %collective-permute-start.7 = (s16[264,1024]{1,0:T(8,128)(2,1)S(1)}, s16[264,1024]{1,0:T(8,128)(2,1)S(1)}, u32[]{:S(2)}, u32[]{:S(2)}) collective-permute-start(s16[264,1024]{1,0:T(8,128)(2,1)S(1)} %get-tuple-element.62), channel_id=1, source_target_pairs={{0,6},{2,0},{4,2},{6,4},{1,7},{3,1},{5,3},{7,5},{8,14},{10,8},{12,... | collective-permute-start | bytes 1622024 | tf_op jit(solution)/shard_map/ppermute | solution.py:349
  52.9 0.9 shard_map.139
  53.9 0.9 shard_map.135
  54.8 7.0 %collective-permute-done.5.refs_1_ = s16[264,1024]{1,0:T(8,128)(2,1)S(1)} collective-permute-done((s16[264,1024]{1,0:T(8,128)(2,1)S(1)}, s16[264,1024]{1,0:T(8,128)(2,1)S(1)}, u32[]{:S(2)}, u32[]{:S(2)}) %collective-permute-start.5) | collective-permute-done | bytes 540704 | tf_op jit(solution)/shard_map/ppermute | solution.py:349
  61.8 0.9 collective-permute-start.22
  63.5 2.7 %collective-permute-start.15 = (s16[136,1024]{1,0:T(8,128)(2,1)S(1)}, s16[136,1024]{1,0:T(8,128)(2,1)S(1)}, u32[]{:S(2)}, u32[]{:S(2)}) collective-permute-start(s16[136,1024]{1,0:T(8,128)(2,1)S(1)} %get-tuple-element.71), channel_id=1, source_target_pairs={{0,24},{8,0},{16,8},{24,16},{1,25},{9,1},{17,9},{25,17},{2,26},{10... | collective-permute-start | bytes 835592 | tf_op jit(solution)/shard_map/ppermute | solution.py:349
  66.2 0.9 shard_map.137
  67.9 1.7 %shard_map.130.acc = f32[2,4,128,1024]{3,2,1,0:T(8,128)S(1)} custom-call(bf16[16,2,2,128,1024]{4,3,2,1,0:T(8,128)(2,1)S(1)} %bitcast.15, bf16[4,2,128,1024]{3,2,1,0:T(8,128)(2,1)S(1)} %collective-permute-done.2.came, s16[264,1024]{1,0:T(8,128)(2,1)S(1)} %collective-permute-done.4.refs_0_, s16[264,1024]{1,0:T(8,128)(2,1)S(1)} %collective-permute-done.5.refs_1_, ...), custom_call_target="tpu_custom_call" | custom-call | flops 26214400 | bytes 10485760 | tf_op jit(solution)/shard_map/pallas_call | solution.py:231
  69.6 2.2 %collective-permute-start.20 = (s16[136,1024]{1,0:T(8,128)(2,1)S(1)}, s16[136,1024]{1,0:T(8,128)(2,1)S(1)}, u32[]{:S(2)}, u32[]{:S(2)}) collective-permute-start(s16[136,1024]{1,0:T(8,128)(2,1)S(1)} %get-tuple-element.76), channel_id=1, source_target_pairs={{0,6},{2,0},{4,2},{6,4},{1,7},{3,1},{5,3},{7,5},{8,14},{10,8},{12,... | collective-permute-start | bytes 835592 | tf_op jit(solution)/shard_map/ppermute | solution.py:349
  71.8 0.9 shard_map.133
  72.8 2.7 %collective-permute-start.13 = (s16[136,1024]{1,0:T(8,128)(2,1)S(1)}, s16[136,1024]{1,0:T(8,128)(2,1)S(1)}, u32[]{:S(2)}, u32[]{:S(2)}) collective-permute-start(s16[136,1024]{1,0:T(8,128)(2,1)S(1)} %get-tuple-element.68), channel_id=1, source_target_pairs={{0,24},{8,0},{16,8},{24,16},{1,25},{9,1},{17,9},{25,17},{2,26},{10... | collective-permute-start | bytes 835592 | tf_op jit(solution)/shard_map/ppermute | solution.py:349
  79.0 0.9 collective-permute-done.12.first
  79.9 1.7 %collective-permute-start.27 = (s16[136,1024]{1,0:T(8,128)(2,1)S(1)}, s16[136,1024]{1,0:T(8,128)(2,1)S(1)}, u32[]{:S(2)}, u32[]{:S(2)}) collective-permute-start(s16[136,1024]{1,0:T(8,128)(2,1)S(1)} %get-tuple-element.86), channel_id=1, source_target_pairs={{0,24},{8,0},{16,8},{24,16},{1,25},{9,1},{17,9},{25,17},{2,26},{10... | collective-permute-start | bytes 835592 | tf_op jit(solution)/shard_map/ppermute | solution.py:349
  84.1 1.7 %collective-permute-start.25 = (s16[136,1024]{1,0:T(8,128)(2,1)S(1)}, s16[136,1024]{1,0:T(8,128)(2,1)S(1)}, u32[]{:S(2)}, u32[]{:S(2)}) collective-permute-start(s16[136,1024]{1,0:T(8,128)(2,1)S(1)} %get-tuple-element.83), channel_id=1, source_target_pairs={{0,6},{2,0},{4,2},{6,4},{1,7},{3,1},{5,3},{7,5},{8,14},{10,8},{12,... | collective-permute-start | bytes 835592 | tf_op jit(solution)/shard_map/ppermute | solution.py:349
  86.1 4.1 %collective-permute-done.26.refs_4_ = s16[136,1024]{1,0:T(8,128)(2,1)S(1)} collective-permute-done((s16[136,1024]{1,0:T(8,128)(2,1)S(1)}, s16[136,1024]{1,0:T(8,128)(2,1)S(1)}, u32[]{:S(2)}, u32[]{:S(2)}) %collective-permute-start.26) | collective-permute-done | bytes 278560 | tf_op jit(solution)/shard_map/ppermute | solution.py:349
  90.2 2.1 %collective-permute-done.25.refs_2_ = s16[136,1024]{1,0:T(8,128)(2,1)S(1)} collective-permute-done((s16[136,1024]{1,0:T(8,128)(2,1)S(1)}, s16[136,1024]{1,0:T(8,128)(2,1)S(1)}, u32[]{:S(2)}, u32[]{:S(2)}) %collective-permute-start.25) | collective-permute-done | bytes 278560 | tf_op jit(solution)/shard_map/ppermute | solution.py:349
  92.3 1.3 shard_map.142
  93.6 17.6 %all-to-all-start = ((f32[128,1,128]{2,1,0:T(1,128)}), f32[128,1,128]{2,1,0:T(1,128)S(1)}, u32[]{:S(2)}, u32[]{:S(2)}) async-start(f32[128,1,128]{2,1,0:T(1,128)} %bitcast.2), calls=%async_computation | async-start | bytes 131072 | tf_op jit(solution)/shard_map/all_to_all | solution.py:513
  111.7 1.0 copy-done.1
  112.7 1.0 copy-done.3
  113.7 6.9 %all-to-all-done = f32[128,1,128]{2,1,0:T(1,128)S(1)} async-done(((f32[128,1,128]{2,1,0:T(1,128)}), f32[128,1,128]{2,1,0:T(1,128)S(1)}, u32[]{:S(2)}, u32[]{:S(2)}) %all-to-all-start) | async-done | bytes 65568 | tf_op jit(solution)/shard_map/all_to_all | solution.py:513
  120.6 1.2 copy-done.2
  121.8 1.2 copy-done.4
  123.0 1.2 shard_map.144
  124.3 4.7 %all-to-all-start.1 = ((f32[32,16,128]{2,1,0:T(8,128)}), f32[32,16,128]{2,1,0:T(8,128)S(1)}, u32[]{:S(2)}, u32[]{:S(2)}) async-start(f32[32,16,128]{2,1,0:T(8,128)} %get-tuple-element.94), calls=%async_computation.1 | async-start | bytes 524288 | tf_op jit(solution)/shard_map/all_to_all | solution.py:513
  129.0 1.3 row_outputs.1
  130.4 7.7 %all-to-all-done.1.peaks = f32[32,16,128]{2,1,0:T(8,128)S(1)} async-done(((f32[32,16,128]{2,1,0:T(8,128)}), f32[32,16,128]{2,1,0:T(8,128)S(1)}, u32[]{:S(2)}, u32[]{:S(2)}) %all-to-all-start.1) | async-done | bytes 262176 | tf_op jit(solution)/shard_map/all_to_all | solution.py:513
  138.1 2.0 %scaled_outputs.1 = (f32[1,256,1024]{2,1,0:T(8,128)}, f32[1,256,1024]{2,1,0:T(8,128)}, f32[1,1024]{1,0:T(1,128)}, f32[1,1024]{1,0:T(1,128)}) custom-call(f32[32,16,128]{2,1,0:T(8,128)S(1)} %all-to-all-done.1.peaks, f32[256,1024]{1,0:T(8,128)S(1)} %get-tuple-element.91.first_new, f32[256,1024]{1,0:T(8,128)S(1)} %get-tuple-element.92.second_new, ...), custom_call_target="tpu_custom_call" | custom-call | flops 2097152 | bytes 4194304 | tf_op jit(solution)/shard_map/scaled_outputs/pallas_call | solution.py:499
  (64 shorter events, 10.3 us)
Async XLA Ops:
  0.6 6.4 %copy-start = (bf16[1,1,8192,1024]{3,2,1,0:T(8,128)(2,1)S(1)}, bf16[1,1,8192,1024]{3,2,1,0:T(8,128)(2,1)}, u32[]{:S(2)}) copy-start(bf16[1,1,8192,1024]{3,2,1,0:T(8,128)(2,1)} %param.7) | copy-start | bytes 50331652
  2.4 3.7 %collective-permute-start = (bf16[2,2,128,1024]{3,2,1,0:T(8,128)(2,1)S(1)}, bf16[2,2,128,1024]{3,2,1,0:T(8,128)(2,1)S(1)}, u32[]{:S(2)}, u32[]{:S(2)}) collective-permute-start(bf16[2,2,128,1024]{3,2,1,0:T(8,128)(2,1)S(1)} %get-tuple-element.55), channel_id=1, source_target_pairs={{0,1},{1,0},{2,3},{3,2},{4,5},{5,4},{6,7},{7,6},{8,9},{9,8},{10,11... | collective-permute-start | bytes 3145736 | tf_op jit(solution)/shard_map/ppermute | solution.py:352
  8.3 3.7 %collective-permute-start.3 = (bf16[2,2,128,1024]{3,2,1,0:T(8,128)(2,1)S(1)}, bf16[2,2,128,1024]{3,2,1,0:T(8,128)(2,1)S(1)}, u32[]{:S(2)}, u32[]{:S(2)}) collective-permute-start(bf16[2,2,128,1024]{3,2,1,0:T(8,128)(2,1)S(1)} %get-tuple-element.58), channel_id=1, source_target_pairs={{0,1},{1,0},{2,3},{3,2},{4,5},{5,4},{6,7},{7,6},{8,9},{9,8},{10,11... | collective-permute-start | bytes 3145736 | tf_op jit(solution)/shard_map/ppermute | solution.py:352
  9.8 6.2 %collective-permute-start.1 = (bf16[2,2,128,1024]{3,2,1,0:T(8,128)(2,1)S(1)}, bf16[2,2,128,1024]{3,2,1,0:T(8,128)(2,1)S(1)}, u32[]{:S(2)}, u32[]{:S(2)}) collective-permute-start(bf16[2,2,128,1024]{3,2,1,0:T(8,128)(2,1)S(1)} %get-tuple-element.56), channel_id=1, source_target_pairs={{0,1},{1,0},{2,3},{3,2},{4,5},{5,4},{6,7},{7,6},{8,9},{9,8},{10,11... | collective-permute-start | bytes 3145736 | tf_op jit(solution)/shard_map/ppermute | solution.py:352
  12.1 3.9 %slice-start = ((s8[16777216]{0:T(1024)(128)(4,1)}), s8[4194304]{0:T(1024)(128)(4,1)S(1)}, s32[]{:S(2)}) async-start(s8[16777216]{0:T(1024)(128)(4,1)} %bitcast.9), calls=%async_computation.2 | async-start | bytes 8388608
  12.1 3.9 %slice-start.1 = ((s8[16777216]{0:T(1024)(128)(4,1)}), s8[4194304]{0:T(1024)(128)(4,1)S(1)}, s32[]{:S(2)}) async-start(s8[16777216]{0:T(1024)(128)(4,1)} %bitcast.9), calls=%async_computation.3 | async-start | bytes 8388608
  13.3 3.9 %slice-start.2 = ((s8[16777216]{0:T(1024)(128)(4,1)}), s8[4194304]{0:T(1024)(128)(4,1)S(1)}, s32[]{:S(2)}) async-start(s8[16777216]{0:T(1024)(128)(4,1)} %bitcast.9), calls=%async_computation.4 | async-start | bytes 8388608
  13.3 5.1 %slice-start.3 = ((s8[16777216]{0:T(1024)(128)(4,1)}), s8[4194304]{0:T(1024)(128)(4,1)S(1)}, s32[]{:S(2)}) async-start(s8[16777216]{0:T(1024)(128)(4,1)} %bitcast.9), calls=%async_computation.5 | async-start | bytes 8388608
  13.4 36.8 %collective-permute-start.8 = (bf16[4,2,128,1024]{3,2,1,0:T(8,128)(2,1)S(1)}, bf16[4,2,128,1024]{3,2,1,0:T(8,128)(2,1)S(1)}, u32[]{:S(2)}, u32[]{:S(2)}) collective-permute-start(bf16[4,2,128,1024]{3,2,1,0:T(8,128)(2,1)S(1)} %get-tuple-element.63), channel_id=1, source_target_pairs={{0,1},{1,0},{2,3},{3,2},{4,5},{5,4},{6,7},{7,6},{8,9},{9,8},{10,11... | collective-permute-start | bytes 6291464 | tf_op jit(solution)/shard_map/ppermute | solution.py:352
  15.8 8.2 %collective-permute-start.9 = (bf16[2,2,128,1024]{3,2,1,0:T(8,128)(2,1)S(1)}, bf16[2,2,128,1024]{3,2,1,0:T(8,128)(2,1)S(1)}, u32[]{:S(2)}, u32[]{:S(2)}) collective-permute-start(bf16[2,2,128,1024]{3,2,1,0:T(8,128)(2,1)S(1)} %shard_map.131), channel_id=1, source_target_pairs={{0,1},{1,0},{2,3},{3,2},{4,5},{5,4},{6,7},{7,6},{8,9},{9,8},{10,11... | collective-permute-start | bytes 3145736 | tf_op jit(solution)/shard_map/ppermute | solution.py:352
  19.7 47.4 %collective-permute-start.2 = (bf16[4,2,128,1024]{3,2,1,0:T(8,128)(2,1)S(1)}, bf16[4,2,128,1024]{3,2,1,0:T(8,128)(2,1)S(1)}, u32[]{:S(2)}, u32[]{:S(2)}) collective-permute-start(bf16[4,2,128,1024]{3,2,1,0:T(8,128)(2,1)S(1)} %get-tuple-element.57), channel_id=1, source_target_pairs={{0,1},{1,0},{2,3},{3,2},{4,5},{5,4},{6,7},{7,6},{8,9},{9,8},{10,11... | collective-permute-start | bytes 6291464 | tf_op jit(solution)/shard_map/ppermute | solution.py:352
  20.2 16.4 %collective-permute-start.17 = (s16[264,1024]{1,0:T(8,128)(2,1)S(1)}, s16[264,1024]{1,0:T(8,128)(2,1)S(1)}, u32[]{:S(2)}, u32[]{:S(2)}) collective-permute-start(s16[264,1024]{1,0:T(8,128)(2,1)S(1)} %get-tuple-element.73), channel_id=1, source_target_pairs={{0,2},{2,4},{4,6},{6,0},{1,3},{3,5},{5,7},{7,1},{8,10},{10,12},{12... | collective-permute-start | bytes 1622024 | tf_op jit(solution)/shard_map/ppermute | solution.py:349
  21.9 17.4 %collective-permute-start.18 = (s16[264,1024]{1,0:T(8,128)(2,1)S(1)}, s16[264,1024]{1,0:T(8,128)(2,1)S(1)}, u32[]{:S(2)}, u32[]{:S(2)}) collective-permute-start(s16[264,1024]{1,0:T(8,128)(2,1)S(1)} %get-tuple-element.74), channel_id=1, source_target_pairs={{0,6},{2,0},{4,2},{6,4},{1,7},{3,1},{5,3},{7,5},{8,14},{10,8},{12,... | collective-permute-start | bytes 1622024 | tf_op jit(solution)/shard_map/ppermute | solution.py:349
  25.2 14.8 %collective-permute-start.10 = (s16[264,1024]{1,0:T(8,128)(2,1)S(1)}, s16[264,1024]{1,0:T(8,128)(2,1)S(1)}, u32[]{:S(2)}, u32[]{:S(2)}) collective-permute-start(s16[264,1024]{1,0:T(8,128)(2,1)S(1)} %get-tuple-element.65), channel_id=1, source_target_pairs={{0,8},{8,16},{16,24},{24,0},{1,9},{9,17},{17,25},{25,1},{2,10},{10... | collective-permute-start | bytes 1622024 | tf_op jit(solution)/shard_map/ppermute | solution.py:349
  36.5 13.7 %collective-permute-start.11 = (s16[264,1024]{1,0:T(8,128)(2,1)S(1)}, s16[264,1024]{1,0:T(8,128)(2,1)S(1)}, u32[]{:S(2)}, u32[]{:S(2)}) collective-permute-start(s16[264,1024]{1,0:T(8,128)(2,1)S(1)} %get-tuple-element.66), channel_id=1, source_target_pairs={{0,24},{8,0},{16,8},{24,16},{1,25},{9,1},{17,9},{25,17},{2,26},{10... | collective-permute-start | bytes 1622024 | tf_op jit(solution)/shard_map/ppermute | solution.py:349
  39.3 14.5 %collective-permute-start.4 = (s16[264,1024]{1,0:T(8,128)(2,1)S(1)}, s16[264,1024]{1,0:T(8,128)(2,1)S(1)}, u32[]{:S(2)}, u32[]{:S(2)}) collective-permute-start(s16[264,1024]{1,0:T(8,128)(2,1)S(1)} %get-tuple-element.59), channel_id=1, source_target_pairs={{0,8},{8,16},{16,24},{24,0},{1,9},{9,17},{17,25},{25,1},{2,10},{10... | collective-permute-start | bytes 1622024 | tf_op jit(solution)/shard_map/ppermute | solution.py:349
  40.0 21.8 %collective-permute-start.5 = (s16[264,1024]{1,0:T(8,128)(2,1)S(1)}, s16[264,1024]{1,0:T(8,128)(2,1)S(1)}, u32[]{:S(2)}, u32[]{:S(2)}) collective-permute-start(s16[264,1024]{1,0:T(8,128)(2,1)S(1)} %get-tuple-element.60), channel_id=1, source_target_pairs={{0,24},{8,0},{16,8},{24,16},{1,25},{9,1},{17,9},{25,17},{2,26},{10... | collective-permute-start | bytes 1622024 | tf_op jit(solution)/shard_map/ppermute | solution.py:349
  50.2 12.5 %collective-permute-start.6 = (s16[264,1024]{1,0:T(8,128)(2,1)S(1)}, s16[264,1024]{1,0:T(8,128)(2,1)S(1)}, u32[]{:S(2)}, u32[]{:S(2)}) collective-permute-start(s16[264,1024]{1,0:T(8,128)(2,1)S(1)} %get-tuple-element.61), channel_id=1, source_target_pairs={{0,2},{2,4},{4,6},{6,0},{1,3},{3,5},{5,7},{7,1},{8,10},{10,12},{12... | collective-permute-start | bytes 1622024 | tf_op jit(solution)/shard_map/ppermute | solution.py:349
  50.2 13.3 %collective-permute-start.7 = (s16[264,1024]{1,0:T(8,128)(2,1)S(1)}, s16[264,1024]{1,0:T(8,128)(2,1)S(1)}, u32[]{:S(2)}, u32[]{:S(2)}) collective-permute-start(s16[264,1024]{1,0:T(8,128)(2,1)S(1)} %get-tuple-element.62), channel_id=1, source_target_pairs={{0,6},{2,0},{4,2},{6,4},{1,7},{3,1},{5,3},{7,5},{8,14},{10,8},{12,... | collective-permute-start | bytes 1622024 | tf_op jit(solution)/shard_map/ppermute | solution.py:349
  53.8 15.8 %collective-permute-start.21 = (s16[136,1024]{1,0:T(8,128)(2,1)S(1)}, s16[136,1024]{1,0:T(8,128)(2,1)S(1)}, u32[]{:S(2)}, u32[]{:S(2)}) collective-permute-start(s16[136,1024]{1,0:T(8,128)(2,1)S(1)} %get-tuple-element.78), channel_id=1, source_target_pairs={{0,2},{2,4},{4,6},{6,0},{1,3},{3,5},{5,7},{7,1},{8,10},{10,12},{12... | collective-permute-start | bytes 835592 | tf_op jit(solution)/shard_map/ppermute | solution.py:349
  61.8 10.9 %collective-permute-start.22 = (s16[136,1024]{1,0:T(8,128)(2,1)S(1)}, s16[136,1024]{1,0:T(8,128)(2,1)S(1)}, u32[]{:S(2)}, u32[]{:S(2)}) collective-permute-start(s16[136,1024]{1,0:T(8,128)(2,1)S(1)} %get-tuple-element.79), channel_id=1, source_target_pairs={{0,6},{2,0},{4,2},{6,4},{1,7},{3,1},{5,3},{7,5},{8,14},{10,8},{12,... | collective-permute-start | bytes 835592 | tf_op jit(solution)/shard_map/ppermute | solution.py:349
  62.7 10.1 %collective-permute-start.14 = (s16[136,1024]{1,0:T(8,128)(2,1)S(1)}, s16[136,1024]{1,0:T(8,128)(2,1)S(1)}, u32[]{:S(2)}, u32[]{:S(2)}) collective-permute-start(s16[136,1024]{1,0:T(8,128)(2,1)S(1)} %get-tuple-element.70), channel_id=1, source_target_pairs={{0,8},{8,16},{16,24},{24,0},{1,9},{9,17},{17,25},{25,1},{2,10},{10... | collective-permute-start | bytes 835592 | tf_op jit(solution)/shard_map/ppermute | solution.py:349
  63.5 12.8 %collective-permute-start.15 = (s16[136,1024]{1,0:T(8,128)(2,1)S(1)}, s16[136,1024]{1,0:T(8,128)(2,1)S(1)}, u32[]{:S(2)}, u32[]{:S(2)}) collective-permute-start(s16[136,1024]{1,0:T(8,128)(2,1)S(1)} %get-tuple-element.71), channel_id=1, source_target_pairs={{0,24},{8,0},{16,8},{24,16},{1,25},{9,1},{17,9},{25,17},{2,26},{10... | collective-permute-start | bytes 835592 | tf_op jit(solution)/shard_map/ppermute | solution.py:349
  67.1 10.0 %collective-permute-start.19 = (s16[136,1024]{1,0:T(8,128)(2,1)S(1)}, s16[136,1024]{1,0:T(8,128)(2,1)S(1)}, u32[]{:S(2)}, u32[]{:S(2)}) collective-permute-start(s16[136,1024]{1,0:T(8,128)(2,1)S(1)} %get-tuple-element.75), channel_id=1, source_target_pairs={{0,2},{2,4},{4,6},{6,0},{1,3},{3,5},{5,7},{7,1},{8,10},{10,12},{12... | collective-permute-start | bytes 835592 | tf_op jit(solution)/shard_map/ppermute | solution.py:349
  69.6 8.3 %collective-permute-start.20 = (s16[136,1024]{1,0:T(8,128)(2,1)S(1)}, s16[136,1024]{1,0:T(8,128)(2,1)S(1)}, u32[]{:S(2)}, u32[]{:S(2)}) collective-permute-start(s16[136,1024]{1,0:T(8,128)(2,1)S(1)} %get-tuple-element.76), channel_id=1, source_target_pairs={{0,6},{2,0},{4,2},{6,4},{1,7},{3,1},{5,3},{7,5},{8,14},{10,8},{12,... | collective-permute-start | bytes 835592 | tf_op jit(solution)/shard_map/ppermute | solution.py:349
  72.7 7.2 %collective-permute-start.12 = (s16[136,1024]{1,0:T(8,128)(2,1)S(1)}, s16[136,1024]{1,0:T(8,128)(2,1)S(1)}, u32[]{:S(2)}, u32[]{:S(2)}) collective-permute-start(s16[136,1024]{1,0:T(8,128)(2,1)S(1)} %get-tuple-element.67), channel_id=1, source_target_pairs={{0,8},{8,16},{16,24},{24,0},{1,9},{9,17},{17,25},{25,1},{2,10},{10... | collective-permute-start | bytes 835592 | tf_op jit(solution)/shard_map/ppermute | solution.py:349
  72.8 9.6 %collective-permute-start.13 = (s16[136,1024]{1,0:T(8,128)(2,1)S(1)}, s16[136,1024]{1,0:T(8,128)(2,1)S(1)}, u32[]{:S(2)}, u32[]{:S(2)}) collective-permute-start(s16[136,1024]{1,0:T(8,128)(2,1)S(1)} %get-tuple-element.68), channel_id=1, source_target_pairs={{0,24},{8,0},{16,8},{24,16},{1,25},{9,1},{17,9},{25,17},{2,26},{10... | collective-permute-start | bytes 835592 | tf_op jit(solution)/shard_map/ppermute | solution.py:349
  76.2 7.9 %collective-permute-start.23 = (s16[136,1024]{1,0:T(8,128)(2,1)S(1)}, s16[136,1024]{1,0:T(8,128)(2,1)S(1)}, u32[]{:S(2)}, u32[]{:S(2)}) collective-permute-start(s16[136,1024]{1,0:T(8,128)(2,1)S(1)} %get-tuple-element.80), channel_id=1, source_target_pairs={{0,16},{8,24},{16,0},{24,8},{1,17},{9,25},{17,1},{25,9},{2,18},{10... | collective-permute-start | bytes 835592 | tf_op jit(solution)/shard_map/ppermute | solution.py:349
  77.1 8.7 %collective-permute-start.16 = (s16[136,1024]{1,0:T(8,128)(2,1)S(1)}, s16[136,1024]{1,0:T(8,128)(2,1)S(1)}, u32[]{:S(2)}, u32[]{:S(2)}) collective-permute-start(s16[136,1024]{1,0:T(8,128)(2,1)S(1)} %get-tuple-element.72), channel_id=1, source_target_pairs={{0,4},{2,6},{4,0},{6,2},{1,5},{3,7},{5,1},{7,3},{8,12},{10,14},{12... | collective-permute-start | bytes 835592 | tf_op jit(solution)/shard_map/ppermute | solution.py:349
  77.9 12.3 %collective-permute-start.26 = (s16[136,1024]{1,0:T(8,128)(2,1)S(1)}, s16[136,1024]{1,0:T(8,128)(2,1)S(1)}, u32[]{:S(2)}, u32[]{:S(2)}) collective-permute-start(s16[136,1024]{1,0:T(8,128)(2,1)S(1)} %get-tuple-element.85), channel_id=1, source_target_pairs={{0,8},{8,16},{16,24},{24,0},{1,9},{9,17},{17,25},{25,1},{2,10},{10... | collective-permute-start | bytes 835592 | tf_op jit(solution)/shard_map/ppermute | solution.py:349
  79.9 10.3 %collective-permute-start.27 = (s16[136,1024]{1,0:T(8,128)(2,1)S(1)}, s16[136,1024]{1,0:T(8,128)(2,1)S(1)}, u32[]{:S(2)}, u32[]{:S(2)}) collective-permute-start(s16[136,1024]{1,0:T(8,128)(2,1)S(1)} %get-tuple-element.86), channel_id=1, source_target_pairs={{0,24},{8,0},{16,8},{24,16},{1,25},{9,1},{17,9},{25,17},{2,26},{10... | collective-permute-start | bytes 835592 | tf_op jit(solution)/shard_map/ppermute | solution.py:349
  82.4 7.8 %collective-permute-start.24 = (s16[136,1024]{1,0:T(8,128)(2,1)S(1)}, s16[136,1024]{1,0:T(8,128)(2,1)S(1)}, u32[]{:S(2)}, u32[]{:S(2)}) collective-permute-start(s16[136,1024]{1,0:T(8,128)(2,1)S(1)} %get-tuple-element.82), channel_id=1, source_target_pairs={{0,2},{2,4},{4,6},{6,0},{1,3},{3,5},{5,7},{7,1},{8,10},{10,12},{12... | collective-permute-start | bytes 835592 | tf_op jit(solution)/shard_map/ppermute | solution.py:349
  83.4 27.9 %copy-start.5 = (s32[1,256,1024]{2,1,0:T(8,128)S(1)}, s32[1,256,1024]{2,1,0:T(8,128)}, u32[]{:S(2)}) copy-start(s32[1,256,1024]{2,1,0:T(8,128)} %refs_0_.1) | copy-start | bytes 3145732
  83.4 27.9 %copy-start.6 = (s32[1,256,1024]{2,1,0:T(8,128)S(1)}, s32[1,256,1024]{2,1,0:T(8,128)}, u32[]{:S(2)}) copy-start(s32[1,256,1024]{2,1,0:T(8,128)} %refs_3_.1) | copy-start | bytes 3145732
  83.4 27.9 %copy-start.7 = (f32[1,1024]{1,0:T(1,128)S(1)}, f32[1,1024]{1,0:T(1,128)}, u32[]{:S(2)}) copy-start(f32[1,1024]{1,0:T(1,128)} %refs_2_.1) | copy-start | bytes 12292
  83.4 27.9 %copy-start.8 = (f32[1,1024]{1,0:T(1,128)S(1)}, f32[1,1024]{1,0:T(1,128)}, u32[]{:S(2)}) copy-start(f32[1,1024]{1,0:T(1,128)} %refs_5_.1) | copy-start | bytes 12292
  83.4 27.9 %copy-start.9 = (f32[1,256]{1,0:T(1,128)S(1)}, f32[1,256]{1,0:T(1,128)}, u32[]{:S(2)}) copy-start(f32[1,256]{1,0:T(1,128)} %refs_1_.1) | copy-start | bytes 3076
  83.4 27.9 %copy-start.10 = (f32[1,256]{1,0:T(1,128)S(1)}, f32[1,256]{1,0:T(1,128)}, u32[]{:S(2)}) copy-start(f32[1,256]{1,0:T(1,128)} %refs_4_.1) | copy-start | bytes 3076
  84.1 8.2 %collective-permute-start.25 = (s16[136,1024]{1,0:T(8,128)(2,1)S(1)}, s16[136,1024]{1,0:T(8,128)(2,1)S(1)}, u32[]{:S(2)}, u32[]{:S(2)}) collective-permute-start(s16[136,1024]{1,0:T(8,128)(2,1)S(1)} %get-tuple-element.83), channel_id=1, source_target_pairs={{0,6},{2,0},{4,2},{6,4},{1,7},{3,1},{5,3},{7,5},{8,14},{10,8},{12,... | collective-permute-start | bytes 835592 | tf_op jit(solution)/shard_map/ppermute | solution.py:349
  93.6 27.0 %all-to-all-start = ((f32[128,1,128]{2,1,0:T(1,128)}), f32[128,1,128]{2,1,0:T(1,128)S(1)}, u32[]{:S(2)}, u32[]{:S(2)}) async-start(f32[128,1,128]{2,1,0:T(1,128)} %bitcast.2), calls=%async_computation | async-start | bytes 131072 | tf_op jit(solution)/shard_map/all_to_all | solution.py:513
  111.7 1.0 copy-start.1
  112.7 1.0 copy-start.3
  120.6 1.2 copy-start.2
  121.8 1.2 copy-start.4
  124.3 13.8 %all-to-all-start.1 = ((f32[32,16,128]{2,1,0:T(8,128)}), f32[32,16,128]{2,1,0:T(8,128)S(1)}, u32[]{:S(2)}, u32[]{:S(2)}) async-start(f32[32,16,128]{2,1,0:T(8,128)} %get-tuple-element.94), calls=%async_computation.1 | async-start | bytes 524288 | tf_op jit(solution)/shard_map/all_to_all | solution.py:513
